TPU v7x, 128 devices: a whole 4x4x4 slice. The times are simulated.
128 devices in a mesh: grp: 4 (over y), dev: 32 (over z, x, core).
Axes of the slice: x: 4, y: 4, z: 4, core: 2. Of those that a mesh axis runs over, the one named last changes fastest.
Arguments:
- ids: int32 [16384, 13, 2], P(('grp', 'dev')), may hold values from 0 to 262143, as said below
- location: int32 [262144], replicated, may hold values from 0 to 262143, as said below
- cold_table: bfloat16 [262144, 128], P(('grp', 'dev')), may hold values from -3 to 3
- hot_index: int32 [16384, 13], P(('grp', 'dev')), may hold values from 0 to 31
- hot_list: int32 [128, 32], P(('grp', 'dev')), may hold values from 0 to 4095, as said below
- hot_table: bfloat16 [4096, 128], replicated, may hold values from -3 to 3
- labels: int32 [16384], P(('grp', 'dev')), may hold values 0 or 1
- cross_u: bfloat16 [1664, 256], replicated, may hold values from -0.15625 to 0.15625
- cross_v: bfloat16 [256, 1664], replicated, may hold values from -0.375 to 0.375
- cross_bias: float32 [1664], replicated, may hold values from -3 to 3
- mlp_weight: bfloat16 [2048, 1664], replicated, may hold values from -0.15625 to 0.15625
- mlp_bias: float32 [2048], replicated, may hold values from -3 to 3
- out_weight: bfloat16 [2048], replicated, may hold values from -0.125 to 0.125
Outputs:
- cold_grad: float32 [262144, 128], P(('grp', 'dev'))
- hot_grad: float32 [4096, 128], replicated
- mlp_weight_grad: float32 [2048, 1664], P(('grp', 'dev'))
- cross_u_grad: float32 [1664, 256], replicated
- cross_v_grad: float32 [256, 1664], replicated
- cross_bias_grad: float32 [1664], replicated
- mlp_bias_grad: float32 [2048], replicated
- out_weight_grad: float32 [2048], replicated
Inputs may be any that keep to these rules, and one draw needn't show every extreme that they name: The owner of an id is location[id] // 2048. Among the ids of one device's 128 samples (an aligned block of rows), at most 39 have any one owner; in every draw one owner has exactly 39 in every block. `location`: A permutation of 0 to 262143. `hot_list`: the 32 entries of each row are different.
All inputs are finite; a program needn't handle non-finite values. No bound on the sum of `labels` on one device may be relied on, other than what follows from the above.
Results may differ from a plain program's by a relative error of at most 0.0067.
Values may be sent and summed in bfloat16 or wider, within the bound.
No kernel may reach another device: no remote copies, remote signals or barrier semaphores. Data moves between devices by JAX's collectives and lax.ppermute only.
A program may use at most 128 MiB of HBM per device.

v0:
```python
import jax
import jax.numpy as jnp
from jax import lax
from jax.sharding import Mesh
from jax.sharding import PartitionSpec as P

GRP_DEV = ("grp", "dev_0", "dev_1", "dev_2")


def split_up(x, dim, length):
    before, after = (x.shape[:dim], x.shape[dim + 1 :])
    return jnp.moveaxis(x.reshape(*before, length, -1, *after), dim, 0)


def sum_by_chip_2(x, chips, core, dim):
    sizes = (lax.axis_size(chips), lax.axis_size(core))
    tiles = split_up(x, dim, sizes[0] * sizes[1])
    inside = tiles.shape[1:]
    tiles = tiles.reshape(*sizes, *inside).swapaxes(0, 1).reshape(-1, *inside)
    tiles = lax.psum_scatter(tiles, core, scatter_dimension=0, tiled=True)
    return lax.psum_scatter(tiles, chips, scatter_dimension=0, tiled=True)[0]


def in_one(arrays, axis):
    flat, at, gathered = (jnp.concatenate([a.reshape(-1) for a in arrays]), 0, [])
    running = lax.psum(flat, axis)
    for a in arrays:
        gathered.append(running[at : at + a.size].reshape(a.shape))
        at += a.size
    return tuple(gathered)


def silu_slope(values):
    squash = jax.nn.sigmoid(values)
    return squash * (1.0 + values * (1.0 - squash))


def contract_rows(former, latter):
    return lax.dot_general(
        former, latter, (((0,), (0,)), ((), ())), preferred_element_type=jnp.float32
    )


def contract_cols(former, latter):
    return lax.dot_general(
        former, latter, (((1,), (1,)), ((), ())), preferred_element_type=jnp.float32
    )


def per_device(
    ids,
    location,
    cold_table,
    hot_index,
    hot_list,
    hot_table,
    labels,
    cross_u,
    cross_v,
    cross_bias,
    mlp_weight,
    mlp_bias,
    out_weight,
):
    devices = lax.axis_size(GRP_DEV)
    samples, features, bag_size = ids.shape
    shard_rows, row_width = cold_table.shape
    requests = samples * features * bag_size
    mean_load = requests // devices
    capacity = mean_load + mean_load // 2
    placed = location[ids.reshape(requests)]
    owners = placed // shard_rows
    row_slot = placed - owners * shard_rows
    ranking = jnp.argsort(owners, stable=True)
    sorted_owner = owners[ranking]
    starts = jnp.searchsorted(sorted_owner, jnp.arange(devices, dtype=jnp.int32), side="left")
    ranked = jnp.arange(requests, dtype=jnp.int32) - starts[sorted_owner]
    position = jnp.zeros((requests,), jnp.int32).at[ranking].set(sorted_owner * capacity + ranked)
    send_slot = jnp.zeros((devices * capacity,), jnp.int32).at[position].set(row_slot)
    wanted = lax.all_to_all(
        send_slot.reshape(devices, capacity), GRP_DEV, split_axis=0, concat_axis=0, tiled=True
    )
    returned = lax.all_to_all(cold_table[wanted], GRP_DEV, split_axis=0, concat_axis=0, tiled=True)
    arrived = returned
    held_slot = wanted
    arrived = arrived.reshape(devices * capacity, row_width)
    held_slot = held_slot.reshape(devices * capacity)
    own_rows = arrived[position].reshape(samples, features, bag_size, row_width)
    pooled = own_rows[:, :, 0].astype(jnp.float32)
    pooled = pooled + own_rows[:, :, 1].astype(jnp.float32)
    hot_rows = hot_list[0][hot_index]
    pooled = pooled + hot_table[hot_rows].astype(jnp.float32)
    first_input = pooled.reshape(samples, features * row_width).astype(jnp.bfloat16)
    cross_low = jnp.dot(first_input, cross_u, preferred_element_type=jnp.float32).astype(
        jnp.bfloat16
    )
    cross_term = jnp.dot(cross_low, cross_v, preferred_element_type=jnp.float32) + cross_bias
    input_wide = first_input.astype(jnp.float32)
    cross_out = (input_wide * cross_term + input_wide).astype(jnp.bfloat16)
    hidden_in = contract_cols(cross_out, mlp_weight) + mlp_bias
    hidden = jax.nn.silu(hidden_in).astype(jnp.bfloat16)
    logits = jnp.dot(hidden, out_weight, preferred_element_type=jnp.float32)
    logit_grad = jax.nn.sigmoid(logits) - labels.astype(jnp.float32)
    out_grad = jnp.dot(logit_grad, hidden.astype(jnp.float32), precision=lax.Precision.HIGHEST)
    hidden_grad = (
        logit_grad[:, None] * out_weight.astype(jnp.float32)[None, :] * silu_slope(hidden_in)
    ).astype(jnp.bfloat16)
    bias_grad = jnp.sum(hidden_grad.astype(jnp.float32), axis=0)
    mlp_weight_grad = sum_by_chip_2(
        contract_rows(hidden_grad, cross_out), ("grp", "dev_0", "dev_1"), "dev_2", 0
    )
    cross_out_grad = jnp.dot(hidden_grad, mlp_weight, preferred_element_type=jnp.float32)
    term_grad = (cross_out_grad * input_wide).astype(jnp.bfloat16)
    cross_bias_part = jnp.sum(term_grad.astype(jnp.float32), axis=0)
    cross_v_part = contract_rows(cross_low, term_grad)
    low_grad = contract_cols(term_grad, cross_v).astype(jnp.bfloat16)
    cross_u_part = contract_rows(first_input, low_grad)
    pooled_grad = (cross_out_grad * (cross_term + 1.0) + contract_cols(low_grad, cross_u)).astype(
        jnp.bfloat16
    )
    grad_rows = jnp.broadcast_to(
        pooled_grad.reshape(samples, features, 1, row_width),
        (samples, features, bag_size, row_width),
    ).reshape(requests, row_width)
    send_grad = jnp.zeros((devices * capacity, row_width), jnp.bfloat16).at[position].set(grad_rows)
    came_grad = lax.all_to_all(send_grad, GRP_DEV, split_axis=0, concat_axis=0, tiled=True)
    cold_grad = (
        jnp.zeros((shard_rows, row_width), jnp.float32)
        .at[held_slot]
        .add(came_grad.astype(jnp.float32))
    )
    hot_slots = hot_list.shape[1]
    selector = (
        jnp.arange(hot_slots, dtype=jnp.int32)[:, None]
        == hot_index.reshape(samples * features)[None, :]
    ).astype(jnp.bfloat16)
    hot_block = jnp.dot(
        selector,
        pooled_grad.reshape(samples * features, row_width),
        preferred_element_type=jnp.float32,
    )
    every_row, every_block = (
        lax.all_gather(hot_list[0], GRP_DEV, axis=0, tiled=True),
        lax.all_gather(hot_block, GRP_DEV, axis=0, tiled=True),
    )
    hot_grad = jnp.zeros(hot_table.shape, jnp.float32).at[every_row].add(every_block)
    cross_u_grad, cross_v_grad, cross_bias_grad, mlp_bias_grad, out_weight_grad = in_one(
        (cross_u_part, cross_v_part, cross_bias_part, bias_grad, out_grad), GRP_DEV
    )
    return (
        cold_grad,
        hot_grad,
        mlp_weight_grad,
        cross_u_grad,
        cross_v_grad,
        cross_bias_grad,
        mlp_bias_grad,
        out_weight_grad,
    )


def solution(mesh):
    torus = Mesh(
        mesh.devices.reshape(mesh.shape["grp"], 4, 4, 2), ("grp", "dev_0", "dev_1", "dev_2")
    )
    placed = (
        P(GRP_DEV, None, None),
        P(),
        P(GRP_DEV, None),
        P(GRP_DEV, None),
        P(GRP_DEV, None),
        P(),
        P(GRP_DEV),
        P(),
        P(),
        P(),
        P(),
        P(),
        P(),
    )
    return jax.shard_map(
        per_device,
        mesh=torus,
        in_specs=placed,
        out_specs=(P(GRP_DEV, None), P(), P(GRP_DEV, None), P(), P(), P(), P(), P()),
        check_vma=False,
    )
```

profile of v0, /device:TPU:0, one launch (start us, length us, event | category | flops | bytes accessed | tf_op | source)
XLA Modules:
  0.0 616.4 jit_solution(11630705549396382278)
XLA Ops:
  9.9 17.5 %gather_fusion.1 = s32[3328]{0:T(1024)S(1)} fusion(s32[262144]{0:T(1024)S(1)} %copy-done.3, s32[4096]{0:T(1024)S(1)} %pad_clamp_fusion.5), kind=kCustom, calls=%fused_computation.1 | custom fusion | bytes 39936 | tf_op jit(solution)/shard_map/gather | solution.py:71
  27.5 5.8 sort.17
  33.2 17.5 %gather_fusion.2 = s32[3328]{0:T(1024)S(1)} fusion(s32[3328]{0:T(1024)S(1)} %get-tuple-element.114, s32[4096]{0:T(1024)S(1)} %pad_clamp_fusion.4), kind=kCustom, calls=%fused_computation.2 | custom fusion | bytes 39936 | tf_op jit(solution)/shard_map/gather | solution.py:75
  50.8 14.6 %while.24 = (s32[]{:T(128)}, u32[128]{0:T(128)S(1)}, u32[128]{0:T(128)S(1)}, s32[3328]{0:T(1024)S(1)}, s32[]{:T(128)}, /*index=5*/s32[]{:T(128)}, s32[]{}) while((s32[]{:T(128)}, u32[128]{0:T(128)S(1)}, u32[128]{0:T(128)S(1)}, s32[3328]{0:T(1024)S(1)}, s32[]{:T(128)}, /*index=5*/s32[]{:T(128)}, s32[]{}) %tuple.45), condition=%wide.region_2.3_spmd.clone, body=%wide.region_1.2_spmd.clone.sunk | while | flops 2692 | bytes 10348 | solution.py:76
  65.5 18.9 %gather_fusion.3 = s32[3328]{0:T(1024)S(1)} fusion(s32[128]{0:T(128)S(1)} %convert_element_type.74, s32[4096]{0:T(1024)S(1)} %pad_clamp_fusion.3), kind=kCustom, calls=%fused_computation.3 | custom fusion | bytes 39936 | tf_op jit(solution)/shard_map/gather | solution.py:77
  84.5 12.7 %scatter_custom_fusion = s32[3328]{0:T(1024)S(1)} fusion(s32[3328]{0:T(1024)S(1)} %compare_select_fusion.7, s32[3328]{0:T(1024)S(1)} %subtract_add_fusion, s32[]{:T(128)} %constant.40.clone.1), kind=kCustom, calls=%fused_computation.84 | custom fusion | bytes 13316 | tf_op jit(solution)/shard_map/scatter | solution.py:78
  97.2 12.7 %scatter_custom_fusion.1 = s32[4992]{0:T(1024)S(1)} fusion(s32[3328]{0:T(1024)S(1)} %compare_select_fusion.6, s32[3328]{0:T(1024)S(1)} %get-tuple-element.113, s32[]{:T(128)} %constant.40.clone.1), kind=kCustom, calls=%fused_computation.80 | custom fusion | bytes 19972 | tf_op jit(solution)/shard_map/scatter | solution.py:79
  110.2 20.3 %all_to_all.26 = s32[128,1,39]{2,1,0:T(1,128)S(1)} all-to-all(s32[128,1,39]{2,1,0:T(1,128)S(1)} %bitcast.65), channel_id=1, replica_groups=mesh['grp'=4,'dev_0'=4,'dev_1'=4,'dev_2'=2] {'grp','dev_0','dev_1','dev_2'}, dimensions={0} | all-to-all | bytes 39936 | tf_op jit(solution)/shard_map/all_to_all | solution.py:80
  130.7 10.0 %gather_fusion.4 = bf16[4992,128]{1,0:T(8,128)(2,1)S(1)} fusion(bf16[2048,128]{1,0:T(8,128)(2,1)S(1)} %copy-done.4, s32[5120]{0:T(1024)S(1)} %pad_clamp_fusion.1), kind=kCustom, calls=%fused_computation.4 | custom fusion | bytes 2575872 | tf_op jit(solution)/shard_map/gather | solution.py:83
  142.0 5.7 all-to-all-start.1
  148.3 9.8 %gather_fusion.6 = s32[1664]{0:T(1024)S(1)} fusion(s32[32]{0:T(128)S(1)} %bitcast.56, s32[2048]{0:T(1024)S(1)} %pad_clamp_fusion.7), kind=kCustom, calls=%fused_computation.6 | custom fusion | bytes 19968 | tf_op jit(solution)/shard_map/gather | solution.py:91
  158.6 3.9 gather_fusion.7
  163.8 5.5 all-to-all-done.1
  169.3 2.2 reshape.186
  171.5 6.5 %gather_fusion.5 = bf16[3328,128]{1,0:T(8,128)(2,1)S(1)} fusion(bf16[4992,128]{1,0:T(8,128)(2,1)S(1)} %reshape.186, s32[4096]{0:T(1024)S(1)} %pad_clamp_fusion.2), kind=kCustom, calls=%fused_computation.5 | custom fusion | bytes 1717248 | tf_op jit(solution)/shard_map/gather | solution.py:88
  186.3 5.3 multiply_convert_fusion.1
  192.8 6.9 %fusion.31 = f32[2048,1664]{1,0:T(8,128)} fusion(bf16[128,2048]{1,0:T(8,128)(2,1)S(1)} %get-tuple-element.102, f32[128,1664]{1,0:T(8,128)S(1)} %convolution_add_fusion.1, bf16[128,1664]{1,0:T(8,128)(2,1)S(1)} %add_convert_fusion), kind=kOutput, calls=%fused_computation.94 | convolution fusion | flops 873267200 | bytes 15433728 | tf_op jit(solution)/shard_map/dot_general | solution.py:39
  199.8 10.8 %copy.42 = f32[2,64,16,1664]{3,2,1,0:T(8,128)} copy(f32[2,64,16,1664]{3,2,0,1:T(8,128)} %bitcast.57) | data formatting | bytes 27262976 | tf_op jit(solution)/shard_map/transpose | solution.py:19
  210.9 5.0 convert_reduce_fusion.1
  217.6 1.7 fusion.38
  219.3 3.0 reshape.192
  234.7 14.0 %scatter_custom_fusion.2 = bf16[4992,128]{1,0:T(8,128)(2,1)S(1)} fusion(s32[3328]{0:T(1024)S(1)} %compare_select_fusion.6, bf16[3328,128]{1,0:T(8,128)(2,1)S(1)} %bitcast.63, bf16[]{:T(256)} %constant.78.clone.1), kind=kCustom, calls=%fused_computation.47 | custom fusion | bytes 1277954 | tf_op jit(solution)/shard_map/scatter | solution.py:125
  250.0 9.5 %all-to-all-start.2 = ((bf16[128,39,128]{2,1,0:T(8,128)(2,1)}), bf16[128,39,128]{2,1,0:T(8,128)(2,1)S(1)}, u32[]{:S(2)}, u32[]{:S(2)}) async-start(bf16[128,39,128]{2,1,0:T(8,128)(2,1)} %all_to_all.21), calls=%async_computation.2 | async-start | bytes 2621440 | tf_op jit(solution)/shard_map/all_to_all | solution.py:126
  259.7 80.3 %all-reduce = s32[4096]{0:T(1024)S(1)} all-reduce(s32[4096]{0:T(1024)S(1)} %bitcast_dynamic-update-slice_fusion), channel_id=2, replica_groups=mesh['grp'=4,'dev_0'=4,'dev_1'=4,'dev_2'=2] {'grp','dev_0','dev_1','dev_2'}, use_global_device_ids=true, to_apply=%add | all-reduce | flops 4096 | bytes 32768 | tf_op jit(solution)/shard_map/all_gather | solution.py:143
  341.6 1.7 reshape.289
  343.3 29.5 %scatter_custom_fusion.3 = f32[2048,128]{1,0:T(8,128)} fusion(s32[4992]{0:T(1024)S(1)} %fusion.20, f32[4992,128]{1,0:T(8,128)} %reshape.289, f32[]{:T(128)} %constant.35.clone.1), kind=kCustom, calls=%fused_computation.49 | custom fusion | flops 638976 | bytes 1049088 | tf_op jit(solution)/shard_map/scatter-add | solution.py:130
  372.8 13.2 %all-reduce.3.cloned.1.call-done = f32[857728]{0:T(1024)} async-done(((f32[857728]{0:T(1024)}), f32[857728]{0:T(1024)}) %all-reduce.3.cloned.1.call-update) | async-done | bytes 3430928 | tf_op jit(solution)/shard_map/psum | solution.py:26
  386.0 3.4 fusion.36
  389.4 2.7 reshape.193
  396.3 57.7 %all-gather.3.cloned.1.call-done = f32[4096,128]{1,0:T(8,128)} async-done(((f32[32,128]{1,0:T(8,128)}), f32[4096,128]{1,0:T(8,128)}) %all-gather.3.cloned.1.call-update) | async-done | bytes 2097168 | tf_op jit(solution)/shard_map/all_gather | solution.py:144
  454.0 24.1 %scatter_custom_fusion.4 = f32[4096,128]{1,0:T(8,128)} fusion(s32[4096]{0:T(1024)S(1)} %compare_select_fusion.5, f32[4096,128]{1,0:T(8,128)} %all-gather.3.cloned.1.call-done, f32[]{:T(128)} %constant.35.clone.1), kind=kCustom, calls=%fused_computation.37 | custom fusion | flops 524288 | bytes 2097664 | tf_op jit(solution)/shard_map/scatter-add | solution.py:146
  478.1 130.4 %reduce-scatter.5.cloned.1.call-done = f32[1,16,1664]{2,1,0:T(8,128)} async-done(((f32[64,16,1664]{2,1,0:T(8,128)}), f32[1,16,1664]{2,1,0:T(8,128)}) %reduce-scatter.5.cloned.1.call-update) | async-done | bytes 106512 | tf_op jit(solution)/shard_map/reduce_scatter | solution.py:21
  (162 shorter events, 50.9 us)
Async XLA Ops:
  8.0 150.6 %copy-start = (bf16[4096,128]{1,0:T(8,128)(2,1)S(1)}, bf16[4096,128]{1,0:T(8,128)(2,1)}, u32[]{:S(2)}) copy-start(bf16[4096,128]{1,0:T(8,128)(2,1)} %param.20) | copy-start | bytes 3145732
  8.0 1.8 copy-start.3
  84.4 46.3 %copy-start.4 = (bf16[2048,128]{1,0:T(8,128)(2,1)S(1)}, bf16[2048,128]{1,0:T(8,128)(2,1)}, u32[]{:S(2)}) copy-start(bf16[2048,128]{1,0:T(8,128)(2,1)} %param.17) | copy-start | bytes 1572868
  140.7 7.2 %copy-start.13 = (bf16[2048]{0:T(1024)(128)(2,1)S(1)}, bf16[2048]{0:T(1024)(128)(2,1)}, u32[]{:S(2)}) copy-start(bf16[2048]{0:T(1024)(128)(2,1)} %param.27) | copy-start | bytes 12292
  140.7 7.3 %copy-start.12 = (s32[128,13]{0,1:T(8,128)S(1)}, s32[128,13]{0,1:T(8,128)}, u32[]{:S(2)}) copy-start(s32[128,13]{0,1:T(8,128)} %param.18) | copy-start | bytes 19972
  140.7 7.6 %copy-start.2 = (s32[1,32]{1,0:T(1,128)S(1)}, s32[1,32]{1,0:T(1,128)}, u32[]{:S(2)}) copy-start(s32[1,32]{1,0:T(1,128)} %param.19) | copy-start | bytes 388
  142.0 27.3 %all-to-all-start.1 = ((bf16[128,39,128]{2,1,0:T(8,128)(2,1)}), bf16[128,39,128]{2,1,0:T(8,128)(2,1)}, u32[]{:S(2)}, u32[]{:S(2)}) async-start(bf16[128,39,128]{2,1,0:T(8,128)(2,1)} %reshape.230), calls=%async_computation.1 | async-start | bytes 2621440 | tf_op jit(solution)/shard_map/all_to_all | solution.py:83
  147.7 85.0 %reduce-scatter.3.cloned.1.call-start = ((), (), s32[]{:S(2)}) async-start(), calls=%async_computation.6 | async-start | bytes 20447232 | tf_op jit(solution)/shard_map/reduce_scatter | solution.py:20
  180.5 2.6 copy-start.8
  183.1 2.8 copy-start.7
  183.1 2.8 copy-start.14
  183.1 3.1 copy-start.16
  186.2 5.3 copy-start.15
  191.6 0.8 copy-start.10
  210.6 175.4 %all-reduce.3.cloned.1.call-start = ((), (), s32[]{:S(2)}) async-start(), calls=%async_computation.8 | async-start | bytes 6864896 | tf_op jit(solution)/shard_map/psum | solution.py:26
  222.3 2.5 copy-start.5
  224.7 4.1 copy-start.11
  226.1 4.8 copy-start.6
  226.1 4.8 copy-start.9
  230.5 223.5 %all-gather.3.cloned.1.call-start = ((), (), s32[]{:S(2)}) async-start(), calls=%async_computation.5 | async-start | bytes 2113536 | tf_op jit(solution)/shard_map/all_gather | solution.py:144
  232.6 375.9 %reduce-scatter.5.cloned.1.call-start = ((), (), s32[]{:S(2)}) async-start(), calls=%async_computation.7 | async-start | bytes 6922240 | tf_op jit(solution)/shard_map/reduce_scatter | solution.py:21
  250.0 91.6 %all-to-all-start.2 = ((bf16[128,39,128]{2,1,0:T(8,128)(2,1)}), bf16[128,39,128]{2,1,0:T(8,128)(2,1)S(1)}, u32[]{:S(2)}, u32[]{:S(2)}) async-start(bf16[128,39,128]{2,1,0:T(8,128)(2,1)} %all_to_all.21), calls=%async_computation.2 | async-start | bytes 2621440 | tf_op jit(solution)/shard_map/all_to_all | solution.py:126
  392.1 216.4 %copy-start.1 = (bf16[4096,128]{1,0:T(8,128)(2,1)S(1)}, bf16[4096,128]{1,0:T(8,128)(2,1)}, u32[]{:S(2)}) copy-start(bf16[4096,128]{1,0:T(8,128)(2,1)} %param.20) | copy-start | bytes 3145732
Sparse Core Ops, SparseCore 0:
  210.7 21.6 reduce-scatter.2
  236.4 372.0 reduce-scatter.4
Sparse Core Ops, SparseCore 1:
  230.6 155.4 all-reduce.2
  389.6 64.4 all-gather.2
where the time goes:
time: 624 us; the launch traced here: 616 us
  waiting for transfers between devices  208 us (33%)
  local copies, waits for them, and re-layouts  190 us (30%)
  blocking collectives  101 us (16%)
  other arithmetic  62.7 us (10%)
  matrix products  23.2 us (4%)
  between operations  16.6 us (3%)
  starting transfers between devices  15.8 us (3%)
    reduce_scatter x1, waiting for transfers between devices, sum_by_chip_2(): return lax.psum_scatter(tiles, chips, scatter_dimension=0, tiled=True)[0]  130 us
    all_gather x1, blocking collectives, per_device(): lax.all_gather(hot_list[0], GRP_DEV, axis=0, tiled=True)  80.3 us
    all_gather x1, waiting for transfers between devices, per_device(): lax.all_gather(hot_block, GRP_DEV, axis=0, tiled=True)  57.7 us
    scatter-add x1, other arithmetic, per_device(): cold_grad = jnp.zeros((shard_rows, row_width), jnp.float32).at[held_slot]...  29.5 us
    scatter-add x1, other arithmetic, per_device(): jnp.zeros(hot_table.shape, jnp.float32).at[every_row].add(every_block)  24.1 us
    all_to_all x1, blocking collectives, per_device(): lax.all_to_all(send_slot.reshape(devices, capacity), GRP_DEV, split_axis=...  20.3 us
    gather x1, local copies, waits for them, and re-layouts, per_device(): ranked = jnp.arange(requests, dtype=jnp.int32) - starts[sorted_owner]  18.9 us
    gather x1, local copies, waits for them, and re-layouts, per_device(): placed = location[ids.reshape(requests)]  17.5 us
  transfers between devices with their start and end apart: 6, of which 4 were waited for; matrix products, arithmetic and copies ran while one was open for 19% of the time, Pallas kernels for 0%

commit v1 on v0

v1 whole, which is shorter than its diff:
```python
import jax
import jax.numpy as jnp
from jax import lax
from jax.experimental import pallas as pl
from jax.experimental.pallas import tpu as pltpu
from jax.sharding import Mesh
from jax.sharding import PartitionSpec as P

GRP_DEV = ("grp", "dev_0", "dev_1", "dev_2")
CHIPS = ("grp", "dev_0", "dev_1")
CORE = "dev_2"
SWAP = [(0, 1), (1, 0)]
CAP = 40
HOT = 32
WAYS = 4
F32, BF16, I32 = jnp.float32, jnp.bfloat16, jnp.int32
VMEM = pl.BlockSpec(memory_space=pltpu.VMEM)
SMEM = pl.BlockSpec(memory_space=pltpu.SMEM)


def route_kernel(ids, hot_list, location, send, inverse, position, found):
    lane = lax.broadcasted_iota(I32, (1, 128), 1)
    rows = lax.broadcasted_iota(I32, (128, 128), 0)
    lanes = lax.broadcasted_iota(I32, (128, 128), 1)
    before = (lanes < rows).astype(BF16)
    diagonal = rows == lanes
    wide = lax.broadcasted_iota(I32, (128, 256), 1)
    wide_rank = wide & 63
    wide_part = wide >> 6
    wide_row = lax.broadcasted_iota(I32, (128, 256), 0)
    blocks = position.shape[0]
    features = blocks // 2

    def block(b, carried):
        seen, table = carried
        for j in range(128):
            number = ids[b, j]
            row = location[pl.ds(number >> 7, 1), :]
            found[pl.ds(j, 1), :] = jnp.where(lane == (number & 127), row, 0)
        placed = jnp.sum(found[...].astype(F32), axis=1, keepdims=True).astype(I32)
        owner = placed >> 11
        slot = (placed & 2047) + 1
        chosen = owner == lanes
        one_hot = chosen.astype(BF16)
        ahead = jnp.dot(before, one_hot, preferred_element_type=F32) + seen
        rank = jnp.sum(jnp.where(chosen, ahead, 0.0), axis=1, keepdims=True).astype(I32)
        seen = seen + jnp.sum(chosen.astype(F32), axis=0, keepdims=True)
        feature = jnp.where(b >= features, b - features, b)
        origin = feature * 128 + wide_row
        value = jnp.where(
            wide_part == 0,
            slot >> 4,
            jnp.where(
                wide_part == 1, slot & 15, jnp.where(wide_part == 2, origin >> 4, origin & 15)
            ),
        )
        value = jnp.where(wide_rank == rank, value, 0).astype(F32).astype(BF16)
        table = table + lax.dot_general(
            one_hot, value, (((0,), (0,)), ((), ())), preferred_element_type=F32
        )
        spot = jnp.where(diagonal, owner * CAP + rank, 0)
        position[pl.ds(b, 1), :] = jnp.sum(spot, axis=0, keepdims=True)
        return seen, table

    seen, table = lax.fori_loop(
        0, blocks, block, (jnp.zeros((1, 128), F32), jnp.zeros((128, 256), F32))
    )
    table = table.astype(I32)
    wanted = (table[:, :64] << 4) + table[:, 64:128] - 1
    wanted = jnp.where(wanted < 0, 2048, wanted)
    send[:, :CAP] = wanted[:, :CAP]
    send[:, CAP : CAP + 32] = jnp.broadcast_to(hot_list[...], (128, 32))
    send[:, CAP + 32 :] = jnp.zeros((128, 128 - CAP - 32), I32)
    inverse[...] = (table[:, 128:192] << 4) + table[:, 192:256]


def route(ids, hot_list, location):
    blocks = ids.shape[0]
    return pl.pallas_call(
        route_kernel,
        out_shape=(
            jax.ShapeDtypeStruct((128, 128), I32),
            jax.ShapeDtypeStruct((128, 64), I32),
            jax.ShapeDtypeStruct((blocks, 128), I32),
        ),
        in_specs=[SMEM, VMEM, VMEM],
        out_specs=(VMEM, VMEM, VMEM),
        scratch_shapes=[pltpu.VMEM((128, 128), I32)],
        name="route",
    )(ids, hot_list, location)


def fetch_kernel(wanted, table, out, wide, picked):
    shard = table.shape[0]
    wide[:shard, :] = table[...].astype(F32)
    wide[shard:, :] = jnp.zeros((8, 128), F32)

    def source(d, carried):
        for i in range(CAP):
            picked[pl.ds(d * CAP + i, 1), :] = wide[pl.ds(wanted[d, i], 1), :]
        return carried

    lax.fori_loop(0, out.shape[0] // CAP, source, 0)
    out[...] = picked[...].astype(BF16)


def fetch(wanted, table):
    count = wanted.shape[0] * CAP
    return pl.pallas_call(
        fetch_kernel,
        out_shape=jax.ShapeDtypeStruct((count, 128), BF16),
        in_specs=[SMEM, VMEM],
        out_specs=VMEM,
        scratch_shapes=[
            pltpu.VMEM((table.shape[0] + 8, 128), F32),
            pltpu.VMEM((count, 128), F32),
        ],
        name="fetch",
    )(wanted, table)


def cold_kernel(wanted, came, out, wide, *sums):
    for way in sums:
        way[...] = jnp.zeros(way.shape, F32)
    wide[...] = came[...].astype(F32)

    def source(d, carried):
        for i in range(CAP // WAYS):
            for k, way in enumerate(sums):
                at = k * (CAP // WAYS) + i
                here = pl.ds(wanted[d, at], 1)
                way[here, :] = way[here, :] + wide[d, at : at + 1, :]
        return carried

    lax.fori_loop(0, wide.shape[0], source, 0)
    shard = out.shape[0]
    total = sums[0][:shard, :]
    for way in sums[1:]:
        total = total + way[:shard, :]
    out[...] = total


def cold_sum(wanted, came, shard_rows):
    return pl.pallas_call(
        cold_kernel,
        out_shape=jax.ShapeDtypeStruct((shard_rows, 128), F32),
        in_specs=[SMEM, VMEM],
        out_specs=VMEM,
        scratch_shapes=[pltpu.VMEM(came.shape, F32)]
        + [pltpu.VMEM((shard_rows + 8, 128), F32)] * WAYS,
        name="cold_sum",
    )(wanted, came)


def hot_kernel(listed, came, out, wide):
    out[...] = jnp.zeros(out.shape, F32)
    wide[...] = came[...].astype(F32)

    def source(d, carried):
        places = [pl.ds(listed[d, CAP + i], 1) for i in range(HOT)]
        held = [out[here, :] + wide[d, i : i + 1, :] for i, here in enumerate(places)]
        for here, row in zip(places, held):
            out[here, :] = row
        return carried

    lax.fori_loop(0, came.shape[0], source, 0)


def hot_sum(listed, came, hot_rows):
    return pl.pallas_call(
        hot_kernel,
        out_shape=jax.ShapeDtypeStruct((hot_rows, 128), F32),
        in_specs=[SMEM, VMEM],
        out_specs=VMEM,
        scratch_shapes=[pltpu.VMEM(came.shape, F32)],
        name="hot_sum",
    )(listed, came)


def silu_slope(values):
    squash = jax.nn.sigmoid(values)
    return squash * (1.0 + values * (1.0 - squash))


def contract_rows(former, latter):
    return lax.dot_general(former, latter, (((0,), (0,)), ((), ())), preferred_element_type=F32)


def contract_cols(former, latter):
    return lax.dot_general(former, latter, (((1,), (1,)), ((), ())), preferred_element_type=F32)


def exchange(x, axes):
    return lax.all_to_all(x, axes, split_axis=0, concat_axis=0, tiled=True)


def by_core(x):
    return x.reshape(-1, 2, 16, *x.shape[1:]).swapaxes(0, 1).reshape(x.shape)


def from_core(x):
    return x.reshape(2, -1, 16).swapaxes(0, 1).reshape(-1)


def per_device(
    ids,
    location,
    cold_table,
    hot_index,
    hot_list,
    hot_table,
    labels,
    cross_u,
    cross_v,
    cross_bias,
    mlp_weight,
    mlp_bias,
    out_weight,
):
    devices = lax.axis_size(GRP_DEV)
    chips = lax.axis_size(CHIPS)
    samples, features, bag_size = ids.shape
    width = cold_table.shape[1]
    pairs = samples * features
    hidden_units, inputs = mlp_weight.shape
    rank = cross_u.shape[1]
    core = lax.axis_index(CORE)

    ids_rows = ids.transpose(2, 1, 0).reshape(bag_size * features, samples)
    send, inverse, position = route(ids_rows, hot_list, location.reshape(-1, 128))
    got = exchange(send.reshape(devices, 1, 128), GRP_DEV).reshape(devices, 128)
    rows = fetch(got, cold_table)
    arrived = exchange(rows.reshape(devices, CAP, width), GRP_DEV).reshape(devices * CAP, width)

    mlp_weight = by_core(mlp_weight)
    mlp_bias = by_core(mlp_bias)
    out_weight = by_core(out_weight)
    hot_pick = (
        hot_index.T.reshape(pairs)[:, None] == jnp.arange(HOT, dtype=I32)[None, :]
    ).astype(BF16)
    hot_part = jnp.dot(hot_pick, hot_table[hot_list[0]], preferred_element_type=F32)

    own = arrived[position.reshape(-1)].reshape(bag_size, pairs, width)
    pooled = own[0].astype(F32) + own[1].astype(F32) + hot_part
    first_input = (
        pooled.reshape(features, samples, width)
        .swapaxes(0, 1)
        .reshape(samples, inputs)
        .astype(BF16)
    )
    cross_low = jnp.dot(first_input, cross_u, preferred_element_type=F32).astype(BF16)
    cross_term = jnp.dot(cross_low, cross_v, preferred_element_type=F32) + cross_bias
    input_wide = first_input.astype(F32)
    cross_out = (input_wide * cross_term + input_wide).astype(BF16)
    hidden_in = contract_cols(cross_out, mlp_weight) + mlp_bias
    hidden = jax.nn.silu(hidden_in).astype(BF16)
    logits = jnp.dot(hidden, out_weight, preferred_element_type=F32)
    logit_grad = jax.nn.sigmoid(logits) - labels.astype(F32)
    out_grad = jnp.dot(logit_grad, hidden.astype(F32), precision=lax.Precision.HIGHEST)
    hidden_grad = (
        logit_grad[:, None] * out_weight.astype(F32)[None, :] * silu_slope(hidden_in)
    ).astype(BF16)
    bias_grad = jnp.sum(hidden_grad.astype(F32), axis=0)

    half = hidden_units // 2
    mine = lax.dynamic_slice(hidden_grad, (0, core * half), (samples, half))
    other = lax.dynamic_slice(hidden_grad, (0, (1 - core) * half), (samples, half))
    other = lax.ppermute(jnp.concatenate([other, cross_out], axis=1), CORE, SWAP)
    mlp_part = contract_rows(
        jnp.concatenate([mine, other[:, :half]], axis=0),
        jnp.concatenate([cross_out, other[:, half:]], axis=0),
    ).astype(BF16)
    mlp_parts = exchange(mlp_part.reshape(chips, half // chips, inputs), CHIPS)
    mlp_weight_grad = jnp.sum(mlp_parts.astype(F32), axis=0)

    cross_out_grad = jnp.dot(hidden_grad, mlp_weight, preferred_element_type=F32)
    term_grad = (cross_out_grad * input_wide).astype(BF16)
    cross_bias_part = jnp.sum(term_grad.astype(F32), axis=0)
    low_grad = contract_cols(term_grad, cross_v).astype(BF16)
    pooled_grad = (
        cross_out_grad * (cross_term + 1.0) + contract_cols(low_grad, cross_u)
    ).astype(BF16)

    grad_rows = pooled_grad.reshape(samples, features, width).swapaxes(0, 1).reshape(pairs, width)
    hot_block = contract_rows(hot_pick, grad_rows).astype(BF16)
    payload = jnp.concatenate(
        [
            grad_rows[inverse[:, :CAP].reshape(-1)].reshape(devices, CAP, width),
            jnp.broadcast_to(hot_block[None], (devices, HOT, width)),
        ],
        axis=1,
    )
    back = exchange(payload, GRP_DEV)
    cold_grad = cold_sum(got, back[:, :CAP], cold_table.shape[0])
    hot_grad = hot_sum(got, back[:, CAP:], hot_table.shape[0])

    first = core == 0
    pair_u = jnp.concatenate([low_grad, first_input], axis=1)
    pair_v = jnp.concatenate([cross_low, term_grad], axis=1)
    held = jnp.where(first, pair_u, pair_v)
    came = lax.ppermute(jnp.where(first, pair_v, pair_u), CORE, SWAP)
    both = jnp.concatenate([held, came], axis=0)
    cross_part = contract_rows(both[:, :rank], both[:, rank:])
    vectors = jnp.concatenate([cross_bias_part, bias_grad, out_grad])
    vector_rows = vectors.size // 128
    vectors = jnp.pad(vectors.reshape(vector_rows, 128), ((0, rank - vector_rows), (0, 0)))
    cross_part = jnp.concatenate([cross_part, vectors], axis=1).astype(BF16)
    cross_parts = exchange(cross_part.reshape(chips, rank // chips, inputs + 128), CHIPS)
    cross_sum = jnp.sum(cross_parts.astype(F32), axis=0).astype(BF16)
    cross_full = exchange(jnp.broadcast_to(cross_sum[None], cross_parts.shape), CHIPS)
    cross_full = cross_full.reshape(rank, inputs + 128)
    cross_other = lax.ppermute(cross_full, CORE, SWAP)
    cross_u_grad = jnp.where(first, cross_full, cross_other)[:, :inputs].astype(F32).T
    cross_v_grad = jnp.where(first, cross_other, cross_full)[:, :inputs].astype(F32)
    vectors = (
        cross_full[:vector_rows, inputs:].astype(F32)
        + cross_other[:vector_rows, inputs:].astype(F32)
    ).reshape(-1)
    return (
        cold_grad,
        hot_grad,
        mlp_weight_grad,
        cross_u_grad,
        cross_v_grad,
        vectors[:inputs],
        from_core(vectors[inputs : inputs + hidden_units]),
        from_core(vectors[inputs + hidden_units :]),
    )


def solution(mesh):
    torus = Mesh(
        mesh.devices.reshape(mesh.shape["grp"], 4, 4, 2), ("grp", "dev_0", "dev_1", "dev_2")
    )
    placed = (
        P(GRP_DEV, None, None),
        P(),
        P(GRP_DEV, None),
        P(GRP_DEV, None),
        P(GRP_DEV, None),
        P(),
        P(GRP_DEV),
        P(),
        P(),
        P(),
        P(),
        P(),
        P(),
    )
    return jax.shard_map(
        per_device,
        mesh=torus,
        in_specs=placed,
        out_specs=(P(GRP_DEV, None), P(), P(GRP_DEV, None), P(), P(), P(), P(), P()),
        check_vma=False,
    )
```

time: 624 us -> 250 us (0.40)
  local copies, waits for them, and re-layouts: 190 us -> 43.7 us
  waiting for transfers between devices: 208 us -> 72.5 us
  blocking collectives: 101 us -> 21 us
  other arithmetic: 62.7 us -> 12.6 us
  Pallas kernels: 0 us -> 48.5 us
  between operations: 16.6 us -> 1.1 us
  starting transfers between devices: 15.8 us -> 30.8 us
    reduce_scatter x2 -> x0, waiting for transfers between devices: 130 us -> none  [the longest x1 130 us: sum_by_chip_2(): return lax.psum_scatter(tiles, chips, scatter_dimension=0, tiled=True)[0]]
    all_gather x1 -> x0, blocking collectives: 80.3 us -> none  [per_device(): lax.all_gather(hot_list[0], GRP_DEV, axis=0, tiled=True)]
    gather x21 -> x3, local copies, waits for them, and re-layouts: 99.5 us -> 22.2 us  [the longest x1 15.1 us: per_device(): grad_rows[inverse[:, :CAP].reshape(-1)].reshape(devices, CAP, width)]
    all_to_all x2 -> x5, waiting for transfers between devices: 5.46 us -> 68.8 us  [exchange(): return lax.all_to_all(x, axes, split_axis=0, concat_axis=0, tiled=True)]
    all_gather x1 -> x0, waiting for transfers between devices: 57.7 us -> none  [per_device(): lax.all_gather(hot_block, GRP_DEV, axis=0, tiled=True)]
    scatter-add x2 -> x0, other arithmetic: 53.6 us -> none  [the longest x1 29.5 us: per_device(): cold_grad = jnp.zeros((shard_rows, row_width), jnp.float32).at[held_slot]...]
    pallas_call x0 -> x4, Pallas kernels: none -> 48.5 us  [the longest x1 18.5 us: route(): pl.pallas_call(route_kernel, out_shape=(jax.ShapeDtypeStruct((128, 128),...]
    scatter x3 -> x0, local copies, waits for them, and re-layouts: 39.5 us -> none  [the longest x1 14 us: per_device(): jnp.zeros((devices * capacity, row_width), jnp.bfloat16).at[position]]
  transfers between devices with their start and end apart: 6 -> 8, of which waited for: 4 -> 6; matrix products, arithmetic and copies ran while one was open for 19% -> 18% of each run, Pallas kernels for 0% -> 9%
where the time goes in v1:
time: 250 us; the launch traced here: 248 us
  waiting for transfers between devices  72.5 us (29%)
  Pallas kernels  48.5 us (19%)
  local copies, waits for them, and re-layouts  43.7 us (17%)
  starting transfers between devices  30.8 us (12%)
  blocking collectives  21 us (8%)
  matrix products  18.2 us (7%)
  other arithmetic  12.6 us (5%)
    all_to_all x5, waiting for transfers between devices, exchange(): return lax.all_to_all(x, axes, split_axis=0, concat_axis=0, tiled=True)  68.8 us
    all_to_all x5, starting transfers between devices, exchange(): return lax.all_to_all(x, axes, split_axis=0, concat_axis=0, tiled=True)  30.7 us
    all_to_all x1, blocking collectives, exchange(): return lax.all_to_all(x, axes, split_axis=0, concat_axis=0, tiled=True)  21 us
    pallas_call x1, Pallas kernels, route(): pl.pallas_call(route_kernel, out_shape=(jax.ShapeDtypeStruct((128, 128),...  18.5 us
    gather x1, local copies, waits for them, and re-layouts, per_device(): grad_rows[inverse[:, :CAP].reshape(-1)].reshape(devices, CAP, width)  15.1 us
    pallas_call x1, Pallas kernels, cold_sum(): pl.pallas_call(cold_kernel, out_shape=jax.ShapeDtypeStruct((shard_rows, 1...  11.4 us
    pallas_call x1, Pallas kernels, hot_sum(): pl.pallas_call(hot_kernel, out_shape=jax.ShapeDtypeStruct((hot_rows, 128)...  10.8 us
    pallas_call x1, Pallas kernels, fetch(): pl.pallas_call(fetch_kernel, out_shape=jax.ShapeDtypeStruct((count, 128),...  7.83 us
  transfers between devices with their start and end apart: 8, of which 6 were waited for; matrix products, arithmetic and copies ran while one was open for 18% of the time, Pallas kernels for 9%

profile of v1, /device:TPU:0, one launch (start us, length us, event | category | flops | bytes accessed | tf_op | source)
XLA Modules:
  0.0 248.5 jit_solution(1797756625400803497)
XLA Ops:
  2.1 18.5 %route.1 = (s32[128,128]{1,0:T(8,128)}, s32[128,64]{1,0:T(8,128)}, s32[26,128]{1,0:T(8,128)}) custom-call(s32[26,128]{1,0:T(8,128)} %reshape.201.ids, s32[1,32]{1,0:T(1,128)} %hot_list.1, s32[2048,128]{1,0:T(8,128)} %bitcast.94), custom_call_target="tpu_custom_call" | custom-call | tf_op jit(solution)/shard_map/route/pallas_call | solution.py:79
  20.6 21.0 %all_to_all.30 = s32[128,1,128]{2,1,0:T(1,128)} all-to-all(s32[128,1,128]{2,1,0:T(1,128)} %bitcast.106), channel_id=1, replica_groups=mesh['grp'=4,'dev_0'=4,'dev_1'=4,'dev_2'=2] {'grp','dev_0','dev_1','dev_2'}, dimensions={0} | all-to-all | bytes 131072 | tf_op jit(solution)/shard_map/all_to_all | solution.py:194
  41.6 7.8 %fetch.1 = bf16[5120,128]{1,0:T(8,128)(2,1)} custom-call(s32[128,128]{1,0:T(8,128)} %bitcast.95, bf16[2048,128]{1,0:T(8,128)(2,1)} %table.1), custom_call_target="tpu_custom_call" | custom-call | tf_op jit(solution)/shard_map/fetch/pallas_call | solution.py:109
  49.4 4.8 %all-to-all-start.1 = ((bf16[128,40,128]{2,1,0:T(8,128)(2,1)}), bf16[128,40,128]{2,1,0:T(8,128)(2,1)S(1)}, u32[]{:S(2)}, u32[]{:S(2)}) async-start(bf16[128,40,128]{2,1,0:T(8,128)(2,1)} %bitcast.88), calls=%async_computation.1 | async-start | bytes 2621440 | tf_op jit(solution)/shard_map/all_to_all | solution.py:194
  54.7 6.3 %copy.52 = bf16[2,64,16,1664]{3,2,1,0:T(8,128)(2,1)} copy(bf16[2,64,16,1664]{3,2,0,1:T(8,128)(2,1)} %bitcast.87) | data formatting | bytes 13631488 | tf_op jit(solution)/shard_map/transpose | solution.py:198
  61.7 14.4 %all-to-all-done.1 = bf16[128,40,128]{2,1,0:T(8,128)(2,1)S(1)} async-done(((bf16[128,40,128]{2,1,0:T(8,128)(2,1)}), bf16[128,40,128]{2,1,0:T(8,128)(2,1)S(1)}, u32[]{:S(2)}, u32[]{:S(2)}) %all-to-all-start.1) | async-done | bytes 1310752 | tf_op jit(solution)/shard_map/all_to_all | solution.py:194
  76.1 6.5 %gather_fusion = bf16[3328,128]{1,0:T(8,128)(2,1)S(1)} fusion(bf16[5120,128]{1,0:T(8,128)(2,1)S(1)} %bitcast.86, s32[4096]{0:T(1024)S(1)} %pad_clamp_fusion), kind=kCustom, calls=%fused_computation | custom fusion | bytes 1717248 | tf_op jit(solution)/shard_map/gather | solution.py:243
  83.6 1.5 convolution_convert_fusion.3
  85.1 1.2 fusion.8
  86.4 5.5 %multiply_convert_fusion.1 = (bf16[128,2048]{1,0:T(8,128)(2,1)S(1)}, f32[128,2048]{1,0:T(8,128)S(1)}) fusion(f32[2048]{0:T(1024)S(1)} %add.106, bf16[128,1664]{1,0:T(8,128)(2,1)S(1)} %get-tuple-element.58, bf16[2048,1664]{1,0:T(8,128)(2,1)} %bitcast.82), kind=kOutput, calls=%fused_computation.26 | convolution fusion | flops 873988096 | bytes 8822784 | tf_op jit(solution)/shard_map/dot_general | solution.py:190
  92.7 2.1 fusion.27
  96.6 1.6 collective-permute-done.1
  99.0 1.5 convolution_convert_fusion.1
  100.7 1.3 pad_maximum_fusion.1
  102.0 4.8 %all-to-all-start.4 = ((bf16[64,4,1792]{2,1,0:T(4,128)(2,1)}), bf16[64,4,1792]{2,1,0:T(4,128)(2,1)S(1)}, u32[]{:S(2)}, u32[]{:S(2)}) async-start(bf16[64,4,1792]{2,1,0:T(4,128)(2,1)} %pad_maximum_fusion.1), calls=%async_computation.4 | async-start | bytes 1835008 | tf_op jit(solution)/shard_map/all_to_all | solution.py:194
  106.9 17.9 %all-to-all-done.4 = bf16[64,4,1792]{2,1,0:T(4,128)(2,1)S(1)} async-done(((bf16[64,4,1792]{2,1,0:T(4,128)(2,1)}), bf16[64,4,1792]{2,1,0:T(4,128)(2,1)S(1)}, u32[]{:S(2)}, u32[]{:S(2)}) %all-to-all-start.4) | async-done | bytes 917536 | tf_op jit(solution)/shard_map/all_to_all | solution.py:194
  126.4 5.7 %all-to-all-start.5 = ((bf16[64,4,1792]{2,1,0:T(4,128)(2,1)}), bf16[64,4,1792]{2,1,0:T(4,128)(2,1)}, u32[]{:S(2)}, u32[]{:S(2)}) async-start(bf16[64,4,1792]{2,1,0:T(4,128)(2,1)} %broadcast_in_dim.5), calls=%async_computation.5 | async-start | bytes 1835008 | tf_op jit(solution)/shard_map/all_to_all | solution.py:194
  132.1 1.6 fusion.1
  134.2 15.1 %gather_fusion.2 = bf16[5120,128]{1,0:T(8,128)(2,1)S(1)} fusion(bf16[1664,128]{1,0:T(8,128)(2,1)S(1)} %bitcast.80, s32[5120]{0:T(1024)S(1)} %broadcast_clamp_fusion), kind=kCustom, calls=%fused_computation.2 | custom fusion | bytes 2641920 | tf_op jit(solution)/shard_map/gather | solution.py:288
  150.1 1.6 pad_maximum_fusion
  151.7 9.9 %all-to-all-start.2 = ((bf16[128,72,128]{2,1,0:T(8,128)(2,1)}), bf16[128,72,128]{2,1,0:T(8,128)(2,1)S(1)}, u32[]{:S(2)}, u32[]{:S(2)}) async-start(bf16[128,72,128]{2,1,0:T(8,128)(2,1)} %pad_maximum_fusion), calls=%async_computation.2 | async-start | bytes 4718592 | tf_op jit(solution)/shard_map/all_to_all | solution.py:194
  163.9 2.1 collective-permute-done
  166.1 2.9 %convolution_convert_fusion = bf16[1024,1664]{1,0:T(8,128)(2,1)} fusion(bf16[128,1664]{1,0:T(8,128)(2,1)S(1)} %slice.83, bf16[128,1664]{1,0:T(8,128)(2,1)S(1)} %copy-done.7, bf16[128,1024]{1,0:T(8,128)(2,1)S(1)} %slice.82, bf16[128,1024]{1,0:T(8,128)(2,1)S(1)} %get-tuple-element.54), kind=kOutput, calls=%fused_computation.4 | convolution fusion | flops 876871680 | bytes 4784128 | tf_op jit(solution)/shard_map/dot_general | solution.py:186
  169.0 25.8 %all-to-all-done.2 = bf16[128,72,128]{2,1,0:T(8,128)(2,1)S(1)} async-done(((bf16[128,72,128]{2,1,0:T(8,128)(2,1)}), bf16[128,72,128]{2,1,0:T(8,128)(2,1)S(1)}, u32[]{:S(2)}, u32[]{:S(2)}) %all-to-all-start.2) | async-done | bytes 2359328 | tf_op jit(solution)/shard_map/all_to_all | solution.py:194
  194.8 5.6 %all-to-all-start.3 = ((bf16[64,16,1664]{2,1,0:T(8,128)(2,1)}), bf16[64,16,1664]{2,1,0:T(8,128)(2,1)}, u32[]{:S(2)}, u32[]{:S(2)}) async-start(bf16[64,16,1664]{2,1,0:T(8,128)(2,1)} %bitcast.92), calls=%async_computation.3 | async-start | bytes 6815744 | tf_op jit(solution)/shard_map/all_to_all | solution.py:194
  200.4 2.4 reshape.219
  203.9 11.4 %cold_sum.1 = f32[2048,128]{1,0:T(8,128)} custom-call(s32[128,128]{1,0:T(8,128)} %bitcast.96, bf16[128,40,128]{2,1,0:T(8,128)(2,1)} %slice.80.came), custom_call_target="tpu_custom_call" | custom-call | tf_op jit(solution)/shard_map/cold_sum/pallas_call | solution.py:144
  216.4 10.8 %hot_sum.1 = f32[4096,128]{1,0:T(8,128)} custom-call(s32[128,128]{1,0:T(8,128)} %bitcast.97, bf16[128,32,128]{2,1,0:T(8,128)(2,1)} %slice.81.came), custom_call_target="tpu_custom_call" | custom-call | tf_op jit(solution)/shard_map/hot_sum/pallas_call | solution.py:170
  227.2 2.8 %select_convert_fusion = (f32[256,1664]{1,0:T(8,128)}, f32[1664,256]{0,1:T(8,128)S(1)}) fusion(pred[]{:T(512)S(6)} %eq.22, bf16[256,1792]{1,0:T(8,128)(2,1)} %collective-permute-done.2, bf16[256,1792]{1,0:T(8,128)(2,1)} %reshape.219), kind=kLoop, calls=%fused_computation.36 | loop fusion | flops 1703936 | bytes 5111809 | tf_op jit(solution)/shard_map/convert_element_type | solution.py:314
  230.0 1.6 copy.60
  234.7 10.6 %all-to-all-done.3 = bf16[64,16,1664]{2,1,0:T(8,128)(2,1)} async-done(((bf16[64,16,1664]{2,1,0:T(8,128)(2,1)}), bf16[64,16,1664]{2,1,0:T(8,128)(2,1)}, u32[]{:S(2)}, u32[]{:S(2)}) %all-to-all-start.3) | async-done | bytes 3407904 | tf_op jit(solution)/shard_map/all_to_all | solution.py:194
  245.4 3.1 %convert_reduce_fusion = f32[16,1664]{1,0:T(8,128)} fusion(bf16[64,16,1664]{2,1,0:T(8,128)(2,1)} %all-to-all-done.3), kind=kLoop, calls=%fused_computation.3 | loop fusion | flops 3381248 | bytes 3514368 | tf_op jit(solution)/shard_map/reduce_sum | solution.py:274
  (93 shorter events, 17.6 us)
Async XLA Ops:
  0.6 60.4 %copy-start = (bf16[4096,128]{1,0:T(8,128)(2,1)S(1)}, bf16[4096,128]{1,0:T(8,128)(2,1)}, u32[]{:S(2)}) copy-start(bf16[4096,128]{1,0:T(8,128)(2,1)} %param.18) | copy-start | bytes 3145732
  41.6 12.6 %copy-start.12 = (bf16[2048]{0:T(1024)(128)(2,1)S(1)}, bf16[2048]{0:T(1024)(128)(2,1)}, u32[]{:S(2)}) copy-start(bf16[2048]{0:T(1024)(128)(2,1)} %param.25) | copy-start | bytes 12292
  49.4 5.1 %copy-start.11 = (f32[2048]{0:T(1024)S(1)}, f32[2048]{0:T(1024)}, u32[]{:S(2)}) copy-start(f32[2048]{0:T(1024)} %param.24) | copy-start | bytes 24580
  49.4 26.7 %all-to-all-start.1 = ((bf16[128,40,128]{2,1,0:T(8,128)(2,1)}), bf16[128,40,128]{2,1,0:T(8,128)(2,1)S(1)}, u32[]{:S(2)}, u32[]{:S(2)}) async-start(bf16[128,40,128]{2,1,0:T(8,128)(2,1)} %bitcast.88), calls=%async_computation.1 | async-start | bytes 2621440 | tf_op jit(solution)/shard_map/all_to_all | solution.py:194
  54.7 6.3 %copy-start.13 = (s32[1,32]{1,0:T(1,128)S(1)}, s32[1,32]{1,0:T(1,128)}, u32[]{:S(2)}) copy-start(s32[1,32]{1,0:T(1,128)} %hot_list.1) | copy-start | bytes 388
  54.7 6.9 %copy-start.9 = (s32[26,128]{1,0:T(8,128)S(1)}, s32[26,128]{1,0:T(8,128)}, u32[]{:S(2)}) copy-start(s32[26,128]{1,0:T(8,128)} %get-tuple-element.12) | copy-start | bytes 39940
  76.1 6.5 %copy-start.15 = (s32[128,13]{0,1:T(8,128)S(1)}, s32[128,13]{0,1:T(8,128)}, u32[]{:S(2)}) copy-start(s32[128,13]{0,1:T(8,128)} %param.16) | copy-start | bytes 19972
  83.1 2.0 copy-start.2
  83.1 2.0 copy-start.10
  86.3 5.5 %copy-start.6 = (bf16[128,1664]{1,0:T(8,128)(2,1)}, bf16[128,1664]{1,0:T(8,128)(2,1)S(1)}, u32[]{:S(2)}) copy-start(bf16[128,1664]{1,0:T(8,128)(2,1)S(1)} %get-tuple-element.58) | copy-start | bytes 1277956
  86.3 6.3 %slice-start = ((s8[6815744]{0:T(1024)(128)(4,1)}), s8[4194304]{0:T(1024)(128)(4,1)S(1)}, s32[]{:S(2)}) async-start(s8[6815744]{0:T(1024)(128)(4,1)} %bitcast.83), calls=%async_computation.6 | async-start | bytes 8388608
  86.3 5.5 %copy-start.14 = (s32[128]{0:T(128)S(1)}, s32[128]{0:T(128)}, u32[]{:S(2)}) copy-start(s32[128]{0:T(128)} %param.19) | copy-start | bytes 1540
  86.4 6.3 %slice-start.1 = ((s8[6815744]{0:T(1024)(128)(4,1)}), s8[2621440]{0:T(1024)(128)(4,1)S(1)}, s32[]{:S(2)}) async-start(s8[6815744]{0:T(1024)(128)(4,1)} %bitcast.83), calls=%async_computation.7 | async-start | bytes 5242880
  92.7 2.1 copy-start.1
  94.7 1.4 copy-start.8
  96.1 2.1 collective-permute-start.1
  98.2 0.8 copy-start.5
  102.0 22.8 %all-to-all-start.4 = ((bf16[64,4,1792]{2,1,0:T(4,128)(2,1)}), bf16[64,4,1792]{2,1,0:T(4,128)(2,1)S(1)}, u32[]{:S(2)}, u32[]{:S(2)}) async-start(bf16[64,4,1792]{2,1,0:T(4,128)(2,1)} %pad_maximum_fusion.1), calls=%async_computation.4 | async-start | bytes 1835008 | tf_op jit(solution)/shard_map/all_to_all | solution.py:194
  106.9 25.2 %copy-start.3 = (bf16[1664,256]{1,0:T(8,128)(2,1)S(1)}, bf16[1664,256]{1,0:T(8,128)(2,1)}, u32[]{:S(2)}) copy-start(bf16[1664,256]{1,0:T(8,128)(2,1)} %param.20) | copy-start | bytes 2555908
  125.2 6.9 %copy-start.4 = (f32[128,1664]{1,0:T(8,128)S(1)}, f32[128,1664]{1,0:T(8,128)}, u32[]{:S(2)}) copy-start(f32[128,1664]{1,0:T(8,128)} %get-tuple-element.59) | copy-start | bytes 2555908
  126.4 25.3 %all-to-all-start.5 = ((bf16[64,4,1792]{2,1,0:T(4,128)(2,1)}), bf16[64,4,1792]{2,1,0:T(4,128)(2,1)}, u32[]{:S(2)}, u32[]{:S(2)}) async-start(bf16[64,4,1792]{2,1,0:T(4,128)(2,1)} %broadcast_in_dim.5), calls=%async_computation.5 | async-start | bytes 1835008 | tf_op jit(solution)/shard_map/all_to_all | solution.py:194
  151.7 43.1 %all-to-all-start.2 = ((bf16[128,72,128]{2,1,0:T(8,128)(2,1)}), bf16[128,72,128]{2,1,0:T(8,128)(2,1)S(1)}, u32[]{:S(2)}, u32[]{:S(2)}) async-start(bf16[128,72,128]{2,1,0:T(8,128)(2,1)} %pad_maximum_fusion), calls=%async_computation.2 | async-start | bytes 4718592 | tf_op jit(solution)/shard_map/all_to_all | solution.py:194
  161.6 4.5 %copy-start.7 = (bf16[128,1664]{1,0:T(8,128)(2,1)S(1)}, bf16[128,1664]{1,0:T(8,128)(2,1)}, u32[]{:S(2)}) copy-start(bf16[128,1664]{1,0:T(8,128)(2,1)} %copy-done.6) | copy-start | bytes 1277956
  163.8 2.2 collective-permute-start
  194.8 50.6 %all-to-all-start.3 = ((bf16[64,16,1664]{2,1,0:T(8,128)(2,1)}), bf16[64,16,1664]{2,1,0:T(8,128)(2,1)}, u32[]{:S(2)}, u32[]{:S(2)}) async-start(bf16[64,16,1664]{2,1,0:T(8,128)(2,1)} %bitcast.92), calls=%async_computation.3 | async-start | bytes 6815744 | tf_op jit(solution)/shard_map/all_to_all | solution.py:194
  202.8 24.4 %collective-permute-start.2 = (bf16[256,1792]{1,0:T(8,128)(2,1)}, bf16[256,1792]{1,0:T(8,128)(2,1)}, u32[]{:S(2)}, u32[]{:S(2)}) collective-permute-start(bf16[256,1792]{1,0:T(8,128)(2,1)} %reshape.219), channel_id=1, source_target_pairs={{0,1},{1,0},{2,3},{3,2},{4,5},{5,4},{6,7},{7,6},{8,9},{9,8},{10,11... | collective-permute-start | bytes 2752520 | tf_op jit(solution)/shard_map/ppermute | solution.py:312

commit v2 on v1

--- a/solution.py
+++ b/solution.py
@@ -6,71 +6,76 @@
 from jax.sharding import Mesh
 from jax.sharding import PartitionSpec as P
 
+
 GRP_DEV = ("grp", "dev_0", "dev_1", "dev_2")
 CHIPS = ("grp", "dev_0", "dev_1")
 CORE = "dev_2"
 SWAP = [(0, 1), (1, 0)]
+ORDER = ((2, 1, 0), (0, 2, 1))
 CAP = 40
 HOT = 32
-WAYS = 4
+WIDE = 512
+WAYS = 8
 F32, BF16, I32 = jnp.float32, jnp.bfloat16, jnp.int32
 VMEM = pl.BlockSpec(memory_space=pltpu.VMEM)
 SMEM = pl.BlockSpec(memory_space=pltpu.SMEM)
 
 
-def route_kernel(ids, hot_list, location, send, inverse, position, found):
-    lane = lax.broadcasted_iota(I32, (1, 128), 1)
+def spread(x, ones):
+    return jnp.dot(x.astype(F32).astype(BF16), ones, preferred_element_type=F32).astype(I32)
+
+
+def route_kernel(ids, hot_list, ids_lanes, location, send, inverse, position, found):
+    blocks = position.shape[0]
+    features = blocks // 2
+
+    def pick(b, carried):
+        for j in range(128):
+            found[pl.ds(b * 128 + j, 1), :] = location[pl.ds(ids[b, j] >> 7, 1), :]
+        return carried
+
+    lax.fori_loop(0, blocks, pick, 0)
     rows = lax.broadcasted_iota(I32, (128, 128), 0)
     lanes = lax.broadcasted_iota(I32, (128, 128), 1)
     before = (lanes < rows).astype(BF16)
     diagonal = rows == lanes
-    wide = lax.broadcasted_iota(I32, (128, 256), 1)
-    wide_rank = wide & 63
-    wide_part = wide >> 6
-    wide_row = lax.broadcasted_iota(I32, (128, 256), 0)
-    blocks = position.shape[0]
-    features = blocks // 2
-
-    def block(b, carried):
-        seen, table = carried
-        for j in range(128):
-            number = ids[b, j]
-            row = location[pl.ds(number >> 7, 1), :]
-            found[pl.ds(j, 1), :] = jnp.where(lane == (number & 127), row, 0)
-        placed = jnp.sum(found[...].astype(F32), axis=1, keepdims=True).astype(I32)
-        owner = placed >> 11
-        slot = (placed & 2047) + 1
-        chosen = owner == lanes
-        one_hot = chosen.astype(BF16)
-        ahead = jnp.dot(before, one_hot, preferred_element_type=F32) + seen
-        rank = jnp.sum(jnp.where(chosen, ahead, 0.0), axis=1, keepdims=True).astype(I32)
-        seen = seen + jnp.sum(chosen.astype(F32), axis=0, keepdims=True)
-        feature = jnp.where(b >= features, b - features, b)
-        origin = feature * 128 + wide_row
-        value = jnp.where(
-            wide_part == 0,
-            slot >> 4,
-            jnp.where(
-                wide_part == 1, slot & 15, jnp.where(wide_part == 2, origin >> 4, origin & 15)
-            ),
+    ones = jnp.ones((128, 128), BF16)
+    low = [
+        spread(jnp.where(diagonal, ids_lanes[b : b + 1, :] & 127, 0), ones) for b in range(blocks)
+    ]
+    value = [
+        jnp.where(low[b] == lanes, found[b * 128 : (b + 1) * 128, :], 0) for b in range(blocks)
+    ]
+    owner = [spread(v >> 11, ones) for v in value]
+    high = [spread((v & 2047) >> 4, ones) for v in value]
+    deep = [spread(v & 15, ones) for v in value]
+    chosen = [o == lanes for o in owner]
+    one_hot = [c.astype(F32).astype(BF16) for c in chosen]
+    ahead = [jnp.dot(before, o, preferred_element_type=F32) for o in one_hot]
+    seen = jnp.zeros((1, 128), F32)
+    table = jnp.zeros((128, 256), F32)
+    lane_rank = lanes & 63
+    left = lanes < 64
+    for b in range(blocks):
+        rank = spread(jnp.where(chosen[b], ahead[b] + seen, 0.0), ones)
+        seen = seen + ahead[b][127:, :] + chosen[b][127:, :].astype(F32)
+        hit = lane_rank == rank
+        origin = (b % features) * 128 + rows
+        slots = jnp.where(hit, jnp.where(left, high[b], deep[b]), 0)
+        origins = jnp.where(hit, jnp.where(left, origin >> 4, origin & 15), 0)
+        marks = jnp.concatenate(
+            [slots.astype(F32).astype(BF16), origins.astype(F32).astype(BF16)], axis=1
         )
-        value = jnp.where(wide_rank == rank, value, 0).astype(F32).astype(BF16)
-        table = table + lax.dot_general(
-            one_hot, value, (((0,), (0,)), ((), ())), preferred_element_type=F32
-        )
-        spot = jnp.where(diagonal, owner * CAP + rank, 0)
-        position[pl.ds(b, 1), :] = jnp.sum(spot, axis=0, keepdims=True)
-        return seen, table
-
-    seen, table = lax.fori_loop(
-        0, blocks, block, (jnp.zeros((1, 128), F32), jnp.zeros((128, 256), F32))
-    )
+        table = table + contract_rows(one_hot[b], marks)
+        spot = jnp.where(diagonal, owner[b] * CAP + rank, 0)
+        position[b : b + 1, :] = jnp.sum(spot, axis=0, keepdims=True)
     table = table.astype(I32)
-    wanted = (table[:, :64] << 4) + table[:, 64:128] - 1
-    wanted = jnp.where(wanted < 0, 2048, wanted)
+    held = spread(jnp.where(diagonal, jnp.broadcast_to(seen, (128, 128)), 0.0), ones)
+    wanted = (table[:, :64] << 4) + table[:, 64:128]
+    wanted = jnp.where(lanes[:, :64] < held[:, :64], wanted, 2048)
     send[:, :CAP] = wanted[:, :CAP]
-    send[:, CAP : CAP + 32] = jnp.broadcast_to(hot_list[...], (128, 32))
-    send[:, CAP + 32 :] = jnp.zeros((128, 128 - CAP - 32), I32)
+    send[:, CAP : CAP + HOT] = jnp.broadcast_to(hot_list[...], (128, HOT))
+    send[:, CAP + HOT :] = jnp.zeros((128, 128 - CAP - HOT), I32)
     inverse[...] = (table[:, 128:192] << 4) + table[:, 192:256]
 
 
@@ -83,17 +88,18 @@
             jax.ShapeDtypeStruct((128, 64), I32),
             jax.ShapeDtypeStruct((blocks, 128), I32),
         ),
-        in_specs=[SMEM, VMEM, VMEM],
+        in_specs=[SMEM, VMEM, VMEM, VMEM],
         out_specs=(VMEM, VMEM, VMEM),
-        scratch_shapes=[pltpu.VMEM((128, 128), I32)],
+        scratch_shapes=[pltpu.VMEM((blocks * 128, 128), I32)],
         name="route",
-    )(ids, hot_list, location)
+    )(ids, hot_list, ids, location)
 
 
 def fetch_kernel(wanted, table, out, wide, picked):
-    shard = table.shape[0]
-    wide[:shard, :] = table[...].astype(F32)
-    wide[shard:, :] = jnp.zeros((8, 128), F32)
+    count, width = table.shape
+    for f in range(width // 128):
+        wide[f * count : (f + 1) * count, :] = table[:, f * 128 : (f + 1) * 128].astype(F32)
+    wide[count * width // 128 :, :] = jnp.zeros((8, 128), F32)
 
     def source(d, carried):
         for i in range(CAP):
@@ -112,7 +118,7 @@
         in_specs=[SMEM, VMEM],
         out_specs=VMEM,
         scratch_shapes=[
-            pltpu.VMEM((table.shape[0] + 8, 128), F32),
+            pltpu.VMEM((table.size // 128 + 8, 128), F32),
             pltpu.VMEM((count, 128), F32),
         ],
         name="fetch",
@@ -177,6 +183,72 @@
     )(listed, came)
 
 
+def unpack_kernel(core, held, came, u_out, v_out, bias_out, mlp_bias_out, out_weight_out, wide):
+    first = core[0] == 0
+    rank = v_out.shape[0]
+
+    def block(c, chip, lanes):
+        here = slice(chip * 16, (chip + 1) * 16)
+        own, other = held[here, lanes].astype(F32), came[here, lanes].astype(F32)
+        return jnp.where(first, own, other) if c == 0 else jnp.where(first, other, own)
+
+    def chip_of(c, spot):
+        place = [0, 0, 0]
+        for axis, at in zip(ORDER[c], spot):
+            place[axis] = at
+        return (place[0] * 4 + place[1]) * 4 + place[2]
+
+    blocks = rank // 16
+    for q in range(4):
+        count = WIDE if q < 3 else v_out.shape[1] - 3 * WIDE
+        for r in range(blocks):
+            spot = (q, r // 4, r % 4)
+            rows = slice(r * 16, (r + 1) * 16)
+            wide[rows, :count] = block(0, chip_of(0, spot), slice(0, count))
+            v_out[rows, q * WIDE : q * WIDE + count] = block(1, chip_of(1, spot), slice(0, count))
+        u_out[q * WIDE : q * WIDE + count, :] = wide[:, :count].T
+
+    lanes = slice(128, 256)
+    sums = jnp.concatenate(
+        [
+            block(0, chip_of(0, (3, r // 4, r % 4)), lanes)
+            + block(1, chip_of(1, (3, r // 4, r % 4)), lanes)
+            for r in range(3)
+        ]
+    )
+    bias_out[...] = sums[: bias_out.shape[0]]
+    start = bias_out.shape[0]
+    for out in (mlp_bias_out, out_weight_out):
+        tall = out.shape[0]
+        part = sums[start : start + tall]
+        start += tall
+        for c in range(2):
+            for at in range(64):
+                spot = (at // 16, at // 4 % 4, at % 4)
+                chip = chip_of(c, spot)
+                come, go = c * 64 + at, chip * 2 + c
+                out[go // 8 : go // 8 + 1, go % 8 * 16 : go % 8 * 16 + 16] = part[
+                    come // 8 : come // 8 + 1, come % 8 * 16 : come % 8 * 16 + 16
+                ]
+
+
+def unpack(core, held, came, inputs, rank, hidden_units):
+    return pl.pallas_call(
+        unpack_kernel,
+        out_shape=(
+            jax.ShapeDtypeStruct((inputs, rank), F32),
+            jax.ShapeDtypeStruct((rank, inputs), F32),
+            jax.ShapeDtypeStruct((inputs // 128, 128), F32),
+            jax.ShapeDtypeStruct((hidden_units // 128, 128), F32),
+            jax.ShapeDtypeStruct((hidden_units // 128, 128), F32),
+        ),
+        in_specs=[SMEM, VMEM, VMEM],
+        out_specs=(VMEM,) * 5,
+        scratch_shapes=[pltpu.VMEM((rank, WIDE), F32)],
+        name="unpack",
+    )(core.reshape(1), held, came)
+
+
 def silu_slope(values):
     squash = jax.nn.sigmoid(values)
     return squash * (1.0 + values * (1.0 - squash))
@@ -194,12 +266,43 @@
     return lax.all_to_all(x, axes, split_axis=0, concat_axis=0, tiled=True)
 
 
+def route_pairs(phase, shift):
+    pairs = []
+    for d in range(128):
+        spot = [d // 32, d // 8 % 4, d // 2 % 4]
+        axis = ORDER[d % 2][phase]
+        spot[axis] = (spot[axis] + shift) % 4
+        pairs.append((d, ((spot[0] * 4 + spot[1]) * 4 + spot[2]) * 2 + d % 2))
+    return pairs
+
+
+def scatter_phase(x, phase, core):
+    here = jnp.where(
+        core == 0, lax.axis_index(CHIPS[ORDER[0][phase]]), lax.axis_index(CHIPS[ORDER[1][phase]])
+    )
+    tiles = x.reshape(4, -1, x.shape[-1])
+    came = [
+        lax.ppermute(
+            lax.dynamic_index_in_dim(tiles, (here + s) % 4, 0, False),
+            GRP_DEV,
+            route_pairs(phase, s),
+        )
+        for s in (1, 3, 2)
+    ]
+    total = lax.dynamic_index_in_dim(tiles, here, 0, False).astype(F32)
+    for tile in came:
+        total = total + tile.astype(F32)
+    return total
+
+
 def by_core(x):
-    return x.reshape(-1, 2, 16, *x.shape[1:]).swapaxes(0, 1).reshape(x.shape)
-
-
-def from_core(x):
-    return x.reshape(2, -1, 16).swapaxes(0, 1).reshape(-1)
+    parts = x.reshape(4, 4, 4, 2, 16, *x.shape[1:])
+    halves = []
+    for c in range(2):
+        rest = tuple(range(3, 3 + x.ndim))
+        half = parts[:, :, :, c].transpose(*ORDER[c], *rest)
+        halves.append(half.reshape(-1, *x.shape[1:]))
+    return jnp.concatenate(halves)
 
 
 def per_device(
@@ -270,8 +373,6 @@
         jnp.concatenate([mine, other[:, :half]], axis=0),
         jnp.concatenate([cross_out, other[:, half:]], axis=0),
     ).astype(BF16)
-    mlp_parts = exchange(mlp_part.reshape(chips, half // chips, inputs), CHIPS)
-    mlp_weight_grad = jnp.sum(mlp_parts.astype(F32), axis=0)
 
     cross_out_grad = jnp.dot(hidden_grad, mlp_weight, preferred_element_type=F32)
     term_grad = (cross_out_grad * input_wide).astype(BF16)
@@ -281,18 +382,7 @@
         cross_out_grad * (cross_term + 1.0) + contract_cols(low_grad, cross_u)
     ).astype(BF16)
 
-    grad_rows = pooled_grad.reshape(samples, features, width).swapaxes(0, 1).reshape(pairs, width)
-    hot_block = contract_rows(hot_pick, grad_rows).astype(BF16)
-    payload = jnp.concatenate(
-        [
-            grad_rows[inverse[:, :CAP].reshape(-1)].reshape(devices, CAP, width),
-            jnp.broadcast_to(hot_block[None], (devices, HOT, width)),
-        ],
-        axis=1,
-    )
-    back = exchange(payload, GRP_DEV)
-    cold_grad = cold_sum(got, back[:, :CAP], cold_table.shape[0])
-    hot_grad = hot_sum(got, back[:, CAP:], hot_table.shape[0])
+    mlp_sum = scatter_phase(mlp_part, 0, core).astype(BF16)
 
     first = core == 0
     pair_u = jnp.concatenate([low_grad, first_input], axis=1)
@@ -303,28 +393,48 @@
     cross_part = contract_rows(both[:, :rank], both[:, rank:])
     vectors = jnp.concatenate([cross_bias_part, bias_grad, out_grad])
     vector_rows = vectors.size // 128
-    vectors = jnp.pad(vectors.reshape(vector_rows, 128), ((0, rank - vector_rows), (0, 0)))
-    cross_part = jnp.concatenate([cross_part, vectors], axis=1).astype(BF16)
-    cross_parts = exchange(cross_part.reshape(chips, rank // chips, inputs + 128), CHIPS)
-    cross_sum = jnp.sum(cross_parts.astype(F32), axis=0).astype(BF16)
-    cross_full = exchange(jnp.broadcast_to(cross_sum[None], cross_parts.shape), CHIPS)
-    cross_full = cross_full.reshape(rank, inputs + 128)
-    cross_other = lax.ppermute(cross_full, CORE, SWAP)
-    cross_u_grad = jnp.where(first, cross_full, cross_other)[:, :inputs].astype(F32).T
-    cross_v_grad = jnp.where(first, cross_other, cross_full)[:, :inputs].astype(F32)
-    vectors = (
-        cross_full[:vector_rows, inputs:].astype(F32)
-        + cross_other[:vector_rows, inputs:].astype(F32)
-    ).reshape(-1)
+    vectors = jnp.pad(
+        vectors.reshape(vector_rows, 128), ((0, rank - vector_rows), (0, 4 * WIDE - inputs - 128))
+    )
+    cross_part = jnp.concatenate(
+        [cross_part[:, q * WIDE : (q + 1) * WIDE] for q in range(3)]
+        + [jnp.concatenate([cross_part[:, 3 * WIDE :], vectors], axis=1)],
+        axis=0,
+    ).astype(BF16)
+    cross_sum = scatter_phase(cross_part, 0, core).astype(BF16)
+
+    grad_rows = pooled_grad.reshape(samples, features, width).swapaxes(0, 1).reshape(pairs, width)
+    hot_block = contract_rows(hot_pick, grad_rows).astype(BF16)
+    payload = jnp.concatenate(
+        [
+            fetch(inverse, pooled_grad).reshape(devices, CAP, width),
+            jnp.broadcast_to(hot_block[None], (devices, HOT, width)),
+        ],
+        axis=1,
+    )
+    back = exchange(payload, GRP_DEV)
+
+    sums = scatter_phase(jnp.concatenate([mlp_sum, cross_sum], axis=1), 1, core)
+    sums = scatter_phase(sums, 2, core)
+    mlp_weight_grad = sums[:, :inputs]
+    shared = jnp.broadcast_to(sums[None, :, inputs:].astype(BF16), (chips, 16, WIDE))
+    shared, back = lax.optimization_barrier((shared, back))
+    shared = exchange(shared, CHIPS).reshape(-1, WIDE)
+    cold_grad = cold_sum(got, back[:, :CAP], cold_table.shape[0])
+    hot_grad = hot_sum(got, back[:, CAP:], hot_table.shape[0])
+    other_shared = lax.ppermute(shared, CORE, SWAP)
+    cross_u_grad, cross_v_grad, cross_bias_grad, mlp_bias_grad, out_weight_grad = unpack(
+        core, shared, other_shared, inputs, rank, hidden_units
+    )
     return (
         cold_grad,
         hot_grad,
         mlp_weight_grad,
         cross_u_grad,
         cross_v_grad,
-        vectors[:inputs],
-        from_core(vectors[inputs : inputs + hidden_units]),
-        from_core(vectors[inputs + hidden_units :]),
+        cross_bias_grad.reshape(-1),
+        mlp_bias_grad.reshape(-1),
+        out_weight_grad.reshape(-1),
     )
 
 

time: 250 us -> 219 us (0.88)
  waiting for transfers between devices: 72.5 us -> 55 us
  local copies, waits for them, and re-layouts: 43.7 us -> 32.2 us
  matrix products: 18.2 us -> 10.3 us
  starting transfers between devices: 30.8 us -> 36.6 us
  blocking collectives: 21 us -> 24.1 us
  other arithmetic: 12.6 us -> 9.79 us
    all_to_all x5 -> x3, waiting for transfers between devices: 68.8 us -> 20.8 us  [exchange(): return lax.all_to_all(x, axes, split_axis=0, concat_axis=0, tiled=True)]
    ppermute x1 -> x13, waiting for transfers between devices: 0.01 us -> 33.3 us  [the longest x12 33.3 us: scatter_phase(): lax.ppermute(lax.dynamic_index_in_dim(tiles, (here + s) % 4, 0, False), G...]
    ppermute x1 -> x13, starting transfers between devices: 0.01 us -> 15.2 us  [the longest x12 15.2 us: scatter_phase(): lax.ppermute(lax.dynamic_index_in_dim(tiles, (here + s) % 4, 0, False), G...]
    gather x1 -> x0, local copies, waits for them, and re-layouts: 15.1 us -> none  [per_device(): grad_rows[inverse[:, :CAP].reshape(-1)].reshape(devices, CAP, width)]
    all_to_all x5 -> x3, starting transfers between devices: 30.7 us -> 20.8 us  [exchange(): return lax.all_to_all(x, axes, split_axis=0, concat_axis=0, tiled=True)]
    pallas_call x1, Pallas kernels: 18.5 us -> 9.33 us  [route(): pl.pallas_call(route_kernel, out_shape=(jax.ShapeDtypeStruct((128, 128),...]
    pallas_call x1 -> x2, Pallas kernels: 7.83 us -> 15.4 us  [fetch(): pl.pallas_call(fetch_kernel, out_shape=jax.ShapeDtypeStruct((count, 128),...]
    squeeze x0 -> x4, local copies, waits for them, and re-layouts: none -> 4 us  [scatter_phase(): lax.dynamic_index_in_dim(tiles, (here + s) % 4, 0, False)]
  transfers between devices with their start and end apart: 8 -> 18, of which waited for: 6 -> 9; matrix products, arithmetic and copies ran while one was open for 18% -> 14% of each run, Pallas kernels for 9% -> 12%
where the time goes in v2:
time: 219 us; the launch traced here: 217 us
  waiting for transfers between devices  55 us (25%)
  Pallas kernels  47.8 us (22%)
  starting transfers between devices  36.6 us (17%)
  local copies, waits for them, and re-layouts  32.2 us (15%)
  blocking collectives  24.1 us (11%)
  matrix products  10.3 us (5%)
  other arithmetic  9.79 us (4%)
    ppermute x12, waiting for transfers between devices, scatter_phase(): lax.ppermute(lax.dynamic_index_in_dim(tiles, (here + s) % 4, 0, False), G...  33.3 us
    all_to_all x1, blocking collectives, exchange(): return lax.all_to_all(x, axes, split_axis=0, concat_axis=0, tiled=True)  24.1 us
    all_to_all x3, starting transfers between devices, exchange(): return lax.all_to_all(x, axes, split_axis=0, concat_axis=0, tiled=True)  20.8 us
    all_to_all x3, waiting for transfers between devices, exchange(): return lax.all_to_all(x, axes, split_axis=0, concat_axis=0, tiled=True)  20.8 us
    pallas_call x2, Pallas kernels, fetch(): pl.pallas_call(fetch_kernel, out_shape=jax.ShapeDtypeStruct((count, 128),...  15.4 us
    ppermute x12, starting transfers between devices, scatter_phase(): lax.ppermute(lax.dynamic_index_in_dim(tiles, (here + s) % 4, 0, False), G...  15.2 us
    pallas_call x1, Pallas kernels, hot_sum(): pl.pallas_call(hot_kernel, out_shape=jax.ShapeDtypeStruct((hot_rows, 128)...  10.9 us
    pallas_call x1, Pallas kernels, route(): pl.pallas_call(route_kernel, out_shape=(jax.ShapeDtypeStruct((128, 128),...  9.33 us
  transfers between devices with their start and end apart: 18, of which 9 were waited for; matrix products, arithmetic and copies ran while one was open for 14% of the time, Pallas kernels for 12%

profile of v2, /device:TPU:0, one launch (start us, length us, event | category | flops | bytes accessed | tf_op | source)
XLA Modules:
  0.0 217.1 jit_solution(2921103179376648098)
XLA Ops:
  2.1 9.3 %route.1 = (s32[128,128]{1,0:T(8,128)}, s32[128,64]{1,0:T(8,128)}, s32[26,128]{1,0:T(8,128)}) custom-call(s32[26,128]{1,0:T(8,128)} %reshape.199.ids.ids_lanes, s32[1,32]{1,0:T(1,128)} %hot_list.1, s32[26,128]{1,0:T(8,128)} %reshape.199.ids.ids_lanes, s32[2048,128]{1,0:T(8,128)} %bitcast.158), custom_call_target="tpu_custom_call" | custom-call | tf_op jit(solution)/shard_map/route/pallas_call | solution.py:84
  11.4 11.2 %all-to-all-start = ((s32[128,1,128]{2,1,0:T(1,128)}), s32[128,1,128]{2,1,0:T(1,128)S(1)}, u32[]{:S(2)}, u32[]{:S(2)}) async-start(s32[128,1,128]{2,1,0:T(1,128)} %bitcast.168), calls=%async_computation | async-start | bytes 131072 | tf_op jit(solution)/shard_map/all_to_all | solution.py:266
  23.8 8.1 %all-to-all-done = s32[128,1,128]{2,1,0:T(1,128)S(1)} async-done(((s32[128,1,128]{2,1,0:T(1,128)}), s32[128,1,128]{2,1,0:T(1,128)S(1)}, u32[]{:S(2)}, u32[]{:S(2)}) %all-to-all-start) | async-done | bytes 65568 | tf_op jit(solution)/shard_map/all_to_all | solution.py:266
  32.5 7.7 %fetch.2 = bf16[5120,128]{1,0:T(8,128)(2,1)} custom-call(s32[128,128]{1,0:T(8,128)} %bitcast.159, bf16[2048,128]{1,0:T(8,128)(2,1)} %table.1), custom_call_target="tpu_custom_call" | custom-call | tf_op jit(solution)/shard_map/fetch/pallas_call | solution.py:115
  40.2 5.0 %all-to-all-start.1 = ((bf16[128,40,128]{2,1,0:T(8,128)(2,1)}), bf16[128,40,128]{2,1,0:T(8,128)(2,1)S(1)}, u32[]{:S(2)}, u32[]{:S(2)}) async-start(bf16[128,40,128]{2,1,0:T(8,128)(2,1)} %bitcast.142), calls=%async_computation.1 | async-start | bytes 2621440 | tf_op jit(solution)/shard_map/all_to_all | solution.py:266
  45.2 3.6 %slice_bitcast_fusion.1 = (bf16[4,4,4,16,1664]{4,3,0,1,2:T(8,128)(2,1)S(1)}, bf16[4,4,4,16,1664]{4,3,1,2,0:T(8,128)(2,1)S(1)}) fusion(bf16[4,4,4,2,16,1664]{5,4,3,2,1,0:T(8,128)(2,1)} %bitcast.140), kind=kLoop, calls=%fused_computation.7 | loop fusion | bytes 13631488 | tf_op jit(solution)/shard_map/transpose | solution.py:303
  48.7 2.2 %copy.49 = bf16[4,4,4,16,1664]{4,3,2,1,0:T(8,128)(2,1)} copy(bf16[4,4,4,16,1664]{4,3,0,1,2:T(8,128)(2,1)S(1)} %get-tuple-element.32) | data formatting | bytes 6815744 | tf_op jit(solution)/shard_map/transpose | solution.py:303
  50.9 2.1 copy.50
  54.2 12.7 %all-to-all-done.1 = bf16[128,40,128]{2,1,0:T(8,128)(2,1)S(1)} async-done(((bf16[128,40,128]{2,1,0:T(8,128)(2,1)}), bf16[128,40,128]{2,1,0:T(8,128)(2,1)S(1)}, u32[]{:S(2)}, u32[]{:S(2)}) %all-to-all-start.1) | async-done | bytes 1310752 | tf_op jit(solution)/shard_map/all_to_all | solution.py:266
  66.9 6.5 %gather_fusion = bf16[3328,128]{1,0:T(8,128)(2,1)S(1)} fusion(bf16[5120,128]{1,0:T(8,128)(2,1)S(1)} %bitcast.139, s32[4096]{0:T(1024)S(1)} %pad_clamp_fusion), kind=kCustom, calls=%fused_computation | custom fusion | bytes 1717248 | tf_op jit(solution)/shard_map/gather | solution.py:346
  75.3 1.4 copy-done.5
  76.6 4.5 %multiply_convert_fusion.1 = (bf16[128,2048]{1,0:T(8,128)(2,1)S(1)}, f32[128,2048]{1,0:T(8,128)S(1)}) fusion(f32[2048]{0:T(1024)S(1)} %pad_maximum_fusion.12, bf16[128,1664]{1,0:T(8,128)(2,1)S(1)} %get-tuple-element.57, bf16[1024,1664]{1,0:T(8,128)(2,1)} %bitcast.153, bf16[1024,1664]{1,0:T(8,128)(2,1)S(1)} %bitcast.151), kind=kOutput, calls=%fused_computation.40 | convolution fusion | flops 887619584 | bytes 8822784 | tf_op jit(solution)/shard_map/dot_general | solution.py:262
  89.0 1.6 dynamic-slice_bitcast_fusion.2
  91.7 3.1 %collective-permute-start.2 = (bf16[256,1664]{1,0:T(8,128)(2,1)}, bf16[256,1664]{1,0:T(8,128)(2,1)}, u32[]{:S(2)}, u32[]{:S(2)}) collective-permute-start(bf16[256,1664]{1,0:T(8,128)(2,1)} %get-tuple-element.36), channel_id=1, source_target_pairs={{0,6},{1,97},{2,0},{3,99},{4,2},{5,101},{6,4},{7,103},{8,14},{9,10... | collective-permute-start | bytes 2555912 | tf_op jit(solution)/shard_map/ppermute | solution.py:285
  97.4 2.8 %collective-permute-start.7 = (bf16[256,512]{1,0:T(8,128)(2,1)}, bf16[256,512]{1,0:T(8,128)(2,1)}, u32[]{:S(2)}, u32[]{:S(2)}) collective-permute-start(bf16[256,512]{1,0:T(8,128)(2,1)} %get-tuple-element.41), channel_id=1, source_target_pairs={{0,4},{1,65},{2,6},{3,67},{4,0},{5,69},{6,2},{7,71},{8,12},{9,73},... | collective-permute-start | bytes 786440 | tf_op jit(solution)/shard_map/ppermute | solution.py:285
  100.8 7.7 %fetch.3 = bf16[5120,128]{1,0:T(8,128)(2,1)} custom-call(s32[128,64]{1,0:T(8,128)} %get-tuple-element.20.wanted, bf16[128,1664]{1,0:T(8,128)(2,1)} %copy-done.3), custom_call_target="tpu_custom_call" | custom-call | tf_op jit(solution)/shard_map/fetch/pallas_call | solution.py:115
  108.6 2.9 %pad_maximum_fusion.5 = bf16[128,72,128]{2,1,0:T(8,128)(2,1)} fusion(bf16[128,32,128]{2,1,0:T(8,128)(2,1)S(1)} %broadcast_in_dim.5, bf16[128,40,128]{2,1,0:T(8,128)(2,1)} %bitcast.141), kind=kLoop, calls=%fused_computation.15 | loop fusion | flops 4718592 | bytes 4718592 | tf_op jit(solution)/shard_map/concatenate | solution.py:408
  111.5 4.7 %all-to-all-start.2 = ((bf16[128,72,128]{2,1,0:T(8,128)(2,1)}), bf16[128,72,128]{2,1,0:T(8,128)(2,1)S(1)}, u32[]{:S(2)}, u32[]{:S(2)}) async-start(bf16[128,72,128]{2,1,0:T(8,128)(2,1)} %pad_maximum_fusion.5), calls=%async_computation.2 | async-start | bytes 4718592 | tf_op jit(solution)/shard_map/all_to_all | solution.py:266
  116.2 8.5 %collective-permute-done.6 = bf16[256,512]{1,0:T(8,128)(2,1)} collective-permute-done((bf16[256,512]{1,0:T(8,128)(2,1)}, bf16[256,512]{1,0:T(8,128)(2,1)}, u32[]{:S(2)}, u32[]{:S(2)}) %collective-permute-start.6) | collective-permute-done | bytes 262176 | tf_op jit(solution)/shard_map/ppermute | solution.py:285
  124.7 1.2 fusion.31
  126.0 2.4 %fusion.10 = bf16[256,1664]{1,0:T(8,128)(2,1)S(1)} fusion(bf16[256,1664]{1,0:T(8,128)(2,1)} %collective-permute-done.3, bf16[256,1664]{1,0:T(8,128)(2,1)} %collective-permute-done.2, bf16[256,1664]{1,0:T(8,128)(2,1)} %collective-permute-done.1, bf16[4,256,1664]{2,1,0:T(8,128)(2,1)} %bitcast.150, s32[]{:T(128)S(6)} %select_n.142), kind=kLoop, calls=%fused_computation.24 | loop fusion | flops 3407872 | bytes 4259844 | tf_op jit(solution)/shard_map/convert_element_type | solution.py:385
  130.2 3.2 %collective-permute-start.9 = (bf16[64,2176]{1,0:T(8,128)(2,1)S(1)}, bf16[64,2176]{1,0:T(8,128)(2,1)}, u32[]{:S(2)}, u32[]{:S(2)}) collective-permute-start(bf16[64,2176]{1,0:T(8,128)(2,1)S(1)} %get-tuple-element.39), channel_id=1, source_target_pairs={{0,24},{1,7},{2,26},{3,1},{4,28},{5,3},{6,30},{7,5},{8,0},{9,15},{... | collective-permute-start | bytes 835592 | tf_op jit(solution)/shard_map/ppermute | solution.py:285
  133.4 17.0 %collective-permute-done.10 = bf16[64,2176]{1,0:T(8,128)(2,1)S(1)} collective-permute-done((bf16[64,2176]{1,0:T(8,128)(2,1)}, bf16[64,2176]{1,0:T(8,128)(2,1)S(1)}, u32[]{:S(2)}, u32[]{:S(2)}) %collective-permute-start.10) | collective-permute-done | bytes 278560 | tf_op jit(solution)/shard_map/ppermute | solution.py:285
  150.4 2.2 %collective-permute-done.8 = bf16[64,2176]{1,0:T(8,128)(2,1)} collective-permute-done((bf16[64,2176]{1,0:T(8,128)(2,1)S(1)}, bf16[64,2176]{1,0:T(8,128)(2,1)}, u32[]{:S(2)}, u32[]{:S(2)}) %collective-permute-start.8) | collective-permute-done | bytes 278560 | tf_op jit(solution)/shard_map/ppermute | solution.py:285
  152.7 1.3 fusion.25
  154.8 3.1 %collective-permute-start.12 = (f32[16,2176]{1,0:T(8,128)S(1)}, f32[16,2176]{1,0:T(8,128)S(1)}, u32[]{:S(2)}, u32[]{:S(2)}) collective-permute-start(f32[16,2176]{1,0:T(8,128)S(1)} %get-tuple-element.50), channel_id=1, source_target_pairs={{0,96},{1,25},{2,98},{3,27},{4,100},{5,29},{6,102},{7,31},{8,104},... | collective-permute-start | bytes 417800 | tf_op jit(solution)/shard_map/ppermute | solution.py:285
  158.3 2.8 %collective-permute-done.11 = f32[16,2176]{1,0:T(8,128)S(1)} collective-permute-done((f32[16,2176]{1,0:T(8,128)}, f32[16,2176]{1,0:T(8,128)S(1)}, u32[]{:S(2)}, u32[]{:S(2)}) %collective-permute-start.11) | collective-permute-done | bytes 139296 | tf_op jit(solution)/shard_map/ppermute | solution.py:285
  162.6 1.9 collective-permute-done.13
  167.0 24.1 %all_to_all.20 = bf16[64,16,512]{2,1,0:T(8,128)(2,1)} all-to-all(bf16[64,16,512]{2,1,0:T(8,128)(2,1)S(1)} %broadcast_in_dim.4), channel_id=1, replica_groups=mesh['grp'=4,'dev_0'=4,'dev_1'=4,'dev_2'=2] {'grp','dev_0','dev_1'}, dimensions={0} | all-to-all | bytes 2097152 | tf_op jit(solution)/shard_map/all_to_all | solution.py:266
  194.0 10.9 %hot_sum.1 = f32[4096,128]{1,0:T(8,128)} custom-call(s32[128,128]{1,0:T(8,128)} %bitcast.160, bf16[128,32,128]{2,1,0:T(8,128)(2,1)} %slice.85.came), custom_call_target="tpu_custom_call" | custom-call | tf_op jit(solution)/shard_map/hot_sum/pallas_call | solution.py:176
  204.9 8.5 %cold_sum.1 = f32[2048,128]{1,0:T(8,128)} custom-call(s32[128,128]{1,0:T(8,128)} %bitcast.161, bf16[128,40,128]{2,1,0:T(8,128)(2,1)} %slice.84.came), custom_call_target="tpu_custom_call" | custom-call | tf_op jit(solution)/shard_map/cold_sum/pallas_call | solution.py:150
  213.4 3.7 %unpack.1 = (f32[1664,256]{1,0:T(8,128)}, f32[256,1664]{1,0:T(8,128)}, f32[13,128]{1,0:T(8,128)}, f32[16,128]{1,0:T(8,128)}, f32[16,128]{1,0:T(8,128)}) custom-call(s32[1]{0:T(128)} %bitcast.56.core, bf16[1024,512]{1,0:T(8,128)(2,1)} %bitcast.57.held, bf16[1024,512]{1,0:T(8,128)(2,1)} %collective-permute-done.14.came), custom_call_target="tpu_custom_call" | custom-call | tf_op jit(solution)/shard_map/unpack/pallas_call | solution.py:236
  (118 shorter events, 28.1 us)
Async XLA Ops:
  0.6 52.8 %copy-start = (bf16[4096,128]{1,0:T(8,128)(2,1)S(1)}, bf16[4096,128]{1,0:T(8,128)(2,1)}, u32[]{:S(2)}) copy-start(bf16[4096,128]{1,0:T(8,128)(2,1)} %param.18) | copy-start | bytes 3145732
  11.4 20.4 %all-to-all-start = ((s32[128,1,128]{2,1,0:T(1,128)}), s32[128,1,128]{2,1,0:T(1,128)S(1)}, u32[]{:S(2)}, u32[]{:S(2)}) async-start(s32[128,1,128]{2,1,0:T(1,128)} %bitcast.168), calls=%async_computation | async-start | bytes 131072 | tf_op jit(solution)/shard_map/all_to_all | solution.py:266
  40.2 26.8 %all-to-all-start.1 = ((bf16[128,40,128]{2,1,0:T(8,128)(2,1)}), bf16[128,40,128]{2,1,0:T(8,128)(2,1)S(1)}, u32[]{:S(2)}, u32[]{:S(2)}) async-start(bf16[128,40,128]{2,1,0:T(8,128)(2,1)} %bitcast.142), calls=%async_computation.1 | async-start | bytes 2621440 | tf_op jit(solution)/shard_map/all_to_all | solution.py:266
  50.9 2.1 copy-start.14
  50.9 2.5 %copy-start.15 = (s32[1,32]{1,0:T(1,128)S(1)}, s32[1,32]{1,0:T(1,128)}, u32[]{:S(2)}) copy-start(s32[1,32]{1,0:T(1,128)} %hot_list.1) | copy-start | bytes 388
  50.9 3.2 %copy-start.12 = (s32[26,128]{1,0:T(8,128)S(1)}, s32[26,128]{1,0:T(8,128)}, u32[]{:S(2)}) copy-start(s32[26,128]{1,0:T(8,128)} %get-tuple-element.19) | copy-start | bytes 39940
  66.9 6.6 %copy-start.17 = (s32[128,13]{0,1:T(8,128)S(1)}, s32[128,13]{0,1:T(8,128)}, u32[]{:S(2)}) copy-start(s32[128,13]{0,1:T(8,128)} %param.16) | copy-start | bytes 19972
  73.5 1.5 copy-start.7
  73.5 1.5 copy-start.13
  74.6 2.0 copy-start.5
  76.6 4.5 %copy-start.16 = (s32[128]{0:T(128)S(1)}, s32[128]{0:T(128)}, u32[]{:S(2)}) copy-start(s32[128]{0:T(128)} %param.19) | copy-start | bytes 1540
  76.6 5.3 %copy-start.6 = (bf16[4,4,4,16,1664]{4,3,2,1,0:T(8,128)(2,1)S(1)}, bf16[4,4,4,16,1664]{4,3,2,1,0:T(8,128)(2,1)}, u32[]{:S(2)}) copy-start(bf16[4,4,4,16,1664]{4,3,2,1,0:T(8,128)(2,1)} %copy.50) | copy-start | bytes 10223620
  83.7 1.9 collective-permute-start.4
  83.9 3.8 %collective-permute-start = (bf16[128,2688]{1,0:T(8,128)(2,1)S(1)}, bf16[128,2688]{1,0:T(8,128)(2,1)S(1)}, u32[]{:S(2)}, u32[]{:S(2)}) collective-permute-start(bf16[128,2688]{1,0:T(8,128)(2,1)S(1)} %pad_maximum_fusion.9), channel_id=1, source_target_pairs={{0,1},{1,0},{2,3},{3,2},{4,5},{5,4},{6,7},{7,6},{8,9},{9,8},{10,11... | collective-permute-start | bytes 2064392 | tf_op jit(solution)/shard_map/ppermute | solution.py:371
  87.2 10.2 %collective-permute-start.5 = (bf16[256,512]{1,0:T(8,128)(2,1)S(1)}, bf16[256,512]{1,0:T(8,128)(2,1)S(1)}, u32[]{:S(2)}, u32[]{:S(2)}) collective-permute-start(bf16[256,512]{1,0:T(8,128)(2,1)S(1)} %get-tuple-element.40), channel_id=1, source_target_pairs={{0,2},{1,33},{2,4},{3,35},{4,6},{5,37},{6,0},{7,39},{8,10},{9,41},... | collective-permute-start | bytes 786440 | tf_op jit(solution)/shard_map/ppermute | solution.py:285
  89.0 2.5 %copy-start.4 = (bf16[1024,1664]{1,0:T(8,128)(2,1)}, bf16[1024,1664]{1,0:T(8,128)(2,1)S(1)}, u32[]{:S(2)}) copy-start(bf16[1024,1664]{1,0:T(8,128)(2,1)S(1)} %convolution_convert_fusion) | copy-start | bytes 10223620
  91.5 34.4 %collective-permute-start.1 = (bf16[256,1664]{1,0:T(8,128)(2,1)}, bf16[256,1664]{1,0:T(8,128)(2,1)}, u32[]{:S(2)}, u32[]{:S(2)}) collective-permute-start(bf16[256,1664]{1,0:T(8,128)(2,1)} %get-tuple-element.34), channel_id=1, source_target_pairs={{0,2},{1,33},{2,4},{3,35},{4,6},{5,37},{6,0},{7,39},{8,10},{9,41},... | collective-permute-start | bytes 2555912 | tf_op jit(solution)/shard_map/ppermute | solution.py:285
  91.7 34.3 %collective-permute-start.2 = (bf16[256,1664]{1,0:T(8,128)(2,1)}, bf16[256,1664]{1,0:T(8,128)(2,1)}, u32[]{:S(2)}, u32[]{:S(2)}) collective-permute-start(bf16[256,1664]{1,0:T(8,128)(2,1)} %get-tuple-element.36), channel_id=1, source_target_pairs={{0,6},{1,97},{2,0},{3,99},{4,2},{5,101},{6,4},{7,103},{8,14},{9,10... | collective-permute-start | bytes 2555912 | tf_op jit(solution)/shard_map/ppermute | solution.py:285
  94.8 31.2 %collective-permute-start.3 = (bf16[256,1664]{1,0:T(8,128)(2,1)}, bf16[256,1664]{1,0:T(8,128)(2,1)}, u32[]{:S(2)}, u32[]{:S(2)}) collective-permute-start(bf16[256,1664]{1,0:T(8,128)(2,1)} %get-tuple-element.35), channel_id=1, source_target_pairs={{0,4},{1,65},{2,6},{3,67},{4,0},{5,69},{6,2},{7,71},{8,12},{9,73},... | collective-permute-start | bytes 2555912 | tf_op jit(solution)/shard_map/ppermute | solution.py:285
  96.1 4.7 %copy-start.3 = (bf16[128,1664]{1,0:T(8,128)(2,1)}, bf16[128,1664]{1,0:T(8,128)(2,1)S(1)}, u32[]{:S(2)}) copy-start(bf16[128,1664]{1,0:T(8,128)(2,1)S(1)} %fusion.4.table) | copy-start | bytes 1277956
  96.6 28.1 %collective-permute-start.6 = (bf16[256,512]{1,0:T(8,128)(2,1)}, bf16[256,512]{1,0:T(8,128)(2,1)}, u32[]{:S(2)}, u32[]{:S(2)}) collective-permute-start(bf16[256,512]{1,0:T(8,128)(2,1)} %get-tuple-element.42), channel_id=1, source_target_pairs={{0,6},{1,97},{2,0},{3,99},{4,2},{5,101},{6,4},{7,103},{8,14},{9,10... | collective-permute-start | bytes 786440 | tf_op jit(solution)/shard_map/ppermute | solution.py:285
  97.4 14.1 %copy-start.10 = (bf16[256,512]{1,0:T(8,128)(2,1)}, bf16[256,512]{1,0:T(8,128)(2,1)S(1)}, u32[]{:S(2)}) copy-start(bf16[256,512]{1,0:T(8,128)(2,1)S(1)} %collective-permute-done.5) | copy-start | bytes 786436
  97.4 27.3 %collective-permute-start.7 = (bf16[256,512]{1,0:T(8,128)(2,1)}, bf16[256,512]{1,0:T(8,128)(2,1)}, u32[]{:S(2)}, u32[]{:S(2)}) collective-permute-start(bf16[256,512]{1,0:T(8,128)(2,1)} %get-tuple-element.41), channel_id=1, source_target_pairs={{0,4},{1,65},{2,6},{3,67},{4,0},{5,69},{6,2},{7,71},{8,12},{9,73},... | collective-permute-start | bytes 786440 | tf_op jit(solution)/shard_map/ppermute | solution.py:285
  111.5 54.6 %all-to-all-start.2 = ((bf16[128,72,128]{2,1,0:T(8,128)(2,1)}), bf16[128,72,128]{2,1,0:T(8,128)(2,1)S(1)}, u32[]{:S(2)}, u32[]{:S(2)}) async-start(bf16[128,72,128]{2,1,0:T(8,128)(2,1)} %pad_maximum_fusion.5), calls=%async_computation.2 | async-start | bytes 4718592 | tf_op jit(solution)/shard_map/all_to_all | solution.py:266
  130.2 20.2 %collective-permute-start.10 = (bf16[64,2176]{1,0:T(8,128)(2,1)}, bf16[64,2176]{1,0:T(8,128)(2,1)S(1)}, u32[]{:S(2)}, u32[]{:S(2)}) collective-permute-start(bf16[64,2176]{1,0:T(8,128)(2,1)} %get-tuple-element.38), channel_id=1, source_target_pairs={{0,16},{1,5},{2,18},{3,7},{4,20},{5,1},{6,22},{7,3},{8,24},{9,13},... | collective-permute-start | bytes 835592 | tf_op jit(solution)/shard_map/ppermute | solution.py:285
  130.2 22.5 %collective-permute-start.8 = (bf16[64,2176]{1,0:T(8,128)(2,1)S(1)}, bf16[64,2176]{1,0:T(8,128)(2,1)}, u32[]{:S(2)}, u32[]{:S(2)}) collective-permute-start(bf16[64,2176]{1,0:T(8,128)(2,1)S(1)} %get-tuple-element.37), channel_id=1, source_target_pairs={{0,8},{1,3},{2,10},{3,5},{4,12},{5,7},{6,14},{7,1},{8,16},{9,11},{... | collective-permute-start | bytes 835592 | tf_op jit(solution)/shard_map/ppermute | solution.py:285
  130.2 22.5 %collective-permute-start.9 = (bf16[64,2176]{1,0:T(8,128)(2,1)S(1)}, bf16[64,2176]{1,0:T(8,128)(2,1)}, u32[]{:S(2)}, u32[]{:S(2)}) collective-permute-start(bf16[64,2176]{1,0:T(8,128)(2,1)S(1)} %get-tuple-element.39), channel_id=1, source_target_pairs={{0,24},{1,7},{2,26},{3,1},{4,28},{5,3},{6,30},{7,5},{8,0},{9,15},{... | collective-permute-start | bytes 835592 | tf_op jit(solution)/shard_map/ppermute | solution.py:285
  154.6 6.5 %collective-permute-start.11 = (f32[16,2176]{1,0:T(8,128)}, f32[16,2176]{1,0:T(8,128)S(1)}, u32[]{:S(2)}, u32[]{:S(2)}) collective-permute-start(f32[16,2176]{1,0:T(8,128)} %get-tuple-element.48), channel_id=1, source_target_pairs={{0,32},{1,9},{2,34},{3,11},{4,36},{5,13},{6,38},{7,15},{8,40},{9,1... | collective-permute-start | bytes 417800 | tf_op jit(solution)/shard_map/ppermute | solution.py:285
  154.8 7.2 %collective-permute-start.12 = (f32[16,2176]{1,0:T(8,128)S(1)}, f32[16,2176]{1,0:T(8,128)S(1)}, u32[]{:S(2)}, u32[]{:S(2)}) collective-permute-start(f32[16,2176]{1,0:T(8,128)S(1)} %get-tuple-element.50), channel_id=1, source_target_pairs={{0,96},{1,25},{2,98},{3,27},{4,100},{5,29},{6,102},{7,31},{8,104},... | collective-permute-start | bytes 417800 | tf_op jit(solution)/shard_map/ppermute | solution.py:285
  157.9 6.7 %collective-permute-start.13 = (f32[16,2176]{1,0:T(8,128)S(1)}, f32[16,2176]{1,0:T(8,128)}, u32[]{:S(2)}, u32[]{:S(2)}) collective-permute-start(f32[16,2176]{1,0:T(8,128)S(1)} %get-tuple-element.49), channel_id=1, source_target_pairs={{0,64},{1,17},{2,66},{3,19},{4,68},{5,21},{6,70},{7,23},{8,72},{9,... | collective-permute-start | bytes 417800 | tf_op jit(solution)/shard_map/ppermute | solution.py:285
  191.1 22.3 %collective-permute-start.14 = (bf16[1024,512]{1,0:T(8,128)(2,1)}, bf16[1024,512]{1,0:T(8,128)(2,1)}, u32[]{:S(2)}, u32[]{:S(2)}) collective-permute-start(bf16[1024,512]{1,0:T(8,128)(2,1)} %bitcast.57.held), channel_id=1, source_target_pairs={{0,1},{1,0},{2,3},{3,2},{4,5},{5,4},{6,7},{7,6},{8,9},{9,8},{10,11... | collective-permute-start | bytes 3145736 | tf_op jit(solution)/shard_map/ppermute | solution.py:425
  194.0 23.1 %copy-start.1 = (bf16[4096,128]{1,0:T(8,128)(2,1)S(1)}, bf16[4096,128]{1,0:T(8,128)(2,1)}, u32[]{:S(2)}) copy-start(bf16[4096,128]{1,0:T(8,128)(2,1)} %param.18) | copy-start | bytes 3145732
  (4 other events, 3.4 us)

commit v3 on v2

--- a/solution.py
+++ b/solution.py
@@ -96,10 +96,9 @@
 
 
 def fetch_kernel(wanted, table, out, wide, picked):
-    count, width = table.shape
-    for f in range(width // 128):
-        wide[f * count : (f + 1) * count, :] = table[:, f * 128 : (f + 1) * 128].astype(F32)
-    wide[count * width // 128 :, :] = jnp.zeros((8, 128), F32)
+    shard = table.shape[0]
+    wide[:shard, :] = table[...].astype(F32)
+    wide[shard:, :] = jnp.zeros((8, 128), F32)
 
     def source(d, carried):
         for i in range(CAP):
@@ -118,17 +117,83 @@
         in_specs=[SMEM, VMEM],
         out_specs=VMEM,
         scratch_shapes=[
-            pltpu.VMEM((table.size // 128 + 8, 128), F32),
+            pltpu.VMEM((table.shape[0] + 8, 128), F32),
             pltpu.VMEM((count, 128), F32),
         ],
         name="fetch",
     )(wanted, table)
 
 
+def pool_kernel(position, hot_index, hot_rows, arrived, out, wide, total):
+    features, samples = hot_index.shape
+    wide[...] = arrived[...].astype(F32)
+    slots = lax.broadcasted_iota(I32, (HOT, samples), 0)
+
+    def feature(f, carried):
+        for s in range(samples):
+            total[s : s + 1, :] = (
+                wide[pl.ds(position[f, s], 1), :] + wide[pl.ds(position[features + f, s], 1), :]
+            )
+        picked = (slots == hot_index[pl.ds(f, 1), :]).astype(F32).astype(BF16)
+        both = total[...] + contract_rows(picked, hot_rows[...])
+        out[:, pl.ds(pl.multiple_of(f * 128, 128), 128)] = both.astype(BF16)
+        return carried
+
+    lax.fori_loop(0, features, feature, 0)
+
+
+def pool(position, hot_index, hot_rows, arrived):
+    features, samples = hot_index.shape
+    return pl.pallas_call(
+        pool_kernel,
+        out_shape=jax.ShapeDtypeStruct((samples, features * 128), BF16),
+        in_specs=[SMEM, VMEM, VMEM, VMEM],
+        out_specs=VMEM,
+        scratch_shapes=[pltpu.VMEM(arrived.shape, F32), pltpu.VMEM((samples, 128), F32)],
+        name="pool",
+    )(position, hot_index, hot_rows, arrived)
+
+
+def pack_kernel(inverse, hot_index, grad, out, wide, picked):
+    samples, inputs = grad.shape
+    devices = out.shape[0]
+    slots = lax.broadcasted_iota(I32, (HOT, samples), 0)
+    hot_block = jnp.zeros((HOT, 128), F32)
+    for f in range(inputs // 128):
+        part = grad[:, f * 128 : (f + 1) * 128]
+        wide[f * samples : (f + 1) * samples, :] = part.astype(F32)
+        one_hot = (slots == hot_index[f : f + 1, :]).astype(F32).astype(BF16)
+        hot_block = hot_block + jnp.dot(one_hot, part, preferred_element_type=F32)
+
+    def source(d, carried):
+        for i in range(CAP):
+            picked[pl.ds(d * CAP + i, 1), :] = wide[pl.ds(inverse[d, i], 1), :]
+        return carried
+
+    lax.fori_loop(0, devices, source, 0)
+    out[:, :CAP, :] = picked[...].reshape(devices, CAP, 128).astype(BF16)
+    out[:, CAP:, :] = jnp.broadcast_to(hot_block.astype(BF16)[None], (devices, HOT, 128))
+
+
+def pack(inverse, hot_index, grad):
+    devices = inverse.shape[0]
+    return pl.pallas_call(
+        pack_kernel,
+        out_shape=jax.ShapeDtypeStruct((devices, CAP + HOT, 128), BF16),
+        in_specs=[SMEM, VMEM, VMEM],
+        out_specs=VMEM,
+        scratch_shapes=[
+            pltpu.VMEM((grad.size // 128, 128), F32),
+            pltpu.VMEM((devices * CAP, 128), F32),
+        ],
+        name="pack",
+    )(inverse, hot_index, grad)
+
+
 def cold_kernel(wanted, came, out, wide, *sums):
     for way in sums:
         way[...] = jnp.zeros(way.shape, F32)
-    wide[...] = came[...].astype(F32)
+    wide[...] = came[:, :CAP, :].astype(F32)
 
     def source(d, carried):
         for i in range(CAP // WAYS):
@@ -152,7 +217,7 @@
         out_shape=jax.ShapeDtypeStruct((shard_rows, 128), F32),
         in_specs=[SMEM, VMEM],
         out_specs=VMEM,
-        scratch_shapes=[pltpu.VMEM(came.shape, F32)]
+        scratch_shapes=[pltpu.VMEM((came.shape[0], CAP, 128), F32)]
         + [pltpu.VMEM((shard_rows + 8, 128), F32)] * WAYS,
         name="cold_sum",
     )(wanted, came)
@@ -160,7 +225,7 @@
 
 def hot_kernel(listed, came, out, wide):
     out[...] = jnp.zeros(out.shape, F32)
-    wide[...] = came[...].astype(F32)
+    wide[...] = came[:, CAP:, :].astype(F32)
 
     def source(d, carried):
         places = [pl.ds(listed[d, CAP + i], 1) for i in range(HOT)]
@@ -178,7 +243,7 @@
         out_shape=jax.ShapeDtypeStruct((hot_rows, 128), F32),
         in_specs=[SMEM, VMEM],
         out_specs=VMEM,
-        scratch_shapes=[pltpu.VMEM(came.shape, F32)],
+        scratch_shapes=[pltpu.VMEM((came.shape[0], HOT, 128), F32)],
         name="hot_sum",
     )(listed, came)
 
@@ -324,7 +389,6 @@
     chips = lax.axis_size(CHIPS)
     samples, features, bag_size = ids.shape
     width = cold_table.shape[1]
-    pairs = samples * features
     hidden_units, inputs = mlp_weight.shape
     rank = cross_u.shape[1]
     core = lax.axis_index(CORE)
@@ -338,19 +402,9 @@
     mlp_weight = by_core(mlp_weight)
     mlp_bias = by_core(mlp_bias)
     out_weight = by_core(out_weight)
-    hot_pick = (
-        hot_index.T.reshape(pairs)[:, None] == jnp.arange(HOT, dtype=I32)[None, :]
-    ).astype(BF16)
-    hot_part = jnp.dot(hot_pick, hot_table[hot_list[0]], preferred_element_type=F32)
-
-    own = arrived[position.reshape(-1)].reshape(bag_size, pairs, width)
-    pooled = own[0].astype(F32) + own[1].astype(F32) + hot_part
-    first_input = (
-        pooled.reshape(features, samples, width)
-        .swapaxes(0, 1)
-        .reshape(samples, inputs)
-        .astype(BF16)
-    )
+    hot_rows = hot_table[hot_list[0]]
+    hot_index = hot_index.T
+    first_input = pool(position, hot_index, hot_rows, arrived)
     cross_low = jnp.dot(first_input, cross_u, preferred_element_type=F32).astype(BF16)
     cross_term = jnp.dot(cross_low, cross_v, preferred_element_type=F32) + cross_bias
     input_wide = first_input.astype(F32)
@@ -403,15 +457,7 @@
     ).astype(BF16)
     cross_sum = scatter_phase(cross_part, 0, core).astype(BF16)
 
-    grad_rows = pooled_grad.reshape(samples, features, width).swapaxes(0, 1).reshape(pairs, width)
-    hot_block = contract_rows(hot_pick, grad_rows).astype(BF16)
-    payload = jnp.concatenate(
-        [
-            fetch(inverse, pooled_grad).reshape(devices, CAP, width),
-            jnp.broadcast_to(hot_block[None], (devices, HOT, width)),
-        ],
-        axis=1,
-    )
+    payload = pack(inverse, hot_index, pooled_grad)
     back = exchange(payload, GRP_DEV)
 
     sums = scatter_phase(jnp.concatenate([mlp_sum, cross_sum], axis=1), 1, core)
@@ -420,8 +466,8 @@
     shared = jnp.broadcast_to(sums[None, :, inputs:].astype(BF16), (chips, 16, WIDE))
     shared, back = lax.optimization_barrier((shared, back))
     shared = exchange(shared, CHIPS).reshape(-1, WIDE)
-    cold_grad = cold_sum(got, back[:, :CAP], cold_table.shape[0])
-    hot_grad = hot_sum(got, back[:, CAP:], hot_table.shape[0])
+    cold_grad = cold_sum(got, back, cold_table.shape[0])
+    hot_grad = hot_sum(got, back, hot_table.shape[0])
     other_shared = lax.ppermute(shared, CORE, SWAP)
     cross_u_grad, cross_v_grad, cross_bias_grad, mlp_bias_grad, out_weight_grad = unpack(
         core, shared, other_shared, inputs, rank, hidden_units

time: 219 us -> 236 us (1.078)
  waiting for transfers between devices: 55 us -> 70.7 us
  local copies, waits for them, and re-layouts: 32.2 us -> 23 us
  Pallas kernels: 47.8 us -> 54.6 us
  matrix products: 10.3 us -> 15.4 us
  other arithmetic: 9.79 us -> 6.79 us
    ppermute x12, waiting for transfers between devices: 33.3 us -> 49.5 us  [scatter_phase(): lax.ppermute(lax.dynamic_index_in_dim(tiles, (here + s) % 4, 0, False), G...]
    pallas_call x0 -> x2, Pallas kernels: none -> 14.5 us  [the longest x1 8.34 us: pack(): pl.pallas_call(pack_kernel, out_shape=jax.ShapeDtypeStruct((devices, CAP...]
    pallas_call x2 -> x1, Pallas kernels: 15.4 us -> 7.7 us  [fetch(): pl.pallas_call(fetch_kernel, out_shape=jax.ShapeDtypeStruct((count, 128),...]
    gather x2 -> x1, local copies, waits for them, and re-layouts: 7.12 us -> 1.19 us  [per_device(): hot_rows = hot_table[hot_list[0]]]
    concatenate x1 -> x0, other arithmetic: 2.92 us -> none  [per_device(): jnp.concatenate([fetch(inverse, pooled_grad).reshape(devices, CAP, width)...]
  transfers between devices with their start and end apart: 18 -> 18, of which waited for: 9 -> 11; matrix products, arithmetic and copies ran while one was open for 14% -> 10% of each run, Pallas kernels for 12% -> 12%
where the time goes in v3:
time: 236 us; the launch traced here: 234 us
  waiting for transfers between devices  70.7 us (30%)
  Pallas kernels  54.6 us (23%)
  starting transfers between devices  38.4 us (16%)
  blocking collectives  24 us (10%)
  local copies, waits for them, and re-layouts  23 us (10%)
  matrix products  15.4 us (7%)
  other arithmetic  6.79 us (3%)
    ppermute x12, waiting for transfers between devices, scatter_phase(): lax.ppermute(lax.dynamic_index_in_dim(tiles, (here + s) % 4, 0, False), G...  49.5 us
    all_to_all x1, blocking collectives, exchange(): return lax.all_to_all(x, axes, split_axis=0, concat_axis=0, tiled=True)  24 us
    all_to_all x3, starting transfers between devices, exchange(): return lax.all_to_all(x, axes, split_axis=0, concat_axis=0, tiled=True)  21.3 us
    all_to_all x3, waiting for transfers between devices, exchange(): return lax.all_to_all(x, axes, split_axis=0, concat_axis=0, tiled=True)  19.8 us
    ppermute x12, starting transfers between devices, scatter_phase(): lax.ppermute(lax.dynamic_index_in_dim(tiles, (here + s) % 4, 0, False), G...  16.2 us
    pallas_call x1, Pallas kernels, hot_sum(): pl.pallas_call(hot_kernel, out_shape=jax.ShapeDtypeStruct((hot_rows, 128)...  10.9 us
    pallas_call x1, Pallas kernels, route(): pl.pallas_call(route_kernel, out_shape=(jax.ShapeDtypeStruct((128, 128),...  9.33 us
    pallas_call x1, Pallas kernels, cold_sum(): pl.pallas_call(cold_kernel, out_shape=jax.ShapeDtypeStruct((shard_rows, 1...  8.49 us
  transfers between devices with their start and end apart: 18, of which 11 were waited for; matrix products, arithmetic and copies ran while one was open for 10% of the time, Pallas kernels for 12%

profile of v3, /device:TPU:0, one launch (start us, length us, event | category | flops | bytes accessed | tf_op | source)
XLA Modules:
  0.0 233.9 jit_solution(14892951994282201045)
XLA Ops:
  2.1 9.3 %route.1 = (s32[128,128]{1,0:T(8,128)}, s32[128,64]{1,0:T(8,128)}, s32[26,128]{1,0:T(8,128)}) custom-call(s32[26,128]{1,0:T(8,128)} %reshape.148.ids.ids_lanes, s32[1,32]{1,0:T(1,128)} %hot_list.1, s32[26,128]{1,0:T(8,128)} %reshape.148.ids.ids_lanes, s32[2048,128]{1,0:T(8,128)} %bitcast.139), custom_call_target="tpu_custom_call" | custom-call | tf_op jit(solution)/shard_map/route/pallas_call | solution.py:84
  11.4 11.2 %all-to-all-start = ((s32[128,1,128]{2,1,0:T(1,128)}), s32[128,1,128]{2,1,0:T(1,128)S(1)}, u32[]{:S(2)}, u32[]{:S(2)}) async-start(s32[128,1,128]{2,1,0:T(1,128)} %bitcast.144), calls=%async_computation | async-start | bytes 131072 | tf_op jit(solution)/shard_map/all_to_all | solution.py:331
  24.5 7.3 %all-to-all-done = s32[128,1,128]{2,1,0:T(1,128)S(1)} async-done(((s32[128,1,128]{2,1,0:T(1,128)}), s32[128,1,128]{2,1,0:T(1,128)S(1)}, u32[]{:S(2)}, u32[]{:S(2)}) %all-to-all-start) | async-done | bytes 65568 | tf_op jit(solution)/shard_map/all_to_all | solution.py:331
  32.4 7.7 %fetch.1 = bf16[5120,128]{1,0:T(8,128)(2,1)} custom-call(s32[128,128]{1,0:T(8,128)} %bitcast.136, bf16[2048,128]{1,0:T(8,128)(2,1)} %table.1), custom_call_target="tpu_custom_call" | custom-call | tf_op jit(solution)/shard_map/fetch/pallas_call | solution.py:114
  40.1 4.8 %all-to-all-start.1 = ((bf16[128,40,128]{2,1,0:T(8,128)(2,1)}), bf16[128,40,128]{2,1,0:T(8,128)(2,1)S(1)}, u32[]{:S(2)}, u32[]{:S(2)}) async-start(bf16[128,40,128]{2,1,0:T(8,128)(2,1)} %bitcast.123), calls=%async_computation.1 | async-start | bytes 2621440 | tf_op jit(solution)/shard_map/all_to_all | solution.py:331
  45.3 3.5 %slice_bitcast_fusion.1 = (bf16[4,4,4,16,1664]{4,3,0,1,2:T(8,128)(2,1)S(1)}, bf16[4,4,4,16,1664]{4,3,1,2,0:T(8,128)(2,1)S(1)}) fusion(bf16[4,4,4,2,16,1664]{5,4,3,2,1,0:T(8,128)(2,1)} %bitcast.121), kind=kLoop, calls=%fused_computation.6 | loop fusion | bytes 13631488 | tf_op jit(solution)/shard_map/transpose | solution.py:368
  48.8 2.1 copy.37
  50.9 2.2 copy.36
  54.3 12.5 %all-to-all-done.1 = bf16[128,40,128]{2,1,0:T(8,128)(2,1)S(1)} async-done(((bf16[128,40,128]{2,1,0:T(8,128)(2,1)}), bf16[128,40,128]{2,1,0:T(8,128)(2,1)S(1)}, u32[]{:S(2)}, u32[]{:S(2)}) %all-to-all-start.1) | async-done | bytes 1310752 | tf_op jit(solution)/shard_map/all_to_all | solution.py:331
  67.9 6.1 %pool.1 = bf16[128,1664]{1,0:T(8,128)(2,1)} custom-call(s32[26,128]{1,0:T(8,128)} %get-tuple-element.19.position, s32[13,128]{1,0:T(8,128)} %bitcast.145, bf16[32,128]{1,0:T(8,128)(2,1)} %gather_fusion, bf16[5120,128]{1,0:T(8,128)(2,1)} %bitcast.122), custom_call_target="tpu_custom_call" | custom-call | tf_op jit(solution)/shard_map/pool/pallas_call | solution.py:147
  74.1 1.7 convolution_convert_fusion.3
  75.8 2.2 fusion.18
  78.1 4.5 %multiply_convert_fusion.1 = (bf16[128,2048]{1,0:T(8,128)(2,1)S(1)}, f32[128,2048]{1,0:T(8,128)S(1)}) fusion(f32[2048]{0:T(1024)S(1)} %pad_maximum_fusion.11, bf16[128,1664]{1,0:T(8,128)(2,1)S(1)} %get-tuple-element.57, bf16[1024,1664]{1,0:T(8,128)(2,1)S(1)} %bitcast.130, bf16[1024,1664]{1,0:T(8,128)(2,1)} %bitcast.132), kind=kOutput, calls=%fused_computation.35 | convolution fusion | flops 887619584 | bytes 8822784 | tf_op jit(solution)/shard_map/dot_general | solution.py:327
  83.7 2.1 fusion.43
  90.5 1.5 dynamic-slice_bitcast_fusion.2
  93.8 2.5 %collective-permute-start.2 = (bf16[256,1664]{1,0:T(8,128)(2,1)}, bf16[256,1664]{1,0:T(8,128)(2,1)}, u32[]{:S(2)}, u32[]{:S(2)}) collective-permute-start(bf16[256,1664]{1,0:T(8,128)(2,1)} %get-tuple-element.36), channel_id=1, source_target_pairs={{0,6},{1,97},{2,0},{3,99},{4,2},{5,101},{6,4},{7,103},{8,14},{9,10... | collective-permute-start | bytes 2555912 | tf_op jit(solution)/shard_map/ppermute | solution.py:350
  97.1 2.3 collective-permute-start.7
  100.3 19.1 %collective-permute-done.7 = bf16[256,512]{1,0:T(8,128)(2,1)S(1)} collective-permute-done((bf16[256,512]{1,0:T(8,128)(2,1)S(1)}, bf16[256,512]{1,0:T(8,128)(2,1)S(1)}, u32[]{:S(2)}, u32[]{:S(2)}) %collective-permute-start.7) | collective-permute-done | bytes 262176 | tf_op jit(solution)/shard_map/ppermute | solution.py:350
  120.1 2.3 fusion.3.grad
  122.4 8.3 %pack.1 = bf16[128,72,128]{2,1,0:T(8,128)(2,1)} custom-call(s32[128,64]{1,0:T(8,128)} %get-tuple-element.20.inverse, s32[13,128]{1,0:T(8,128)} %bitcast.146, bf16[128,1664]{1,0:T(8,128)(2,1)} %fusion.3.grad), custom_call_target="tpu_custom_call" | custom-call | tf_op jit(solution)/shard_map/pack/pallas_call | solution.py:180
  130.7 5.3 %all-to-all-start.2 = ((bf16[128,72,128]{2,1,0:T(8,128)(2,1)}), bf16[128,72,128]{2,1,0:T(8,128)(2,1)S(1)}, u32[]{:S(2)}, u32[]{:S(2)}) async-start(bf16[128,72,128]{2,1,0:T(8,128)(2,1)} %pack.1), calls=%async_computation.2 | async-start | bytes 4718592 | tf_op jit(solution)/shard_map/all_to_all | solution.py:331
  137.4 2.4 %fusion.9 = bf16[256,1664]{1,0:T(8,128)(2,1)S(1)} fusion(bf16[256,1664]{1,0:T(8,128)(2,1)} %collective-permute-done.3, bf16[256,1664]{1,0:T(8,128)(2,1)} %collective-permute-done.2, bf16[256,1664]{1,0:T(8,128)(2,1)} %collective-permute-done.1, bf16[4,256,1664]{2,1,0:T(8,128)(2,1)} %bitcast.129, s32[]{:T(128)S(6)} %select_n.131), kind=kLoop, calls=%fused_computation.20 | loop fusion | flops 3407872 | bytes 4259844 | tf_op jit(solution)/shard_map/convert_element_type | solution.py:439
  141.6 2.9 %collective-permute-start.10 = (bf16[64,2176]{1,0:T(8,128)(2,1)}, bf16[64,2176]{1,0:T(8,128)(2,1)S(1)}, u32[]{:S(2)}, u32[]{:S(2)}) collective-permute-start(bf16[64,2176]{1,0:T(8,128)(2,1)} %get-tuple-element.38), channel_id=1, source_target_pairs={{0,16},{1,5},{2,18},{3,7},{4,20},{5,1},{6,22},{7,3},{8,24},{9,13},... | collective-permute-start | bytes 835592 | tf_op jit(solution)/shard_map/ppermute | solution.py:350
  146.5 22.9 %collective-permute-done.10 = bf16[64,2176]{1,0:T(8,128)(2,1)S(1)} collective-permute-done((bf16[64,2176]{1,0:T(8,128)(2,1)}, bf16[64,2176]{1,0:T(8,128)(2,1)S(1)}, u32[]{:S(2)}, u32[]{:S(2)}) %collective-permute-start.10) | collective-permute-done | bytes 278560 | tf_op jit(solution)/shard_map/ppermute | solution.py:350
  169.9 2.1 collective-permute-done.8
  174.0 2.2 collective-permute-start.13
  178.2 2.6 %collective-permute-done.13 = f32[16,2176]{1,0:T(8,128)S(1)} collective-permute-done((f32[16,2176]{1,0:T(8,128)}, f32[16,2176]{1,0:T(8,128)S(1)}, u32[]{:S(2)}, u32[]{:S(2)}) %collective-permute-start.13) | collective-permute-done | bytes 139296 | tf_op jit(solution)/shard_map/ppermute | solution.py:350
  181.9 1.8 collective-permute-done.11
  186.1 24.0 %all_to_all.20 = bf16[64,16,512]{2,1,0:T(8,128)(2,1)} all-to-all(bf16[64,16,512]{2,1,0:T(8,128)(2,1)S(1)} %broadcast_in_dim.2), channel_id=1, replica_groups=mesh['grp'=4,'dev_0'=4,'dev_1'=4,'dev_2'=2] {'grp','dev_0','dev_1'}, dimensions={0} | all-to-all | bytes 2097152 | tf_op jit(solution)/shard_map/all_to_all | solution.py:331
  210.8 8.5 %cold_sum.1 = f32[2048,128]{1,0:T(8,128)} custom-call(s32[128,128]{1,0:T(8,128)} %bitcast.137, bf16[128,72,128]{2,1,0:T(8,128)(2,1)} %copy-done.2), custom_call_target="tpu_custom_call" | custom-call | tf_op jit(solution)/shard_map/cold_sum/pallas_call | solution.py:215
  219.3 10.9 %hot_sum.1 = f32[4096,128]{1,0:T(8,128)} custom-call(s32[128,128]{1,0:T(8,128)} %bitcast.138, bf16[128,72,128]{2,1,0:T(8,128)(2,1)} %copy-done.2), custom_call_target="tpu_custom_call" | custom-call | tf_op jit(solution)/shard_map/hot_sum/pallas_call | solution.py:241
  230.2 3.7 %unpack.1 = (f32[1664,256]{1,0:T(8,128)}, f32[256,1664]{1,0:T(8,128)}, f32[13,128]{1,0:T(8,128)}, f32[16,128]{1,0:T(8,128)}, f32[16,128]{1,0:T(8,128)}) custom-call(s32[1]{0:T(128)} %bitcast.47.core, bf16[1024,512]{1,0:T(8,128)(2,1)} %bitcast.48.held, bf16[1024,512]{1,0:T(8,128)(2,1)} %collective-permute-done.14.came), custom_call_target="tpu_custom_call" | custom-call | tf_op jit(solution)/shard_map/unpack/pallas_call | solution.py:301
  (106 shorter events, 30.3 us)
Async XLA Ops:
  0.6 52.5 %copy-start = (bf16[4096,128]{1,0:T(8,128)(2,1)S(1)}, bf16[4096,128]{1,0:T(8,128)(2,1)}, u32[]{:S(2)}) copy-start(bf16[4096,128]{1,0:T(8,128)(2,1)} %param.18) | copy-start | bytes 3145732
  11.4 20.4 %all-to-all-start = ((s32[128,1,128]{2,1,0:T(1,128)}), s32[128,1,128]{2,1,0:T(1,128)S(1)}, u32[]{:S(2)}, u32[]{:S(2)}) async-start(s32[128,1,128]{2,1,0:T(1,128)} %bitcast.144), calls=%async_computation | async-start | bytes 131072 | tf_op jit(solution)/shard_map/all_to_all | solution.py:331
  40.1 26.8 %all-to-all-start.1 = ((bf16[128,40,128]{2,1,0:T(8,128)(2,1)}), bf16[128,40,128]{2,1,0:T(8,128)(2,1)S(1)}, u32[]{:S(2)}, u32[]{:S(2)}) async-start(bf16[128,40,128]{2,1,0:T(8,128)(2,1)} %bitcast.123), calls=%async_computation.1 | async-start | bytes 2621440 | tf_op jit(solution)/shard_map/all_to_all | solution.py:331
  50.9 2.2 copy-start.16
  53.1 22.7 %copy-start.9 = (bf16[256,1664]{1,0:T(8,128)(2,1)S(1)}, bf16[256,1664]{1,0:T(8,128)(2,1)}, u32[]{:S(2)}) copy-start(bf16[256,1664]{1,0:T(8,128)(2,1)} %param.21) | copy-start | bytes 2555908
  53.1 22.7 %copy-start.15 = (f32[1664]{0:T(1024)S(1)}, f32[1664]{0:T(1024)}, u32[]{:S(2)}) copy-start(f32[1664]{0:T(1024)} %param.22) | copy-start | bytes 19972
  74.1 4.0 %copy-start.7 = (bf16[4,4,4,16,1664]{4,3,2,1,0:T(8,128)(2,1)S(1)}, bf16[4,4,4,16,1664]{4,3,2,1,0:T(8,128)(2,1)}, u32[]{:S(2)}) copy-start(bf16[4,4,4,16,1664]{4,3,2,1,0:T(8,128)(2,1)} %copy.37) | copy-start | bytes 10223620
  78.1 4.5 %copy-start.17 = (s32[128]{0:T(128)S(1)}, s32[128]{0:T(128)}, u32[]{:S(2)}) copy-start(s32[128]{0:T(128)} %param.19) | copy-start | bytes 1540
  78.1 5.6 %copy-start.8 = (bf16[4,4,4,16,1664]{4,3,2,1,0:T(8,128)(2,1)S(1)}, bf16[4,4,4,16,1664]{4,3,2,1,0:T(8,128)(2,1)}, u32[]{:S(2)}) copy-start(bf16[4,4,4,16,1664]{4,3,2,1,0:T(8,128)(2,1)} %copy.36) | copy-start | bytes 10223620
  82.5 1.1 copy-start.3
  86.3 1.9 collective-permute-start.4
  86.6 2.7 %collective-permute-start = (bf16[128,2688]{1,0:T(8,128)(2,1)S(1)}, bf16[128,2688]{1,0:T(8,128)(2,1)S(1)}, u32[]{:S(2)}, u32[]{:S(2)}) collective-permute-start(bf16[128,2688]{1,0:T(8,128)(2,1)S(1)} %pad_maximum_fusion.8), channel_id=1, source_target_pairs={{0,1},{1,0},{2,3},{3,2},{4,5},{5,4},{6,7},{7,6},{8,9},{9,8},{10,11... | collective-permute-start | bytes 2064392 | tf_op jit(solution)/shard_map/ppermute | solution.py:425
  90.5 2.5 %copy-start.6 = (bf16[1024,1664]{1,0:T(8,128)(2,1)}, bf16[1024,1664]{1,0:T(8,128)(2,1)S(1)}, u32[]{:S(2)}) copy-start(bf16[1024,1664]{1,0:T(8,128)(2,1)S(1)} %convolution_convert_fusion) | copy-start | bytes 10223620
  90.5 29.6 %copy-start.11 = (f32[128,1664]{1,0:T(8,128)S(1)}, f32[128,1664]{1,0:T(8,128)}, u32[]{:S(2)}) copy-start(f32[128,1664]{1,0:T(8,128)} %get-tuple-element.58) | copy-start | bytes 2555908
  93.0 27.1 %copy-start.10 = (bf16[1664,256]{1,0:T(8,128)(2,1)S(1)}, bf16[1664,256]{1,0:T(8,128)(2,1)}, u32[]{:S(2)}) copy-start(bf16[1664,256]{1,0:T(8,128)(2,1)} %param.20) | copy-start | bytes 2555908
  93.0 44.4 %collective-permute-start.3 = (bf16[256,1664]{1,0:T(8,128)(2,1)}, bf16[256,1664]{1,0:T(8,128)(2,1)}, u32[]{:S(2)}, u32[]{:S(2)}) collective-permute-start(bf16[256,1664]{1,0:T(8,128)(2,1)} %get-tuple-element.35), channel_id=1, source_target_pairs={{0,4},{1,65},{2,6},{3,67},{4,0},{5,69},{6,2},{7,71},{8,12},{9,73},... | collective-permute-start | bytes 2555912 | tf_op jit(solution)/shard_map/ppermute | solution.py:350
  93.8 43.6 %collective-permute-start.2 = (bf16[256,1664]{1,0:T(8,128)(2,1)}, bf16[256,1664]{1,0:T(8,128)(2,1)}, u32[]{:S(2)}, u32[]{:S(2)}) collective-permute-start(bf16[256,1664]{1,0:T(8,128)(2,1)} %get-tuple-element.36), channel_id=1, source_target_pairs={{0,6},{1,97},{2,0},{3,99},{4,2},{5,101},{6,4},{7,103},{8,14},{9,10... | collective-permute-start | bytes 2555912 | tf_op jit(solution)/shard_map/ppermute | solution.py:350
  96.2 41.1 %collective-permute-start.1 = (bf16[256,1664]{1,0:T(8,128)(2,1)}, bf16[256,1664]{1,0:T(8,128)(2,1)}, u32[]{:S(2)}, u32[]{:S(2)}) collective-permute-start(bf16[256,1664]{1,0:T(8,128)(2,1)} %get-tuple-element.34), channel_id=1, source_target_pairs={{0,2},{1,33},{2,4},{3,35},{4,6},{5,37},{6,0},{7,39},{8,10},{9,41},... | collective-permute-start | bytes 2555912 | tf_op jit(solution)/shard_map/ppermute | solution.py:350
  97.1 22.3 %collective-permute-start.7 = (bf16[256,512]{1,0:T(8,128)(2,1)S(1)}, bf16[256,512]{1,0:T(8,128)(2,1)S(1)}, u32[]{:S(2)}, u32[]{:S(2)}) collective-permute-start(bf16[256,512]{1,0:T(8,128)(2,1)S(1)} %get-tuple-element.41), channel_id=1, source_target_pairs={{0,4},{1,65},{2,6},{3,67},{4,0},{5,69},{6,2},{7,71},{8,12},{9,73},... | collective-permute-start | bytes 786440 | tf_op jit(solution)/shard_map/ppermute | solution.py:350
  99.4 36.7 %collective-permute-start.6 = (bf16[256,512]{1,0:T(8,128)(2,1)}, bf16[256,512]{1,0:T(8,128)(2,1)}, u32[]{:S(2)}, u32[]{:S(2)}) collective-permute-start(bf16[256,512]{1,0:T(8,128)(2,1)} %get-tuple-element.42), channel_id=1, source_target_pairs={{0,6},{1,97},{2,0},{3,99},{4,2},{5,101},{6,4},{7,103},{8,14},{9,10... | collective-permute-start | bytes 786440 | tf_op jit(solution)/shard_map/ppermute | solution.py:350
  119.4 11.4 %copy-start.13 = (bf16[256,512]{1,0:T(8,128)(2,1)}, bf16[256,512]{1,0:T(8,128)(2,1)S(1)}, u32[]{:S(2)}) copy-start(bf16[256,512]{1,0:T(8,128)(2,1)S(1)} %collective-permute-done.7) | copy-start | bytes 786436
  119.4 16.7 %collective-permute-start.5 = (bf16[256,512]{1,0:T(8,128)(2,1)}, bf16[256,512]{1,0:T(8,128)(2,1)}, u32[]{:S(2)}, u32[]{:S(2)}) collective-permute-start(bf16[256,512]{1,0:T(8,128)(2,1)} %get-tuple-element.40), channel_id=1, source_target_pairs={{0,2},{1,33},{2,4},{3,35},{4,6},{5,37},{6,0},{7,39},{8,10},{9,41},... | collective-permute-start | bytes 786440 | tf_op jit(solution)/shard_map/ppermute | solution.py:350
  130.7 54.5 %all-to-all-start.2 = ((bf16[128,72,128]{2,1,0:T(8,128)(2,1)}), bf16[128,72,128]{2,1,0:T(8,128)(2,1)S(1)}, u32[]{:S(2)}, u32[]{:S(2)}) async-start(bf16[128,72,128]{2,1,0:T(8,128)(2,1)} %pack.1), calls=%async_computation.2 | async-start | bytes 4718592 | tf_op jit(solution)/shard_map/all_to_all | solution.py:331
  141.6 27.7 %collective-permute-start.10 = (bf16[64,2176]{1,0:T(8,128)(2,1)}, bf16[64,2176]{1,0:T(8,128)(2,1)S(1)}, u32[]{:S(2)}, u32[]{:S(2)}) collective-permute-start(bf16[64,2176]{1,0:T(8,128)(2,1)} %get-tuple-element.38), channel_id=1, source_target_pairs={{0,16},{1,5},{2,18},{3,7},{4,20},{5,1},{6,22},{7,3},{8,24},{9,13},... | collective-permute-start | bytes 835592 | tf_op jit(solution)/shard_map/ppermute | solution.py:350
  144.4 25.5 %collective-permute-start.9 = (bf16[64,2176]{1,0:T(8,128)(2,1)S(1)}, bf16[64,2176]{1,0:T(8,128)(2,1)}, u32[]{:S(2)}, u32[]{:S(2)}) collective-permute-start(bf16[64,2176]{1,0:T(8,128)(2,1)S(1)} %get-tuple-element.39), channel_id=1, source_target_pairs={{0,24},{1,7},{2,26},{3,1},{4,28},{5,3},{6,30},{7,5},{8,0},{9,15},{... | collective-permute-start | bytes 835592 | tf_op jit(solution)/shard_map/ppermute | solution.py:350
  145.3 26.7 %collective-permute-start.8 = (bf16[64,2176]{1,0:T(8,128)(2,1)S(1)}, bf16[64,2176]{1,0:T(8,128)(2,1)}, u32[]{:S(2)}, u32[]{:S(2)}) collective-permute-start(bf16[64,2176]{1,0:T(8,128)(2,1)S(1)} %get-tuple-element.37), channel_id=1, source_target_pairs={{0,8},{1,3},{2,10},{3,5},{4,12},{5,7},{6,14},{7,1},{8,16},{9,11},{... | collective-permute-start | bytes 835592 | tf_op jit(solution)/shard_map/ppermute | solution.py:350
  174.0 6.8 %collective-permute-start.13 = (f32[16,2176]{1,0:T(8,128)}, f32[16,2176]{1,0:T(8,128)S(1)}, u32[]{:S(2)}, u32[]{:S(2)}) collective-permute-start(f32[16,2176]{1,0:T(8,128)} %get-tuple-element.49), channel_id=1, source_target_pairs={{0,64},{1,17},{2,66},{3,19},{4,68},{5,21},{6,70},{7,23},{8,72},{9,... | collective-permute-start | bytes 417800 | tf_op jit(solution)/shard_map/ppermute | solution.py:350
  176.1 5.1 %collective-permute-start.12 = (f32[16,2176]{1,0:T(8,128)S(1)}, f32[16,2176]{1,0:T(8,128)S(1)}, u32[]{:S(2)}, u32[]{:S(2)}) collective-permute-start(f32[16,2176]{1,0:T(8,128)S(1)} %get-tuple-element.50), channel_id=1, source_target_pairs={{0,96},{1,25},{2,98},{3,27},{4,100},{5,29},{6,102},{7,31},{8,104},... | collective-permute-start | bytes 417800 | tf_op jit(solution)/shard_map/ppermute | solution.py:350
  177.3 6.4 %collective-permute-start.11 = (f32[16,2176]{1,0:T(8,128)S(1)}, f32[16,2176]{1,0:T(8,128)}, u32[]{:S(2)}, u32[]{:S(2)}) collective-permute-start(f32[16,2176]{1,0:T(8,128)S(1)} %get-tuple-element.48), channel_id=1, source_target_pairs={{0,32},{1,9},{2,34},{3,11},{4,36},{5,13},{6,38},{7,15},{8,40},{9,1... | collective-permute-start | bytes 417800 | tf_op jit(solution)/shard_map/ppermute | solution.py:350
  185.3 25.5 %copy-start.2 = (bf16[128,72,128]{2,1,0:T(8,128)(2,1)}, bf16[128,72,128]{2,1,0:T(8,128)(2,1)S(1)}, u32[]{:S(2)}) copy-start(bf16[128,72,128]{2,1,0:T(8,128)(2,1)S(1)} %all-to-all-done.2.came) | copy-start | bytes 7077892
  210.1 20.1 %collective-permute-start.14 = (bf16[1024,512]{1,0:T(8,128)(2,1)}, bf16[1024,512]{1,0:T(8,128)(2,1)}, u32[]{:S(2)}, u32[]{:S(2)}) collective-permute-start(bf16[1024,512]{1,0:T(8,128)(2,1)} %bitcast.48.held), channel_id=1, source_target_pairs={{0,1},{1,0},{2,3},{3,2},{4,5},{5,4},{6,7},{7,6},{8,9},{9,8},{10,11... | collective-permute-start | bytes 3145736 | tf_op jit(solution)/shard_map/ppermute | solution.py:471
  219.3 14.6 %copy-start.1 = (bf16[4096,128]{1,0:T(8,128)(2,1)S(1)}, bf16[4096,128]{1,0:T(8,128)(2,1)}, u32[]{:S(2)}) copy-start(bf16[4096,128]{1,0:T(8,128)(2,1)} %param.18) | copy-start | bytes 3145732
  (4 other events, 3.3 us)

commit v4 on v3

--- a/solution.py
+++ b/solution.py
@@ -154,16 +154,12 @@
     )(position, hot_index, hot_rows, arrived)
 
 
-def pack_kernel(inverse, hot_index, grad, out, wide, picked):
+def pack_kernel(inverse, grad, out, wide, picked):
     samples, inputs = grad.shape
     devices = out.shape[0]
-    slots = lax.broadcasted_iota(I32, (HOT, samples), 0)
-    hot_block = jnp.zeros((HOT, 128), F32)
     for f in range(inputs // 128):
         part = grad[:, f * 128 : (f + 1) * 128]
         wide[f * samples : (f + 1) * samples, :] = part.astype(F32)
-        one_hot = (slots == hot_index[f : f + 1, :]).astype(F32).astype(BF16)
-        hot_block = hot_block + jnp.dot(one_hot, part, preferred_element_type=F32)
 
     def source(d, carried):
         for i in range(CAP):
@@ -171,29 +167,51 @@
         return carried
 
     lax.fori_loop(0, devices, source, 0)
-    out[:, :CAP, :] = picked[...].reshape(devices, CAP, 128).astype(BF16)
-    out[:, CAP:, :] = jnp.broadcast_to(hot_block.astype(BF16)[None], (devices, HOT, 128))
-
-
-def pack(inverse, hot_index, grad):
+    out[...] = picked[...].reshape(devices, CAP, 128).astype(BF16)
+
+
+def pack(inverse, grad):
     devices = inverse.shape[0]
     return pl.pallas_call(
         pack_kernel,
-        out_shape=jax.ShapeDtypeStruct((devices, CAP + HOT, 128), BF16),
-        in_specs=[SMEM, VMEM, VMEM],
+        out_shape=jax.ShapeDtypeStruct((devices, CAP, 128), BF16),
+        in_specs=[SMEM, VMEM],
         out_specs=VMEM,
         scratch_shapes=[
             pltpu.VMEM((grad.size // 128, 128), F32),
             pltpu.VMEM((devices * CAP, 128), F32),
         ],
         name="pack",
-    )(inverse, hot_index, grad)
+    )(inverse, grad)
+
+
+def hot_block_kernel(hot_index, grad, out):
+    features, samples = hot_index.shape
+    slots = lax.broadcasted_iota(I32, (HOT, samples), 0)
+    total = jnp.zeros((HOT, 128), F32)
+    for f in range(features):
+        one_hot = (slots == hot_index[f : f + 1, :]).astype(F32).astype(BF16)
+        part = grad[:, f * 128 : (f + 1) * 128]
+        total = total + jnp.dot(one_hot, part, preferred_element_type=F32)
+    total = total.astype(BF16)
+    for b in range(HOT // 8):
+        out[:, b * 128 : (b + 1) * 128] = total[b * 8 : (b + 1) * 8, :]
+
+
+def hot_block(hot_index, grad):
+    return pl.pallas_call(
+        hot_block_kernel,
+        out_shape=jax.ShapeDtypeStruct((8, HOT // 8 * 128), BF16),
+        in_specs=[VMEM, VMEM],
+        out_specs=VMEM,
+        name="hot_block",
+    )(hot_index, grad)
 
 
 def cold_kernel(wanted, came, out, wide, *sums):
     for way in sums:
         way[...] = jnp.zeros(way.shape, F32)
-    wide[...] = came[:, :CAP, :].astype(F32)
+    wide[...] = came[...].astype(F32)
 
     def source(d, carried):
         for i in range(CAP // WAYS):
@@ -223,29 +241,56 @@
     )(wanted, came)
 
 
-def hot_kernel(listed, came, out, wide):
+def hot_kernel(owners, listed, held, came, out, wide_held, wide_came):
     out[...] = jnp.zeros(out.shape, F32)
-    wide[...] = came[:, CAP:, :].astype(F32)
-
-    def source(d, carried):
-        places = [pl.ds(listed[d, CAP + i], 1) for i in range(HOT)]
-        held = [out[here, :] + wide[d, i : i + 1, :] for i, here in enumerate(places)]
-        for here, row in zip(places, held):
-            out[here, :] = row
+    tall = held.shape[0]
+    for b in range(held.shape[1] // 128):
+        lanes = slice(b * 128, (b + 1) * 128)
+        wide_held[b * tall : (b + 1) * tall, :] = held[:, lanes].astype(F32)
+        wide_came[b * tall : (b + 1) * tall, :] = came[:, lanes].astype(F32)
+
+    def source(k, carried):
+        first, second, third = k >> 4, (k >> 2) & 3, k & 3
+        base = (second * 8 + (first >> 1) * 2) * tall + third * 16 + (first & 1) * 8
+        for side, wide in ((0, wide_held), (1, wide_came)):
+            d = owners[side, k]
+            places = [pl.ds(listed[d, CAP + i], 1) for i in range(HOT)]
+            sums = []
+            for i, here in enumerate(places):
+                at = (i // 16 * 4 + i // 8 % 2) * tall + i % 8
+                sums.append(out[here, :] + wide[pl.ds(base + at, 1), :])
+            for here, row in zip(places, sums):
+                out[here, :] = row
         return carried
 
-    lax.fori_loop(0, came.shape[0], source, 0)
-
-
-def hot_sum(listed, came, hot_rows):
+    lax.fori_loop(0, 64, source, 0)
+
+
+def hot_sum(owners, listed, held, came, hot_rows):
     return pl.pallas_call(
         hot_kernel,
         out_shape=jax.ShapeDtypeStruct((hot_rows, 128), F32),
-        in_specs=[SMEM, VMEM],
+        in_specs=[SMEM, SMEM, VMEM, VMEM],
         out_specs=VMEM,
-        scratch_shapes=[pltpu.VMEM((came.shape[0], HOT, 128), F32)],
+        scratch_shapes=[pltpu.VMEM((held.size // 128, 128), F32)] * 2,
         name="hot_sum",
-    )(listed, came)
+    )(owners, listed, held, came)
+
+
+def hot_owners(spot, core):
+    k = jnp.arange(64, dtype=I32)
+    steps = [k >> 4, (k >> 2) & 3, k & 3]
+    tables = []
+    for c in range(2):
+        place = [0, 0, 0]
+        for axis, step in zip(ORDER[c], steps):
+            back = jnp.where(step == 2, 3, jnp.where(step == 3, 2, step))
+            place[axis] = (spot[axis] - back + 4) & 3
+        tables.append(((place[0] * 4 + place[1]) * 4 + place[2]) * 2 + c)
+    first = core == 0
+    return jnp.stack(
+        [jnp.where(first, tables[0], tables[1]), jnp.where(first, tables[1], tables[0])]
+    )
 
 
 def unpack_kernel(core, held, came, u_out, v_out, bias_out, mlp_bias_out, out_weight_out, wide):
@@ -341,23 +386,106 @@
     return pairs
 
 
-def scatter_phase(x, phase, core):
-    here = jnp.where(
-        core == 0, lax.axis_index(CHIPS[ORDER[0][phase]]), lax.axis_index(CHIPS[ORDER[1][phase]])
-    )
-    tiles = x.reshape(4, -1, x.shape[-1])
-    came = [
-        lax.ppermute(
-            lax.dynamic_index_in_dim(tiles, (here + s) % 4, 0, False),
-            GRP_DEV,
-            route_pairs(phase, s),
-        )
-        for s in (1, 3, 2)
-    ]
-    total = lax.dynamic_index_in_dim(tiles, here, 0, False).astype(F32)
-    for tile in came:
-        total = total + tile.astype(F32)
+SHIFTS = (1, 3, 2)
+
+
+def here_of(phase, core):
+    here = [lax.axis_index(CHIPS[ORDER[c][phase]]) for c in range(2)]
+    return jnp.where(core == 0, here[0], here[1])
+
+
+def send_on(phase, pieces):
+    return [lax.ppermute(p, GRP_DEV, route_pairs(phase, s)) for p, s in zip(pieces, SHIFTS)]
+
+
+def add_up(own, came):
+    total = own.astype(F32)
+    for part in came:
+        total = total + part.astype(F32)
     return total
+
+
+def fold_first_kernel(here, mlp, cross, hot, *refs):
+    mlp_came, cross_came, (outs, own, hot_out, total) = refs[:3], refs[3:6], (
+        refs[6:9],
+        refs[9],
+        refs[10],
+        refs[11],
+    )
+    tall, inputs = mlp.shape
+    part = mlp[...]
+    for c in mlp_came:
+        part = part + c[...].astype(F32)
+    total[:, :inputs] = part
+    part = cross[...]
+    for c in cross_came:
+        part = part + c[:tall, :].astype(F32)
+    total[:, inputs:] = part
+    blocks = [hot[...].astype(F32)] + [c[tall:, :].astype(F32) for c in cross_came]
+    lanes = hot.shape[1] // 2
+    hot_rows = jnp.concatenate(
+        [b[:, :lanes] for b in blocks] + [b[:, lanes:] for b in blocks]
+    ).astype(BF16)
+    hot_out[...] = hot_rows
+    count = tall // 4
+    for out, s in zip(outs, SHIFTS):
+        at = pl.multiple_of(((here[0] + s) & 3) * count, count)
+        out[:, : total.shape[1]] = total[pl.ds(at, count), :].astype(BF16)
+        out[:, total.shape[1] :] = hot_rows
+    own[...] = total[pl.ds(pl.multiple_of(here[0] * count, count), count), :]
+
+
+def fold_first(here, mlp, cross, hot, mlp_came, cross_came):
+    tall, wide = mlp.shape[0], mlp.shape[1] + cross.shape[1]
+    lanes = hot.shape[1] // 2
+    out = jax.ShapeDtypeStruct((tall // 4, wide + lanes), BF16)
+    got = pl.pallas_call(
+        fold_first_kernel,
+        out_shape=(out, out, out)
+        + (
+            jax.ShapeDtypeStruct((tall // 4, wide), F32),
+            jax.ShapeDtypeStruct((tall // 4, lanes), BF16),
+        ),
+        in_specs=[SMEM] + [VMEM] * 9,
+        out_specs=(VMEM,) * 5,
+        scratch_shapes=[pltpu.VMEM((tall, wide), F32)],
+        name="fold_first",
+    )(here.reshape(1), mlp, cross, hot, *mlp_came, *cross_came)
+    return got[:3], got[3], got[4]
+
+
+def fold_second_kernel(here, own_in, hot, *refs):
+    came, outs, own, hot_out, total = refs[:3], refs[3:6], refs[6], refs[7], refs[8]
+    wide = own_in.shape[1]
+    lanes = hot.shape[1]
+    part = own_in[...]
+    for c in came:
+        part = part + c[:, :wide].astype(F32)
+    total[...] = part
+    blocks = [hot[...]] + [c[:, wide:] for c in came]
+    for j, block in enumerate(blocks):
+        for t in range(4):
+            hot_out[:, (j * 4 + t) * lanes : (j * 4 + t + 1) * lanes] = block[t * 16 : t * 16 + 16]
+    for out, s in zip(outs, SHIFTS):
+        at = pl.multiple_of(((here[0] + s) & 3) * 16, 16)
+        out[:, :wide] = total[pl.ds(at, 16), :].astype(BF16)
+        out[:, wide:] = hot_out[...]
+    own[...] = total[pl.ds(pl.multiple_of(here[0] * 16, 16), 16), :]
+
+
+def fold_second(here, own, hot, came):
+    wide, lanes = own.shape[1], 16 * hot.shape[1]
+    out = jax.ShapeDtypeStruct((16, wide + lanes), BF16)
+    got = pl.pallas_call(
+        fold_second_kernel,
+        out_shape=(out, out, out)
+        + (jax.ShapeDtypeStruct((16, wide), F32), jax.ShapeDtypeStruct((16, lanes), BF16)),
+        in_specs=[SMEM] + [VMEM] * 5,
+        out_specs=(VMEM,) * 5,
+        scratch_shapes=[pltpu.VMEM(own.shape, F32)],
+        name="fold_second",
+    )(here.reshape(1), own, hot, *came)
+    return got[:3], got[3], got[4]
 
 
 def by_core(x):
@@ -423,10 +551,13 @@
     mine = lax.dynamic_slice(hidden_grad, (0, core * half), (samples, half))
     other = lax.dynamic_slice(hidden_grad, (0, (1 - core) * half), (samples, half))
     other = lax.ppermute(jnp.concatenate([other, cross_out], axis=1), CORE, SWAP)
-    mlp_part = contract_rows(
-        jnp.concatenate([mine, other[:, :half]], axis=0),
-        jnp.concatenate([cross_out, other[:, half:]], axis=0),
-    ).astype(BF16)
+    left = jnp.concatenate([mine, other[:, :half]], axis=0)
+    right = jnp.concatenate([cross_out, other[:, half:]], axis=0)
+    here = here_of(0, core)
+
+    def mlp_piece(shift):
+        at = (here + shift) % 4 * (half // 4)
+        return contract_rows(lax.dynamic_slice_in_dim(left, at, half // 4, 1), right)
 
     cross_out_grad = jnp.dot(hidden_grad, mlp_weight, preferred_element_type=F32)
     term_grad = (cross_out_grad * input_wide).astype(BF16)
@@ -436,38 +567,52 @@
         cross_out_grad * (cross_term + 1.0) + contract_cols(low_grad, cross_u)
     ).astype(BF16)
 
-    mlp_sum = scatter_phase(mlp_part, 0, core).astype(BF16)
+    mlp_came = send_on(0, [mlp_piece(s).astype(BF16) for s in SHIFTS])
 
     first = core == 0
-    pair_u = jnp.concatenate([low_grad, first_input], axis=1)
-    pair_v = jnp.concatenate([cross_low, term_grad], axis=1)
+    pad = jnp.zeros((samples, 4 * WIDE - inputs), BF16)
+    pair_u = jnp.concatenate([low_grad, first_input, pad], axis=1)
+    pair_v = jnp.concatenate([cross_low, term_grad, pad], axis=1)
     held = jnp.where(first, pair_u, pair_v)
     came = lax.ppermute(jnp.where(first, pair_v, pair_u), CORE, SWAP)
     both = jnp.concatenate([held, came], axis=0)
-    cross_part = contract_rows(both[:, :rank], both[:, rank:])
     vectors = jnp.concatenate([cross_bias_part, bias_grad, out_grad])
     vector_rows = vectors.size // 128
+    start = inputs - 3 * WIDE
     vectors = jnp.pad(
-        vectors.reshape(vector_rows, 128), ((0, rank - vector_rows), (0, 4 * WIDE - inputs - 128))
-    )
-    cross_part = jnp.concatenate(
-        [cross_part[:, q * WIDE : (q + 1) * WIDE] for q in range(3)]
-        + [jnp.concatenate([cross_part[:, 3 * WIDE :], vectors], axis=1)],
-        axis=0,
-    ).astype(BF16)
-    cross_sum = scatter_phase(cross_part, 0, core).astype(BF16)
-
-    payload = pack(inverse, hot_index, pooled_grad)
+        vectors.reshape(vector_rows, 128), ((0, rank - vector_rows), (start, WIDE - start - 128))
+    )
+
+    def cross_piece(shift):
+        at = (here + shift) % 4
+        part = lax.dynamic_slice_in_dim(both, rank + at * WIDE, WIDE, 1)
+        return contract_rows(both[:, :rank], part) + jnp.where(at == 3, vectors, 0.0)
+
+    hot_part = hot_block(hot_index, pooled_grad)
+    cross_came = send_on(
+        0, [jnp.concatenate([cross_piece(s).astype(BF16), hot_part]) for s in SHIFTS]
+    )
+
+    payload = pack(inverse, pooled_grad)
     back = exchange(payload, GRP_DEV)
 
-    sums = scatter_phase(jnp.concatenate([mlp_sum, cross_sum], axis=1), 1, core)
-    sums = scatter_phase(sums, 2, core)
+    pieces, own, hot_part = fold_first(
+        here_of(1, core), mlp_piece(0), cross_piece(0), hot_part, mlp_came, cross_came
+    )
+    came = send_on(1, pieces)
+    pieces, own, hot_part = fold_second(here_of(2, core), own, hot_part, came)
+    came = send_on(2, pieces)
+    wide = own.shape[1]
+    sums = add_up(own, [c[:, :wide] for c in came])
+    hot_part = jnp.concatenate([hot_part] + [c[:, wide:] for c in came])
     mlp_weight_grad = sums[:, :inputs]
     shared = jnp.broadcast_to(sums[None, :, inputs:].astype(BF16), (chips, 16, WIDE))
     shared, back = lax.optimization_barrier((shared, back))
     shared = exchange(shared, CHIPS).reshape(-1, WIDE)
+    hot_other = lax.ppermute(hot_part, CORE, SWAP)
     cold_grad = cold_sum(got, back, cold_table.shape[0])
-    hot_grad = hot_sum(got, back, hot_table.shape[0])
+    owners = hot_owners([lax.axis_index(axis) for axis in CHIPS], core)
+    hot_grad = hot_sum(owners, got, hot_part, hot_other, hot_table.shape[0])
     other_shared = lax.ppermute(shared, CORE, SWAP)
     cross_u_grad, cross_v_grad, cross_bias_grad, mlp_bias_grad, out_weight_grad = unpack(
         core, shared, other_shared, inputs, rank, hidden_units

time: 236 us -> 223 us (0.945)
  waiting for transfers between devices: 70.7 us -> 47.8 us
  Pallas kernels: 54.6 us -> 62.4 us
  local copies, waits for them, and re-layouts: 23 us -> 18.9 us
  matrix products: 15.4 us -> 18.4 us
  starting transfers between devices: 38.4 us -> 40.9 us
    ppermute x12 -> x13, waiting for transfers between devices: 49.5 us -> 27.4 us  [the longest x12 27.4 us: send_on(): lax.ppermute(p, GRP_DEV, route_pairs(phase, s))]
    pallas_call x1 -> x4, Pallas kernels: 8.34 us -> 16.5 us  [the longest x1 7.69 us: pack(): pl.pallas_call(pack_kernel, out_shape=jax.ShapeDtypeStruct((devices, CAP,...]
    dot_general x2 -> x8, matrix products: 1.61 us -> 7.54 us  [contract_rows(): lax.dot_general(former, latter, (((0,), (0,)), ((), ())), preferred_eleme...]
    squeeze x4 -> x0, local copies, waits for them, and re-layouts: 3.84 us -> none  [scatter_phase(): lax.dynamic_index_in_dim(tiles, (here + s) % 4, 0, False)]
    convert_element_type x2 -> x0, other arithmetic: 3.6 us -> none  [the longest x1 2.35 us: per_device(): mlp_sum = scatter_phase(mlp_part, 0, core).astype(BF16)]
    ppermute x12 -> x13, starting transfers between devices: 16.2 us -> 17.1 us  [the longest x12 16.5 us: send_on(): lax.ppermute(p, GRP_DEV, route_pairs(phase, s))]
  transfers between devices with their start and end apart: 18 -> 19, of which waited for: 11 -> 10; matrix products, arithmetic and copies ran while one was open for 10% -> 10% of each run, Pallas kernels for 12% -> 16%
where the time goes in v4:
time: 223 us; the launch traced here: 221 us
  Pallas kernels  62.4 us (28%)
  waiting for transfers between devices  47.8 us (21%)
  starting transfers between devices  40.9 us (18%)
  blocking collectives  26.2 us (12%)
  local copies, waits for them, and re-layouts  18.9 us (8%)
  matrix products  18.4 us (8%)
  other arithmetic  4.96 us (2%)
    ppermute x12, waiting for transfers between devices, send_on(): lax.ppermute(p, GRP_DEV, route_pairs(phase, s))  27.4 us
    all_to_all x1, blocking collectives, exchange(): return lax.all_to_all(x, axes, split_axis=0, concat_axis=0, tiled=True)  26.2 us
    all_to_all x3, starting transfers between devices, exchange(): return lax.all_to_all(x, axes, split_axis=0, concat_axis=0, tiled=True)  23.3 us
    all_to_all x3, waiting for transfers between devices, exchange(): return lax.all_to_all(x, axes, split_axis=0, concat_axis=0, tiled=True)  20.4 us
    ppermute x12, starting transfers between devices, send_on(): lax.ppermute(p, GRP_DEV, route_pairs(phase, s))  16.5 us
    pallas_call x1, Pallas kernels, hot_sum(): pl.pallas_call(hot_kernel, out_shape=jax.ShapeDtypeStruct((hot_rows, 128)...  10.6 us
    pallas_call x1, Pallas kernels, route(): pl.pallas_call(route_kernel, out_shape=(jax.ShapeDtypeStruct((128, 128),...  9.35 us
    pallas_call x1, Pallas kernels, cold_sum(): pl.pallas_call(cold_kernel, out_shape=jax.ShapeDtypeStruct((shard_rows, 1...  8.49 us
  transfers between devices with their start and end apart: 19, of which 10 were waited for; matrix products, arithmetic and copies ran while one was open for 10% of the time, Pallas kernels for 16%

profile of v4, /device:TPU:0, one launch (start us, length us, event | category | flops | bytes accessed | tf_op | source)
XLA Modules:
  0.0 220.9 jit_solution(3611618287186346620)
XLA Ops:
  2.1 9.3 %route.1 = (s32[128,128]{1,0:T(8,128)}, s32[128,64]{1,0:T(8,128)}, s32[26,128]{1,0:T(8,128)}) custom-call(s32[26,128]{1,0:T(8,128)} %reshape.287.ids.ids_lanes, s32[1,32]{1,0:T(1,128)} %hot_list.1, s32[26,128]{1,0:T(8,128)} %reshape.287.ids.ids_lanes, s32[2048,128]{1,0:T(8,128)} %bitcast.89), custom_call_target="tpu_custom_call" | custom-call | tf_op jit(solution)/shard_map/route/pallas_call | solution.py:84
  11.4 11.2 %all-to-all-start = ((s32[128,1,128]{2,1,0:T(1,128)}), s32[128,1,128]{2,1,0:T(1,128)S(1)}, u32[]{:S(2)}, u32[]{:S(2)}) async-start(s32[128,1,128]{2,1,0:T(1,128)} %bitcast.97), calls=%async_computation | async-start | bytes 131072 | tf_op jit(solution)/shard_map/all_to_all | solution.py:376
  23.7 8.1 %all-to-all-done = s32[128,1,128]{2,1,0:T(1,128)S(1)} async-done(((s32[128,1,128]{2,1,0:T(1,128)}), s32[128,1,128]{2,1,0:T(1,128)S(1)}, u32[]{:S(2)}, u32[]{:S(2)}) %all-to-all-start) | async-done | bytes 65568 | tf_op jit(solution)/shard_map/all_to_all | solution.py:376
  32.5 7.7 %fetch.1 = bf16[5120,128]{1,0:T(8,128)(2,1)} custom-call(s32[128,128]{1,0:T(8,128)} %bitcast.90, bf16[2048,128]{1,0:T(8,128)(2,1)} %table.1), custom_call_target="tpu_custom_call" | custom-call | tf_op jit(solution)/shard_map/fetch/pallas_call | solution.py:114
  40.2 4.8 %all-to-all-start.1 = ((bf16[128,40,128]{2,1,0:T(8,128)(2,1)}), bf16[128,40,128]{2,1,0:T(8,128)(2,1)S(1)}, u32[]{:S(2)}, u32[]{:S(2)}) async-start(bf16[128,40,128]{2,1,0:T(8,128)(2,1)} %bitcast.82), calls=%async_computation.1 | async-start | bytes 2621440 | tf_op jit(solution)/shard_map/all_to_all | solution.py:376
  45.0 3.6 %slice_bitcast_fusion.1 = (bf16[4,4,4,16,1664]{4,3,0,1,2:T(8,128)(2,1)S(1)}, bf16[4,4,4,16,1664]{4,3,1,2,0:T(8,128)(2,1)S(1)}) fusion(bf16[4,4,4,2,16,1664]{5,4,3,2,1,0:T(8,128)(2,1)} %bitcast.80), kind=kLoop, calls=%fused_computation.5 | loop fusion | bytes 13631488 | tf_op jit(solution)/shard_map/transpose | solution.py:496
  48.5 2.1 copy.36
  50.7 2.2 copy.37
  54.5 12.4 %all-to-all-done.1 = bf16[128,40,128]{2,1,0:T(8,128)(2,1)S(1)} async-done(((bf16[128,40,128]{2,1,0:T(8,128)(2,1)}), bf16[128,40,128]{2,1,0:T(8,128)(2,1)S(1)}, u32[]{:S(2)}, u32[]{:S(2)}) %all-to-all-start.1) | async-done | bytes 1310752 | tf_op jit(solution)/shard_map/all_to_all | solution.py:376
  68.0 6.1 %pool.1 = bf16[128,1664]{1,0:T(8,128)(2,1)} custom-call(s32[26,128]{1,0:T(8,128)} %get-tuple-element.29.position, s32[13,128]{1,0:T(8,128)} %bitcast.98, bf16[32,128]{1,0:T(8,128)(2,1)} %gather_fusion, bf16[5120,128]{1,0:T(8,128)(2,1)} %bitcast.81), custom_call_target="tpu_custom_call" | custom-call | tf_op jit(solution)/shard_map/pool/pallas_call | solution.py:147
  77.2 4.5 %multiply_convert_fusion.1 = (bf16[128,2048]{1,0:T(8,128)(2,1)S(1)}, f32[128,2048]{1,0:T(8,128)S(1)}) fusion(f32[2048]{0:T(1024)S(1)} %pad_maximum_fusion.11, bf16[128,1664]{1,0:T(8,128)(2,1)S(1)} %get-tuple-element.65, bf16[1024,1664]{1,0:T(8,128)(2,1)} %bitcast.87, bf16[1024,1664]{1,0:T(8,128)(2,1)S(1)} %bitcast.85), kind=kOutput, calls=%fused_computation.46 | convolution fusion | flops 887619584 | bytes 8822784 | tf_op jit(solution)/shard_map/dot_general | solution.py:372
  88.3 1.9 hot_block.1.hot
  96.3 2.5 %collective-permute-start.3 = (bf16[256,1664]{1,0:T(8,128)(2,1)}, bf16[256,1664]{1,0:T(8,128)(2,1)}, u32[]{:S(2)}, u32[]{:S(2)}) collective-permute-start(bf16[256,1664]{1,0:T(8,128)(2,1)} %convolution_convert_fusion.1), channel_id=1, source_target_pairs={{0,6},{1,97},{2,0},{3,99},{4,2},{5,101},{6,4},{7,103},{8,14},{9,10... | collective-permute-start | bytes 2555912 | tf_op jit(solution)/shard_map/ppermute | solution.py:398
  102.3 7.7 %pack.1 = bf16[128,40,128]{2,1,0:T(8,128)(2,1)} custom-call(s32[128,64]{1,0:T(8,128)} %get-tuple-element.39.inverse, bf16[128,1664]{1,0:T(8,128)(2,1)} %fusion.3.grad), custom_call_target="tpu_custom_call" | custom-call | tf_op jit(solution)/shard_map/pack/pallas_call | solution.py:175
  110.0 7.3 %all-to-all-start.2 = ((bf16[128,40,128]{2,1,0:T(8,128)(2,1)}), bf16[128,40,128]{2,1,0:T(8,128)(2,1)}, u32[]{:S(2)}, u32[]{:S(2)}) async-start(bf16[128,40,128]{2,1,0:T(8,128)(2,1)} %pack.1), calls=%async_computation.2 | async-start | bytes 2621440 | tf_op jit(solution)/shard_map/all_to_all | solution.py:376
  117.3 2.2 collective-permute-start.6
  119.4 3.8 %collective-permute-done.5.refs_3_ = bf16[264,512]{1,0:T(8,128)(2,1)} collective-permute-done((bf16[264,512]{1,0:T(8,128)(2,1)}, bf16[264,512]{1,0:T(8,128)(2,1)}, u32[]{:S(2)}, u32[]{:S(2)}) %collective-permute-start.5) | collective-permute-done | bytes 270368 | tf_op jit(solution)/shard_map/ppermute | solution.py:398
  126.5 8.6 %collective-permute-done.6.refs_4_ = bf16[264,512]{1,0:T(8,128)(2,1)} collective-permute-done((bf16[264,512]{1,0:T(8,128)(2,1)}, bf16[264,512]{1,0:T(8,128)(2,1)}, u32[]{:S(2)}, u32[]{:S(2)}) %collective-permute-start.6) | collective-permute-done | bytes 270368 | tf_op jit(solution)/shard_map/ppermute | solution.py:398
  135.1 2.6 %collective-permute-done.7.refs_5_ = bf16[264,512]{1,0:T(8,128)(2,1)} collective-permute-done((bf16[264,512]{1,0:T(8,128)(2,1)}, bf16[264,512]{1,0:T(8,128)(2,1)}, u32[]{:S(2)}, u32[]{:S(2)}) %collective-permute-start.7) | collective-permute-done | bytes 270368 | tf_op jit(solution)/shard_map/ppermute | solution.py:398
  137.7 4.5 %fold_first.1 = (bf16[64,2432]{1,0:T(8,128)(2,1)}, bf16[64,2432]{1,0:T(8,128)(2,1)}, bf16[64,2432]{1,0:T(8,128)(2,1)}, f32[64,2176]{1,0:T(8,128)}, bf16[64,256]{1,0:T(8,128)(2,1)}) custom-call(s32[1]{0:T(128)} %bitcast.6.here, f32[256,1664]{1,0:T(8,128)} %fusion.26.mlp, f32[256,512]{1,0:T(8,128)} %convolution_add_fusion.5.cross, ...), custom_call_target="tpu_custom_call" | custom-call | tf_op jit(solution)/shard_map/fold_first/pallas_call | solution.py:442
  142.2 2.3 %collective-permute-start.10 = (bf16[64,2432]{1,0:T(8,128)(2,1)}, bf16[64,2432]{1,0:T(8,128)(2,1)S(1)}, u32[]{:S(2)}, u32[]{:S(2)}) collective-permute-start(bf16[64,2432]{1,0:T(8,128)(2,1)} %get-tuple-element.34), channel_id=1, source_target_pairs={{0,16},{1,5},{2,18},{3,7},{4,20},{5,1},{6,22},{7,3},{8,24},{9,13},... | collective-permute-start | bytes 933896 | tf_op jit(solution)/shard_map/ppermute | solution.py:398
  145.4 2.4 %collective-permute-start.9 = (bf16[64,2432]{1,0:T(8,128)(2,1)}, bf16[64,2432]{1,0:T(8,128)(2,1)S(1)}, u32[]{:S(2)}, u32[]{:S(2)}) collective-permute-start(bf16[64,2432]{1,0:T(8,128)(2,1)} %get-tuple-element.33), channel_id=1, source_target_pairs={{0,24},{1,7},{2,26},{3,1},{4,28},{5,3},{6,30},{7,5},{8,0},{9,15},{... | collective-permute-start | bytes 933896 | tf_op jit(solution)/shard_map/ppermute | solution.py:398
  147.8 3.2 %collective-permute-done.10.refs_2_ = bf16[64,2432]{1,0:T(8,128)(2,1)S(1)} collective-permute-done((bf16[64,2432]{1,0:T(8,128)(2,1)}, bf16[64,2432]{1,0:T(8,128)(2,1)S(1)}, u32[]{:S(2)}, u32[]{:S(2)}) %collective-permute-start.10) | collective-permute-done | bytes 311328 | tf_op jit(solution)/shard_map/ppermute | solution.py:398
  150.9 3.2 %collective-permute-done.8.refs_0_ = bf16[64,2432]{1,0:T(8,128)(2,1)S(1)} collective-permute-done((bf16[64,2432]{1,0:T(8,128)(2,1)}, bf16[64,2432]{1,0:T(8,128)(2,1)S(1)}, u32[]{:S(2)}, u32[]{:S(2)}) %collective-permute-start.8) | collective-permute-done | bytes 311328 | tf_op jit(solution)/shard_map/ppermute | solution.py:398
  155.0 2.5 %fold_second.1 = (bf16[16,6272]{1,0:T(8,128)(2,1)}, bf16[16,6272]{1,0:T(8,128)(2,1)}, bf16[16,6272]{1,0:T(8,128)(2,1)}, f32[16,2176]{1,0:T(8,128)}, bf16[16,4096]{1,0:T(8,128)(2,1)}) custom-call(s32[1]{0:T(128)} %bitcast.5.here, f32[64,2176]{1,0:T(8,128)} %get-tuple-element.30.own_in, bf16[64,256]{1,0:T(8,128)(2,1)} %get-tuple-element.31.hot, ...), custom_call_target="tpu_custom_call" | custom-call | tf_op jit(solution)/shard_map/fold_second/pallas_call | solution.py:479
  158.5 2.2 collective-permute-start.12
  162.1 2.5 %collective-permute-done.11 = bf16[16,6272]{1,0:T(8,128)(2,1)S(1)} collective-permute-done((bf16[16,6272]{1,0:T(8,128)(2,1)}, bf16[16,6272]{1,0:T(8,128)(2,1)S(1)}, u32[]{:S(2)}, u32[]{:S(2)}) %collective-permute-start.11) | collective-permute-done | bytes 200736 | tf_op jit(solution)/shard_map/ppermute | solution.py:398
  164.6 1.8 collective-permute-done.12
  169.2 26.2 %all_to_all.20 = bf16[64,16,512]{2,1,0:T(8,128)(2,1)S(1)} all-to-all(bf16[64,16,512]{2,1,0:T(8,128)(2,1)S(1)} %broadcast_in_dim.36), channel_id=1, replica_groups=mesh['grp'=4,'dev_0'=4,'dev_1'=4,'dev_2'=2] {'grp','dev_0','dev_1'}, dimensions={0} | all-to-all | bytes 2097152 | tf_op jit(solution)/shard_map/all_to_all | solution.py:376
  197.4 8.5 %cold_sum.1 = f32[2048,128]{1,0:T(8,128)} custom-call(s32[128,128]{1,0:T(8,128)} %bitcast.91, bf16[128,40,128]{2,1,0:T(8,128)(2,1)} %all-to-all-done.2.came), custom_call_target="tpu_custom_call" | custom-call | tf_op jit(solution)/shard_map/cold_sum/pallas_call | solution.py:233
  206.7 10.6 %hot_sum.1 = f32[4096,128]{1,0:T(8,128)} custom-call(s32[2,64]{1,0:T(2,128)} %pad_add_fusion.owners, s32[128,128]{1,0:T(8,128)} %bitcast.92, bf16[64,4096]{1,0:T(8,128)(2,1)} %copy-done.12, bf16[64,4096]{1,0:T(8,128)(2,1)} %copy-done.14), custom_call_target="tpu_custom_call" | custom-call | tf_op jit(solution)/shard_map/hot_sum/pallas_call | solution.py:270
  217.2 3.7 %unpack.1 = (f32[1664,256]{1,0:T(8,128)}, f32[256,1664]{1,0:T(8,128)}, f32[13,128]{1,0:T(8,128)}, f32[16,128]{1,0:T(8,128)}, f32[16,128]{1,0:T(8,128)}) custom-call(s32[1]{0:T(128)} %bitcast.29.core, bf16[1024,512]{1,0:T(8,128)(2,1)} %bitcast.84, bf16[1024,512]{1,0:T(8,128)(2,1)} %collective-permute-done.15.came), custom_call_target="tpu_custom_call" | custom-call | tf_op jit(solution)/shard_map/unpack/pallas_call | solution.py:346
  (126 shorter events, 37.8 us)
Async XLA Ops:
  0.6 52.7 %copy-start = (bf16[4096,128]{1,0:T(8,128)(2,1)S(1)}, bf16[4096,128]{1,0:T(8,128)(2,1)}, u32[]{:S(2)}) copy-start(bf16[4096,128]{1,0:T(8,128)(2,1)} %param.18) | copy-start | bytes 3145732
  11.4 20.4 %all-to-all-start = ((s32[128,1,128]{2,1,0:T(1,128)}), s32[128,1,128]{2,1,0:T(1,128)S(1)}, u32[]{:S(2)}, u32[]{:S(2)}) async-start(s32[128,1,128]{2,1,0:T(1,128)} %bitcast.97), calls=%async_computation | async-start | bytes 131072 | tf_op jit(solution)/shard_map/all_to_all | solution.py:376
  40.2 26.8 %all-to-all-start.1 = ((bf16[128,40,128]{2,1,0:T(8,128)(2,1)}), bf16[128,40,128]{2,1,0:T(8,128)(2,1)S(1)}, u32[]{:S(2)}, u32[]{:S(2)}) async-start(bf16[128,40,128]{2,1,0:T(8,128)(2,1)} %bitcast.82), calls=%async_computation.1 | async-start | bytes 2621440 | tf_op jit(solution)/shard_map/all_to_all | solution.py:376
  53.1 22.8 %copy-start.8 = (bf16[256,1664]{1,0:T(8,128)(2,1)S(1)}, bf16[256,1664]{1,0:T(8,128)(2,1)}, u32[]{:S(2)}) copy-start(bf16[256,1664]{1,0:T(8,128)(2,1)} %param.21) | copy-start | bytes 2555908
  53.1 22.8 %copy-start.20 = (f32[1664]{0:T(1024)S(1)}, f32[1664]{0:T(1024)}, u32[]{:S(2)}) copy-start(f32[1664]{0:T(1024)} %param.22) | copy-start | bytes 19972
  74.1 3.1 %copy-start.6 = (bf16[4,4,4,16,1664]{4,3,2,1,0:T(8,128)(2,1)S(1)}, bf16[4,4,4,16,1664]{4,3,2,1,0:T(8,128)(2,1)}, u32[]{:S(2)}) copy-start(bf16[4,4,4,16,1664]{4,3,2,1,0:T(8,128)(2,1)} %copy.36) | copy-start | bytes 10223620
  77.2 4.6 %copy-start.23 = (s32[128]{0:T(128)S(1)}, s32[128]{0:T(128)}, u32[]{:S(2)}) copy-start(s32[128]{0:T(128)} %param.19) | copy-start | bytes 1540
  77.2 5.3 %copy-start.7 = (bf16[4,4,4,16,1664]{4,3,2,1,0:T(8,128)(2,1)S(1)}, bf16[4,4,4,16,1664]{4,3,2,1,0:T(8,128)(2,1)}, u32[]{:S(2)}) copy-start(bf16[4,4,4,16,1664]{4,3,2,1,0:T(8,128)(2,1)} %copy.37) | copy-start | bytes 10223620
  85.6 4.8 %collective-permute-start.1 = (bf16[128,2304]{1,0:T(8,128)(2,1)}, bf16[128,2304]{1,0:T(8,128)(2,1)S(1)}, u32[]{:S(2)}, u32[]{:S(2)}) collective-permute-start(bf16[128,2304]{1,0:T(8,128)(2,1)} %get-tuple-element.54), channel_id=1, source_target_pairs={{0,1},{1,0},{2,3},{3,2},{4,5},{5,4},{6,7},{7,6},{8,9},{9,8},{10,11... | collective-permute-start | bytes 1769480 | tf_op jit(solution)/shard_map/ppermute | solution.py:577
  86.5 4.2 %collective-permute-start = (bf16[128,2688]{1,0:T(8,128)(2,1)}, bf16[128,2688]{1,0:T(8,128)(2,1)}, u32[]{:S(2)}, u32[]{:S(2)}) collective-permute-start(bf16[128,2688]{1,0:T(8,128)(2,1)} %pad_maximum_fusion.6), channel_id=1, source_target_pairs={{0,1},{1,0},{2,3},{3,2},{4,5},{5,4},{6,7},{7,6},{8,9},{9,8},{10,11... | collective-permute-start | bytes 2064392 | tf_op jit(solution)/shard_map/ppermute | solution.py:553
  87.1 3.1 %copy-start.11 = (bf16[128,2048]{1,0:T(8,128)(2,1)S(1)}, bf16[128,2048]{1,0:T(8,128)(2,1)}, u32[]{:S(2)}) copy-start(bf16[128,2048]{1,0:T(8,128)(2,1)} %copy-done.10) | copy-start | bytes 1572868
  92.7 7.9 %copy-start.2 = (bf16[128,1024]{1,0:T(8,128)(2,1)}, bf16[128,1024]{1,0:T(8,128)(2,1)S(1)}, u32[]{:S(2)}) copy-start(bf16[128,1024]{1,0:T(8,128)(2,1)S(1)} %slice.80) | copy-start | bytes 786436
  94.2 43.5 %collective-permute-start.4 = (bf16[256,1664]{1,0:T(8,128)(2,1)}, bf16[256,1664]{1,0:T(8,128)(2,1)}, u32[]{:S(2)}, u32[]{:S(2)}) collective-permute-start(bf16[256,1664]{1,0:T(8,128)(2,1)} %convolution_convert_fusion), channel_id=1, source_target_pairs={{0,4},{1,65},{2,6},{3,67},{4,0},{5,69},{6,2},{7,71},{8,12},{9,73},... | collective-permute-start | bytes 2555912 | tf_op jit(solution)/shard_map/ppermute | solution.py:398
  96.3 41.4 %collective-permute-start.3 = (bf16[256,1664]{1,0:T(8,128)(2,1)}, bf16[256,1664]{1,0:T(8,128)(2,1)}, u32[]{:S(2)}, u32[]{:S(2)}) collective-permute-start(bf16[256,1664]{1,0:T(8,128)(2,1)} %convolution_convert_fusion.1), channel_id=1, source_target_pairs={{0,6},{1,97},{2,0},{3,99},{4,2},{5,101},{6,4},{7,103},{8,14},{9,10... | collective-permute-start | bytes 2555912 | tf_op jit(solution)/shard_map/ppermute | solution.py:398
  100.1 37.6 %collective-permute-start.2 = (bf16[256,1664]{1,0:T(8,128)(2,1)}, bf16[256,1664]{1,0:T(8,128)(2,1)}, u32[]{:S(2)}, u32[]{:S(2)}) collective-permute-start(bf16[256,1664]{1,0:T(8,128)(2,1)} %convolution_convert_fusion.2), channel_id=1, source_target_pairs={{0,2},{1,33},{2,4},{3,35},{4,6},{5,37},{6,0},{7,39},{8,10},{9,41},... | collective-permute-start | bytes 2555912 | tf_op jit(solution)/shard_map/ppermute | solution.py:398
  102.0 21.3 %collective-permute-start.5 = (bf16[264,512]{1,0:T(8,128)(2,1)}, bf16[264,512]{1,0:T(8,128)(2,1)}, u32[]{:S(2)}, u32[]{:S(2)}) collective-permute-start(bf16[264,512]{1,0:T(8,128)(2,1)} %get-tuple-element.64), channel_id=1, source_target_pairs={{0,2},{1,33},{2,4},{3,35},{4,6},{5,37},{6,0},{7,39},{8,10},{9,41},... | collective-permute-start | bytes 811016 | tf_op jit(solution)/shard_map/ppermute | solution.py:398
  110.0 59.1 %all-to-all-start.2 = ((bf16[128,40,128]{2,1,0:T(8,128)(2,1)}), bf16[128,40,128]{2,1,0:T(8,128)(2,1)}, u32[]{:S(2)}, u32[]{:S(2)}) async-start(bf16[128,40,128]{2,1,0:T(8,128)(2,1)} %pack.1), calls=%async_computation.2 | async-start | bytes 2621440 | tf_op jit(solution)/shard_map/all_to_all | solution.py:376
  117.3 7.6 %copy-start.3 = (bf16[128,1024]{1,0:T(8,128)(2,1)S(1)}, bf16[128,1024]{1,0:T(8,128)(2,1)}, u32[]{:S(2)}) copy-start(bf16[128,1024]{1,0:T(8,128)(2,1)} %copy-done.2) | copy-start | bytes 786436
  117.3 17.8 %collective-permute-start.6 = (bf16[264,512]{1,0:T(8,128)(2,1)}, bf16[264,512]{1,0:T(8,128)(2,1)}, u32[]{:S(2)}, u32[]{:S(2)}) collective-permute-start(bf16[264,512]{1,0:T(8,128)(2,1)} %get-tuple-element.63), channel_id=1, source_target_pairs={{0,6},{1,97},{2,0},{3,99},{4,2},{5,101},{6,4},{7,103},{8,14},{9,10... | collective-permute-start | bytes 811016 | tf_op jit(solution)/shard_map/ppermute | solution.py:398
  123.2 14.5 %collective-permute-start.7 = (bf16[264,512]{1,0:T(8,128)(2,1)}, bf16[264,512]{1,0:T(8,128)(2,1)}, u32[]{:S(2)}, u32[]{:S(2)}) collective-permute-start(bf16[264,512]{1,0:T(8,128)(2,1)} %get-tuple-element.62), channel_id=1, source_target_pairs={{0,4},{1,65},{2,6},{3,67},{4,0},{5,69},{6,2},{7,71},{8,12},{9,73},... | collective-permute-start | bytes 811016 | tf_op jit(solution)/shard_map/ppermute | solution.py:398
  142.2 8.7 %collective-permute-start.10 = (bf16[64,2432]{1,0:T(8,128)(2,1)}, bf16[64,2432]{1,0:T(8,128)(2,1)S(1)}, u32[]{:S(2)}, u32[]{:S(2)}) collective-permute-start(bf16[64,2432]{1,0:T(8,128)(2,1)} %get-tuple-element.34), channel_id=1, source_target_pairs={{0,16},{1,5},{2,18},{3,7},{4,20},{5,1},{6,22},{7,3},{8,24},{9,13},... | collective-permute-start | bytes 933896 | tf_op jit(solution)/shard_map/ppermute | solution.py:398
  144.5 9.6 %collective-permute-start.8 = (bf16[64,2432]{1,0:T(8,128)(2,1)}, bf16[64,2432]{1,0:T(8,128)(2,1)S(1)}, u32[]{:S(2)}, u32[]{:S(2)}) collective-permute-start(bf16[64,2432]{1,0:T(8,128)(2,1)} %get-tuple-element.32), channel_id=1, source_target_pairs={{0,8},{1,3},{2,10},{3,5},{4,12},{5,7},{6,14},{7,1},{8,16},{9,11},{... | collective-permute-start | bytes 933896 | tf_op jit(solution)/shard_map/ppermute | solution.py:398
  145.4 8.8 %collective-permute-start.9 = (bf16[64,2432]{1,0:T(8,128)(2,1)}, bf16[64,2432]{1,0:T(8,128)(2,1)S(1)}, u32[]{:S(2)}, u32[]{:S(2)}) collective-permute-start(bf16[64,2432]{1,0:T(8,128)(2,1)} %get-tuple-element.33), channel_id=1, source_target_pairs={{0,24},{1,7},{2,26},{3,1},{4,28},{5,3},{6,30},{7,5},{8,0},{9,15},{... | collective-permute-start | bytes 933896 | tf_op jit(solution)/shard_map/ppermute | solution.py:398
  150.9 3.2 %copy-start.15 = (bf16[64,2432]{1,0:T(8,128)(2,1)}, bf16[64,2432]{1,0:T(8,128)(2,1)S(1)}, u32[]{:S(2)}) copy-start(bf16[64,2432]{1,0:T(8,128)(2,1)S(1)} %collective-permute-done.10.refs_2_) | copy-start | bytes 933892
  157.4 7.1 %collective-permute-start.11 = (bf16[16,6272]{1,0:T(8,128)(2,1)}, bf16[16,6272]{1,0:T(8,128)(2,1)S(1)}, u32[]{:S(2)}, u32[]{:S(2)}) collective-permute-start(bf16[16,6272]{1,0:T(8,128)(2,1)} %get-tuple-element.36), channel_id=1, source_target_pairs={{0,32},{1,9},{2,34},{3,11},{4,36},{5,13},{6,38},{7,15},{8,40},{9,1... | collective-permute-start | bytes 602120 | tf_op jit(solution)/shard_map/ppermute | solution.py:398
  158.5 7.9 %collective-permute-start.12 = (bf16[16,6272]{1,0:T(8,128)(2,1)}, bf16[16,6272]{1,0:T(8,128)(2,1)S(1)}, u32[]{:S(2)}, u32[]{:S(2)}) collective-permute-start(bf16[16,6272]{1,0:T(8,128)(2,1)} %get-tuple-element.37), channel_id=1, source_target_pairs={{0,96},{1,25},{2,98},{3,27},{4,100},{5,29},{6,102},{7,31},{8,104},... | collective-permute-start | bytes 602120 | tf_op jit(solution)/shard_map/ppermute | solution.py:398
  160.7 7.4 %collective-permute-start.13 = (bf16[16,6272]{1,0:T(8,128)(2,1)}, bf16[16,6272]{1,0:T(8,128)(2,1)S(1)}, u32[]{:S(2)}, u32[]{:S(2)}) collective-permute-start(bf16[16,6272]{1,0:T(8,128)(2,1)} %get-tuple-element.38), channel_id=1, source_target_pairs={{0,64},{1,17},{2,66},{3,19},{4,68},{5,21},{6,70},{7,23},{8,72},{9,... | collective-permute-start | bytes 602120 | tf_op jit(solution)/shard_map/ppermute | solution.py:398
  169.2 26.3 %copy-start.18 = (bf16[16,4096]{1,0:T(8,128)(2,1)S(1)}, bf16[16,4096]{1,0:T(8,128)(2,1)}, u32[]{:S(2)}) copy-start(bf16[16,4096]{1,0:T(8,128)(2,1)} %get-tuple-element.41) | copy-start | bytes 393220
  195.4 10.4 %copy-start.5 = (bf16[64,16,512]{2,1,0:T(8,128)(2,1)}, bf16[64,16,512]{2,1,0:T(8,128)(2,1)S(1)}, u32[]{:S(2)}) copy-start(bf16[64,16,512]{2,1,0:T(8,128)(2,1)S(1)} %all_to_all.20) | copy-start | bytes 3145732
  195.4 21.8 %collective-permute-start.15 = (bf16[1024,512]{1,0:T(8,128)(2,1)S(1)}, bf16[1024,512]{1,0:T(8,128)(2,1)}, u32[]{:S(2)}, u32[]{:S(2)}) collective-permute-start(bf16[1024,512]{1,0:T(8,128)(2,1)S(1)} %bitcast.83), channel_id=1, source_target_pairs={{0,1},{1,0},{2,3},{3,2},{4,5},{5,4},{6,7},{7,6},{8,9},{9,8},{10,11... | collective-permute-start | bytes 3145736 | tf_op jit(solution)/shard_map/ppermute | solution.py:616
  195.5 10.3 %copy-start.12 = (bf16[64,4096]{1,0:T(8,128)(2,1)}, bf16[64,4096]{1,0:T(8,128)(2,1)S(1)}, u32[]{:S(2)}) copy-start(bf16[64,4096]{1,0:T(8,128)(2,1)S(1)} %pad_maximum_fusion.7.held) | copy-start | bytes 1572868
  195.5 10.3 %collective-permute-start.14 = (bf16[64,4096]{1,0:T(8,128)(2,1)S(1)}, bf16[64,4096]{1,0:T(8,128)(2,1)S(1)}, u32[]{:S(2)}, u32[]{:S(2)}) collective-permute-start(bf16[64,4096]{1,0:T(8,128)(2,1)S(1)} %pad_maximum_fusion.7.held), channel_id=1, source_target_pairs={{0,1},{1,0},{2,3},{3,2},{4,5},{5,4},{6,7},{7,6},{8,9},{9,8},{10,11... | collective-permute-start | bytes 1572872 | tf_op jit(solution)/shard_map/ppermute | solution.py:612
  (11 other events, 14.5 us)

commit v5 on v4

--- a/solution.py
+++ b/solution.py
@@ -596,8 +596,10 @@
     payload = pack(inverse, pooled_grad)
     back = exchange(payload, GRP_DEV)
 
+    mlp_own = mlp_piece(0)
+    cross_own = cross_piece(0)
     pieces, own, hot_part = fold_first(
-        here_of(1, core), mlp_piece(0), cross_piece(0), hot_part, mlp_came, cross_came
+        here_of(1, core), mlp_own, cross_own, hot_part, mlp_came, cross_came
     )
     came = send_on(1, pieces)
     pieces, own, hot_part = fold_second(here_of(2, core), own, hot_part, came)
@@ -607,7 +609,6 @@
     hot_part = jnp.concatenate([hot_part] + [c[:, wide:] for c in came])
     mlp_weight_grad = sums[:, :inputs]
     shared = jnp.broadcast_to(sums[None, :, inputs:].astype(BF16), (chips, 16, WIDE))
-    shared, back = lax.optimization_barrier((shared, back))
     shared = exchange(shared, CHIPS).reshape(-1, WIDE)
     hot_other = lax.ppermute(hot_part, CORE, SWAP)
     cold_grad = cold_sum(got, back, cold_table.shape[0])

time: 223 us -> 235 us (1.054)
  waiting for transfers between devices: 47.8 us -> 80.8 us
  blocking collectives: 26.2 us -> 0 us
  local copies, waits for them, and re-layouts: 18.9 us -> 22.6 us
    all_to_all x1 -> x0, blocking collectives: 26.2 us -> none  [exchange(): return lax.all_to_all(x, axes, split_axis=0, concat_axis=0, tiled=True)]
    all_to_all x3 -> x4, waiting for transfers between devices: 20.4 us -> 44.7 us  [exchange(): return lax.all_to_all(x, axes, split_axis=0, concat_axis=0, tiled=True)]
    ppermute x12, waiting for transfers between devices: 27.4 us -> 36.1 us  [send_on(): lax.ppermute(p, GRP_DEV, route_pairs(phase, s))]
    all_to_all x3 -> x4, starting transfers between devices: 23.3 us -> 26.5 us  [exchange(): return lax.all_to_all(x, axes, split_axis=0, concat_axis=0, tiled=True)]
    ppermute x12, starting transfers between devices: 16.5 us -> 13.8 us  [send_on(): lax.ppermute(p, GRP_DEV, route_pairs(phase, s))]
    unnamed x49 -> x55, local copies, waits for them, and re-layouts: 4.21 us -> 5.11 us
  transfers between devices with their start and end apart: 19 -> 20, of which waited for: 10 -> 11; matrix products, arithmetic and copies ran while one was open for 10% -> 11% of each run, Pallas kernels for 16% -> 12%
where the time goes in v5:
time: 235 us; the launch traced here: 234 us
  waiting for transfers between devices  80.8 us (34%)
  Pallas kernels  62.4 us (27%)
  starting transfers between devices  41.4 us (18%)
  local copies, waits for them, and re-layouts  22.6 us (10%)
  matrix products  18.4 us (8%)
  other arithmetic  6.73 us (3%)
    all_to_all x4, waiting for transfers between devices, exchange(): return lax.all_to_all(x, axes, split_axis=0, concat_axis=0, tiled=True)  44.7 us
    ppermute x12, waiting for transfers between devices, send_on(): lax.ppermute(p, GRP_DEV, route_pairs(phase, s))  36.1 us
    all_to_all x4, starting transfers between devices, exchange(): return lax.all_to_all(x, axes, split_axis=0, concat_axis=0, tiled=True)  26.5 us
    ppermute x12, starting transfers between devices, send_on(): lax.ppermute(p, GRP_DEV, route_pairs(phase, s))  13.8 us
    pallas_call x1, Pallas kernels, hot_sum(): pl.pallas_call(hot_kernel, out_shape=jax.ShapeDtypeStruct((hot_rows, 128)...  10.6 us
    pallas_call x1, Pallas kernels, route(): pl.pallas_call(route_kernel, out_shape=(jax.ShapeDtypeStruct((128, 128),...  9.34 us
    pallas_call x1, Pallas kernels, cold_sum(): pl.pallas_call(cold_kernel, out_shape=jax.ShapeDtypeStruct((shard_rows, 1...  8.49 us
    transpose x7, local copies, waits for them, and re-layouts, by_core(): half = parts[:, :, :, c].transpose(*ORDER[c], *rest)  7.89 us
  transfers between devices with their start and end apart: 20, of which 11 were waited for; matrix products, arithmetic and copies ran while one was open for 11% of the time, Pallas kernels for 12%

profile of v5, /device:TPU:0, one launch (start us, length us, event | category | flops | bytes accessed | tf_op | source)
XLA Modules:
  0.0 233.5 jit_solution(7589181115872649623)
XLA Ops:
  2.1 9.3 %route.1 = (s32[128,128]{1,0:T(8,128)}, s32[128,64]{1,0:T(8,128)}, s32[26,128]{1,0:T(8,128)}) custom-call(s32[26,128]{1,0:T(8,128)} %reshape.287.ids.ids_lanes, s32[1,32]{1,0:T(1,128)} %hot_list.1, s32[26,128]{1,0:T(8,128)} %reshape.287.ids.ids_lanes, s32[2048,128]{1,0:T(8,128)} %bitcast.89), custom_call_target="tpu_custom_call" | custom-call | tf_op jit(solution)/shard_map/route/pallas_call | solution.py:84
  11.4 11.2 %all-to-all-start = ((s32[128,1,128]{2,1,0:T(1,128)}), s32[128,1,128]{2,1,0:T(1,128)S(1)}, u32[]{:S(2)}, u32[]{:S(2)}) async-start(s32[128,1,128]{2,1,0:T(1,128)} %bitcast.97), calls=%async_computation | async-start | bytes 131072 | tf_op jit(solution)/shard_map/all_to_all | solution.py:376
  23.7 8.1 %all-to-all-done = s32[128,1,128]{2,1,0:T(1,128)S(1)} async-done(((s32[128,1,128]{2,1,0:T(1,128)}), s32[128,1,128]{2,1,0:T(1,128)S(1)}, u32[]{:S(2)}, u32[]{:S(2)}) %all-to-all-start) | async-done | bytes 65568 | tf_op jit(solution)/shard_map/all_to_all | solution.py:376
  32.4 7.7 %fetch.1 = bf16[5120,128]{1,0:T(8,128)(2,1)} custom-call(s32[128,128]{1,0:T(8,128)} %bitcast.90, bf16[2048,128]{1,0:T(8,128)(2,1)} %table.1), custom_call_target="tpu_custom_call" | custom-call | tf_op jit(solution)/shard_map/fetch/pallas_call | solution.py:114
  40.1 4.8 %all-to-all-start.1 = ((bf16[128,40,128]{2,1,0:T(8,128)(2,1)}), bf16[128,40,128]{2,1,0:T(8,128)(2,1)S(1)}, u32[]{:S(2)}, u32[]{:S(2)}) async-start(bf16[128,40,128]{2,1,0:T(8,128)(2,1)} %bitcast.82), calls=%async_computation.1 | async-start | bytes 2621440 | tf_op jit(solution)/shard_map/all_to_all | solution.py:376
  45.0 3.6 %slice_bitcast_fusion.1 = (bf16[4,4,4,16,1664]{4,3,0,1,2:T(8,128)(2,1)S(1)}, bf16[4,4,4,16,1664]{4,3,1,2,0:T(8,128)(2,1)S(1)}) fusion(bf16[4,4,4,2,16,1664]{5,4,3,2,1,0:T(8,128)(2,1)} %bitcast.80), kind=kLoop, calls=%fused_computation.5 | loop fusion | bytes 13631488 | tf_op jit(solution)/shard_map/transpose | solution.py:496
  48.5 2.2 copy.36
  50.7 2.1 copy.37
  54.5 12.4 %all-to-all-done.1 = bf16[128,40,128]{2,1,0:T(8,128)(2,1)S(1)} async-done(((bf16[128,40,128]{2,1,0:T(8,128)(2,1)}), bf16[128,40,128]{2,1,0:T(8,128)(2,1)S(1)}, u32[]{:S(2)}, u32[]{:S(2)}) %all-to-all-start.1) | async-done | bytes 1310752 | tf_op jit(solution)/shard_map/all_to_all | solution.py:376
  67.9 6.1 %pool.1 = bf16[128,1664]{1,0:T(8,128)(2,1)} custom-call(s32[26,128]{1,0:T(8,128)} %get-tuple-element.28.position, s32[13,128]{1,0:T(8,128)} %bitcast.98, bf16[32,128]{1,0:T(8,128)(2,1)} %gather_fusion, bf16[5120,128]{1,0:T(8,128)(2,1)} %bitcast.81), custom_call_target="tpu_custom_call" | custom-call | tf_op jit(solution)/shard_map/pool/pallas_call | solution.py:147
  77.2 4.5 %multiply_convert_fusion.1 = (bf16[128,2048]{1,0:T(8,128)(2,1)S(1)}, f32[128,2048]{1,0:T(8,128)S(1)}) fusion(f32[2048]{0:T(1024)S(1)} %pad_maximum_fusion.11, bf16[128,1664]{1,0:T(8,128)(2,1)S(1)} %get-tuple-element.61, bf16[1024,1664]{1,0:T(8,128)(2,1)} %bitcast.87, bf16[1024,1664]{1,0:T(8,128)(2,1)S(1)} %bitcast.85), kind=kOutput, calls=%fused_computation.46 | convolution fusion | flops 887619584 | bytes 8822784 | tf_op jit(solution)/shard_map/dot_general | solution.py:372
  88.2 1.9 hot_block.1.hot
  96.2 2.5 %collective-permute-start.3 = (bf16[256,1664]{1,0:T(8,128)(2,1)}, bf16[256,1664]{1,0:T(8,128)(2,1)}, u32[]{:S(2)}, u32[]{:S(2)}) collective-permute-start(bf16[256,1664]{1,0:T(8,128)(2,1)} %convolution_convert_fusion.1), channel_id=1, source_target_pairs={{0,6},{1,97},{2,0},{3,99},{4,2},{5,101},{6,4},{7,103},{8,14},{9,10... | collective-permute-start | bytes 2555912 | tf_op jit(solution)/shard_map/ppermute | solution.py:398
  102.2 2.9 %collective-permute-start.6 = (bf16[264,512]{1,0:T(8,128)(2,1)}, bf16[264,512]{1,0:T(8,128)(2,1)}, u32[]{:S(2)}, u32[]{:S(2)}) collective-permute-start(bf16[264,512]{1,0:T(8,128)(2,1)} %get-tuple-element.59), channel_id=1, source_target_pairs={{0,6},{1,97},{2,0},{3,99},{4,2},{5,101},{6,4},{7,103},{8,14},{9,10... | collective-permute-start | bytes 811016 | tf_op jit(solution)/shard_map/ppermute | solution.py:398
  105.1 15.5 %collective-permute-done.5.refs_3_ = bf16[264,512]{1,0:T(8,128)(2,1)} collective-permute-done((bf16[264,512]{1,0:T(8,128)(2,1)}, bf16[264,512]{1,0:T(8,128)(2,1)}, u32[]{:S(2)}, u32[]{:S(2)}) %collective-permute-start.5) | collective-permute-done | bytes 270368 | tf_op jit(solution)/shard_map/ppermute | solution.py:398
  124.1 4.8 %collective-permute-done.7.refs_5_ = bf16[264,512]{1,0:T(8,128)(2,1)} collective-permute-done((bf16[264,512]{1,0:T(8,128)(2,1)}, bf16[264,512]{1,0:T(8,128)(2,1)}, u32[]{:S(2)}, u32[]{:S(2)}) %collective-permute-start.7) | collective-permute-done | bytes 270368 | tf_op jit(solution)/shard_map/ppermute | solution.py:398
  128.9 4.5 %fold_first.1 = (bf16[64,2432]{1,0:T(8,128)(2,1)}, bf16[64,2432]{1,0:T(8,128)(2,1)}, bf16[64,2432]{1,0:T(8,128)(2,1)}, f32[64,2176]{1,0:T(8,128)}, bf16[64,256]{1,0:T(8,128)(2,1)}) custom-call(s32[1]{0:T(128)} %bitcast.25.here, f32[256,1664]{1,0:T(8,128)} %fusion.26.mlp, f32[256,512]{1,0:T(8,128)} %convolution_add_fusion.5.cross, ...), custom_call_target="tpu_custom_call" | custom-call | tf_op jit(solution)/shard_map/fold_first/pallas_call | solution.py:442
  134.6 2.2 collective-permute-start.9
  136.7 5.4 %collective-permute-done.10.refs_2_ = bf16[64,2432]{1,0:T(8,128)(2,1)S(1)} collective-permute-done((bf16[64,2432]{1,0:T(8,128)(2,1)}, bf16[64,2432]{1,0:T(8,128)(2,1)S(1)}, u32[]{:S(2)}, u32[]{:S(2)}) %collective-permute-start.10) | collective-permute-done | bytes 311328 | tf_op jit(solution)/shard_map/ppermute | solution.py:398
  142.1 3.0 %collective-permute-done.8.refs_0_ = bf16[64,2432]{1,0:T(8,128)(2,1)S(1)} collective-permute-done((bf16[64,2432]{1,0:T(8,128)(2,1)}, bf16[64,2432]{1,0:T(8,128)(2,1)S(1)}, u32[]{:S(2)}, u32[]{:S(2)}) %collective-permute-start.8) | collective-permute-done | bytes 311328 | tf_op jit(solution)/shard_map/ppermute | solution.py:398
  146.0 2.5 %fold_second.1 = (bf16[16,6272]{1,0:T(8,128)(2,1)}, bf16[16,6272]{1,0:T(8,128)(2,1)}, bf16[16,6272]{1,0:T(8,128)(2,1)}, f32[16,2176]{1,0:T(8,128)}, bf16[16,4096]{1,0:T(8,128)(2,1)}) custom-call(s32[1]{0:T(128)} %bitcast.24.here, f32[64,2176]{1,0:T(8,128)} %get-tuple-element.29.own_in, bf16[64,256]{1,0:T(8,128)(2,1)} %get-tuple-element.30.hot, ...), custom_call_target="tpu_custom_call" | custom-call | tf_op jit(solution)/shard_map/fold_second/pallas_call | solution.py:479
  148.9 2.8 %collective-permute-start.12 = (bf16[16,6272]{1,0:T(8,128)(2,1)}, bf16[16,6272]{1,0:T(8,128)(2,1)S(1)}, u32[]{:S(2)}, u32[]{:S(2)}) collective-permute-start(bf16[16,6272]{1,0:T(8,128)(2,1)} %get-tuple-element.36), channel_id=1, source_target_pairs={{0,96},{1,25},{2,98},{3,27},{4,100},{5,29},{6,102},{7,31},{8,104},... | collective-permute-start | bytes 602120 | tf_op jit(solution)/shard_map/ppermute | solution.py:398
  151.7 3.9 %collective-permute-done.11 = bf16[16,6272]{1,0:T(8,128)(2,1)S(1)} collective-permute-done((bf16[16,6272]{1,0:T(8,128)(2,1)}, bf16[16,6272]{1,0:T(8,128)(2,1)S(1)}, u32[]{:S(2)}, u32[]{:S(2)}) %collective-permute-start.11) | collective-permute-done | bytes 200736 | tf_op jit(solution)/shard_map/ppermute | solution.py:398
  155.6 1.8 collective-permute-done.12
  161.9 5.9 %all-to-all-start.3 = ((bf16[64,16,512]{2,1,0:T(8,128)(2,1)}), bf16[64,16,512]{2,1,0:T(8,128)(2,1)S(1)}, u32[]{:S(2)}, u32[]{:S(2)}) async-start(bf16[64,16,512]{2,1,0:T(8,128)(2,1)} %broadcast_in_dim.36), calls=%async_computation.3 | async-start | bytes 2097152 | tf_op jit(solution)/shard_map/all_to_all | solution.py:376
  167.8 7.7 %pack.1 = bf16[128,40,128]{2,1,0:T(8,128)(2,1)} custom-call(s32[128,64]{1,0:T(8,128)} %get-tuple-element.27.inverse, bf16[128,1664]{1,0:T(8,128)(2,1)} %fusion.3.grad), custom_call_target="tpu_custom_call" | custom-call | tf_op jit(solution)/shard_map/pack/pallas_call | solution.py:175
  175.5 7.0 %all-to-all-done.3 = bf16[64,16,512]{2,1,0:T(8,128)(2,1)S(1)} async-done(((bf16[64,16,512]{2,1,0:T(8,128)(2,1)}), bf16[64,16,512]{2,1,0:T(8,128)(2,1)S(1)}, u32[]{:S(2)}, u32[]{:S(2)}) %all-to-all-start.3) | async-done | bytes 1048608 | tf_op jit(solution)/shard_map/all_to_all | solution.py:376
  182.5 4.6 %all-to-all-start.2 = ((bf16[128,40,128]{2,1,0:T(8,128)(2,1)}), bf16[128,40,128]{2,1,0:T(8,128)(2,1)S(1)}, u32[]{:S(2)}, u32[]{:S(2)}) async-start(bf16[128,40,128]{2,1,0:T(8,128)(2,1)} %pack.1), calls=%async_computation.2 | async-start | bytes 2621440 | tf_op jit(solution)/shard_map/all_to_all | solution.py:376
  191.9 17.2 %all-to-all-done.2.came = bf16[128,40,128]{2,1,0:T(8,128)(2,1)S(1)} async-done(((bf16[128,40,128]{2,1,0:T(8,128)(2,1)}), bf16[128,40,128]{2,1,0:T(8,128)(2,1)S(1)}, u32[]{:S(2)}, u32[]{:S(2)}) %all-to-all-start.2) | async-done | bytes 1310752 | tf_op jit(solution)/shard_map/all_to_all | solution.py:376
  210.1 8.5 %cold_sum.1 = f32[2048,128]{1,0:T(8,128)} custom-call(s32[128,128]{1,0:T(8,128)} %bitcast.91, bf16[128,40,128]{2,1,0:T(8,128)(2,1)} %copy-done.5), custom_call_target="tpu_custom_call" | custom-call | tf_op jit(solution)/shard_map/cold_sum/pallas_call | solution.py:233
  219.3 10.6 %hot_sum.1 = f32[4096,128]{1,0:T(8,128)} custom-call(s32[2,64]{1,0:T(2,128)} %pad_add_fusion.owners, s32[128,128]{1,0:T(8,128)} %bitcast.92, bf16[64,4096]{1,0:T(8,128)(2,1)} %pad_maximum_fusion.7.held, bf16[64,4096]{1,0:T(8,128)(2,1)} %collective-permute-done.14.came), custom_call_target="tpu_custom_call" | custom-call | tf_op jit(solution)/shard_map/hot_sum/pallas_call | solution.py:270
  229.9 3.7 %unpack.1 = (f32[1664,256]{1,0:T(8,128)}, f32[256,1664]{1,0:T(8,128)}, f32[13,128]{1,0:T(8,128)}, f32[16,128]{1,0:T(8,128)}, f32[16,128]{1,0:T(8,128)}) custom-call(s32[1]{0:T(128)} %bitcast.29.core, bf16[1024,512]{1,0:T(8,128)(2,1)} %bitcast.84, bf16[1024,512]{1,0:T(8,128)(2,1)} %collective-permute-done.15.came), custom_call_target="tpu_custom_call" | custom-call | tf_op jit(solution)/shard_map/unpack/pallas_call | solution.py:346
  (134 shorter events, 41.6 us)
Async XLA Ops:
  0.6 52.6 %copy-start = (bf16[4096,128]{1,0:T(8,128)(2,1)S(1)}, bf16[4096,128]{1,0:T(8,128)(2,1)}, u32[]{:S(2)}) copy-start(bf16[4096,128]{1,0:T(8,128)(2,1)} %param.18) | copy-start | bytes 3145732
  11.4 20.4 %all-to-all-start = ((s32[128,1,128]{2,1,0:T(1,128)}), s32[128,1,128]{2,1,0:T(1,128)S(1)}, u32[]{:S(2)}, u32[]{:S(2)}) async-start(s32[128,1,128]{2,1,0:T(1,128)} %bitcast.97), calls=%async_computation | async-start | bytes 131072 | tf_op jit(solution)/shard_map/all_to_all | solution.py:376
  40.1 26.8 %all-to-all-start.1 = ((bf16[128,40,128]{2,1,0:T(8,128)(2,1)}), bf16[128,40,128]{2,1,0:T(8,128)(2,1)S(1)}, u32[]{:S(2)}, u32[]{:S(2)}) async-start(bf16[128,40,128]{2,1,0:T(8,128)(2,1)} %bitcast.82), calls=%async_computation.1 | async-start | bytes 2621440 | tf_op jit(solution)/shard_map/all_to_all | solution.py:376
  53.0 22.8 %copy-start.9 = (bf16[256,1664]{1,0:T(8,128)(2,1)S(1)}, bf16[256,1664]{1,0:T(8,128)(2,1)}, u32[]{:S(2)}) copy-start(bf16[256,1664]{1,0:T(8,128)(2,1)} %param.21) | copy-start | bytes 2555908
  53.0 22.8 %copy-start.23 = (f32[1664]{0:T(1024)S(1)}, f32[1664]{0:T(1024)}, u32[]{:S(2)}) copy-start(f32[1664]{0:T(1024)} %param.22) | copy-start | bytes 19972
  74.1 3.1 %copy-start.7 = (bf16[4,4,4,16,1664]{4,3,2,1,0:T(8,128)(2,1)S(1)}, bf16[4,4,4,16,1664]{4,3,2,1,0:T(8,128)(2,1)}, u32[]{:S(2)}) copy-start(bf16[4,4,4,16,1664]{4,3,2,1,0:T(8,128)(2,1)} %copy.36) | copy-start | bytes 10223620
  77.2 4.6 %copy-start.26 = (s32[128]{0:T(128)S(1)}, s32[128]{0:T(128)}, u32[]{:S(2)}) copy-start(s32[128]{0:T(128)} %param.19) | copy-start | bytes 1540
  77.2 5.3 %copy-start.8 = (bf16[4,4,4,16,1664]{4,3,2,1,0:T(8,128)(2,1)S(1)}, bf16[4,4,4,16,1664]{4,3,2,1,0:T(8,128)(2,1)}, u32[]{:S(2)}) copy-start(bf16[4,4,4,16,1664]{4,3,2,1,0:T(8,128)(2,1)} %copy.37) | copy-start | bytes 10223620
  85.6 4.8 %collective-permute-start.1 = (bf16[128,2304]{1,0:T(8,128)(2,1)}, bf16[128,2304]{1,0:T(8,128)(2,1)S(1)}, u32[]{:S(2)}, u32[]{:S(2)}) collective-permute-start(bf16[128,2304]{1,0:T(8,128)(2,1)} %get-tuple-element.50), channel_id=1, source_target_pairs={{0,1},{1,0},{2,3},{3,2},{4,5},{5,4},{6,7},{7,6},{8,9},{9,8},{10,11... | collective-permute-start | bytes 1769480 | tf_op jit(solution)/shard_map/ppermute | solution.py:577
  86.5 4.2 %collective-permute-start = (bf16[128,2688]{1,0:T(8,128)(2,1)}, bf16[128,2688]{1,0:T(8,128)(2,1)}, u32[]{:S(2)}, u32[]{:S(2)}) collective-permute-start(bf16[128,2688]{1,0:T(8,128)(2,1)} %pad_maximum_fusion.6), channel_id=1, source_target_pairs={{0,1},{1,0},{2,3},{3,2},{4,5},{5,4},{6,7},{7,6},{8,9},{9,8},{10,11... | collective-permute-start | bytes 2064392 | tf_op jit(solution)/shard_map/ppermute | solution.py:553
  92.7 7.8 %copy-start.2 = (bf16[128,1024]{1,0:T(8,128)(2,1)}, bf16[128,1024]{1,0:T(8,128)(2,1)S(1)}, u32[]{:S(2)}) copy-start(bf16[128,1024]{1,0:T(8,128)(2,1)S(1)} %slice.80) | copy-start | bytes 786436
  94.1 34.8 %collective-permute-start.4 = (bf16[256,1664]{1,0:T(8,128)(2,1)}, bf16[256,1664]{1,0:T(8,128)(2,1)}, u32[]{:S(2)}, u32[]{:S(2)}) collective-permute-start(bf16[256,1664]{1,0:T(8,128)(2,1)} %convolution_convert_fusion), channel_id=1, source_target_pairs={{0,4},{1,65},{2,6},{3,67},{4,0},{5,69},{6,2},{7,71},{8,12},{9,73},... | collective-permute-start | bytes 2555912 | tf_op jit(solution)/shard_map/ppermute | solution.py:398
  96.2 32.7 %collective-permute-start.3 = (bf16[256,1664]{1,0:T(8,128)(2,1)}, bf16[256,1664]{1,0:T(8,128)(2,1)}, u32[]{:S(2)}, u32[]{:S(2)}) collective-permute-start(bf16[256,1664]{1,0:T(8,128)(2,1)} %convolution_convert_fusion.1), channel_id=1, source_target_pairs={{0,6},{1,97},{2,0},{3,99},{4,2},{5,101},{6,4},{7,103},{8,14},{9,10... | collective-permute-start | bytes 2555912 | tf_op jit(solution)/shard_map/ppermute | solution.py:398
  100.0 28.9 %collective-permute-start.2 = (bf16[256,1664]{1,0:T(8,128)(2,1)}, bf16[256,1664]{1,0:T(8,128)(2,1)}, u32[]{:S(2)}, u32[]{:S(2)}) collective-permute-start(bf16[256,1664]{1,0:T(8,128)(2,1)} %convolution_convert_fusion.2), channel_id=1, source_target_pairs={{0,2},{1,33},{2,4},{3,35},{4,6},{5,37},{6,0},{7,39},{8,10},{9,41},... | collective-permute-start | bytes 2555912 | tf_op jit(solution)/shard_map/ppermute | solution.py:398
  101.9 18.7 %collective-permute-start.5 = (bf16[264,512]{1,0:T(8,128)(2,1)}, bf16[264,512]{1,0:T(8,128)(2,1)}, u32[]{:S(2)}, u32[]{:S(2)}) collective-permute-start(bf16[264,512]{1,0:T(8,128)(2,1)} %get-tuple-element.60), channel_id=1, source_target_pairs={{0,2},{1,33},{2,4},{3,35},{4,6},{5,37},{6,0},{7,39},{8,10},{9,41},... | collective-permute-start | bytes 811016 | tf_op jit(solution)/shard_map/ppermute | solution.py:398
  102.2 20.3 %copy-start.3 = (bf16[128,1024]{1,0:T(8,128)(2,1)S(1)}, bf16[128,1024]{1,0:T(8,128)(2,1)}, u32[]{:S(2)}) copy-start(bf16[128,1024]{1,0:T(8,128)(2,1)} %copy-done.2) | copy-start | bytes 786436
  102.2 21.9 %collective-permute-start.6 = (bf16[264,512]{1,0:T(8,128)(2,1)}, bf16[264,512]{1,0:T(8,128)(2,1)}, u32[]{:S(2)}, u32[]{:S(2)}) collective-permute-start(bf16[264,512]{1,0:T(8,128)(2,1)} %get-tuple-element.59), channel_id=1, source_target_pairs={{0,6},{1,97},{2,0},{3,99},{4,2},{5,101},{6,4},{7,103},{8,14},{9,10... | collective-permute-start | bytes 811016 | tf_op jit(solution)/shard_map/ppermute | solution.py:398
  120.6 8.3 %collective-permute-start.7 = (bf16[264,512]{1,0:T(8,128)(2,1)}, bf16[264,512]{1,0:T(8,128)(2,1)}, u32[]{:S(2)}, u32[]{:S(2)}) collective-permute-start(bf16[264,512]{1,0:T(8,128)(2,1)} %get-tuple-element.58), channel_id=1, source_target_pairs={{0,4},{1,65},{2,6},{3,67},{4,0},{5,69},{6,2},{7,71},{8,12},{9,73},... | collective-permute-start | bytes 811016 | tf_op jit(solution)/shard_map/ppermute | solution.py:398
  133.4 8.7 %collective-permute-start.10 = (bf16[64,2432]{1,0:T(8,128)(2,1)}, bf16[64,2432]{1,0:T(8,128)(2,1)S(1)}, u32[]{:S(2)}, u32[]{:S(2)}) collective-permute-start(bf16[64,2432]{1,0:T(8,128)(2,1)} %get-tuple-element.33), channel_id=1, source_target_pairs={{0,16},{1,5},{2,18},{3,7},{4,20},{5,1},{6,22},{7,3},{8,24},{9,13},... | collective-permute-start | bytes 933896 | tf_op jit(solution)/shard_map/ppermute | solution.py:398
  133.4 11.7 %collective-permute-start.8 = (bf16[64,2432]{1,0:T(8,128)(2,1)}, bf16[64,2432]{1,0:T(8,128)(2,1)S(1)}, u32[]{:S(2)}, u32[]{:S(2)}) collective-permute-start(bf16[64,2432]{1,0:T(8,128)(2,1)} %get-tuple-element.31), channel_id=1, source_target_pairs={{0,8},{1,3},{2,10},{3,5},{4,12},{5,7},{6,14},{7,1},{8,16},{9,11},{... | collective-permute-start | bytes 933896 | tf_op jit(solution)/shard_map/ppermute | solution.py:398
  134.6 10.6 %collective-permute-start.9 = (bf16[64,2432]{1,0:T(8,128)(2,1)}, bf16[64,2432]{1,0:T(8,128)(2,1)S(1)}, u32[]{:S(2)}, u32[]{:S(2)}) collective-permute-start(bf16[64,2432]{1,0:T(8,128)(2,1)} %get-tuple-element.32), channel_id=1, source_target_pairs={{0,24},{1,7},{2,26},{3,1},{4,28},{5,3},{6,30},{7,5},{8,0},{9,15},{... | collective-permute-start | bytes 933896 | tf_op jit(solution)/shard_map/ppermute | solution.py:398
  148.4 7.1 %collective-permute-start.11 = (bf16[16,6272]{1,0:T(8,128)(2,1)}, bf16[16,6272]{1,0:T(8,128)(2,1)S(1)}, u32[]{:S(2)}, u32[]{:S(2)}) collective-permute-start(bf16[16,6272]{1,0:T(8,128)(2,1)} %get-tuple-element.35), channel_id=1, source_target_pairs={{0,32},{1,9},{2,34},{3,11},{4,36},{5,13},{6,38},{7,15},{8,40},{9,1... | collective-permute-start | bytes 602120 | tf_op jit(solution)/shard_map/ppermute | solution.py:398
  148.9 8.5 %collective-permute-start.12 = (bf16[16,6272]{1,0:T(8,128)(2,1)}, bf16[16,6272]{1,0:T(8,128)(2,1)S(1)}, u32[]{:S(2)}, u32[]{:S(2)}) collective-permute-start(bf16[16,6272]{1,0:T(8,128)(2,1)} %get-tuple-element.36), channel_id=1, source_target_pairs={{0,96},{1,25},{2,98},{3,27},{4,100},{5,29},{6,102},{7,31},{8,104},... | collective-permute-start | bytes 602120 | tf_op jit(solution)/shard_map/ppermute | solution.py:398
  151.7 7.4 %collective-permute-start.13 = (bf16[16,6272]{1,0:T(8,128)(2,1)}, bf16[16,6272]{1,0:T(8,128)(2,1)S(1)}, u32[]{:S(2)}, u32[]{:S(2)}) collective-permute-start(bf16[16,6272]{1,0:T(8,128)(2,1)} %get-tuple-element.37), channel_id=1, source_target_pairs={{0,64},{1,17},{2,66},{3,19},{4,68},{5,21},{6,70},{7,23},{8,72},{9,... | collective-permute-start | bytes 602120 | tf_op jit(solution)/shard_map/ppermute | solution.py:398
  155.6 3.5 %copy-start.14 = (bf16[16,6272]{1,0:T(8,128)(2,1)}, bf16[16,6272]{1,0:T(8,128)(2,1)S(1)}, u32[]{:S(2)}) copy-start(bf16[16,6272]{1,0:T(8,128)(2,1)S(1)} %collective-permute-done.11) | copy-start | bytes 602116
  161.9 20.6 %all-to-all-start.3 = ((bf16[64,16,512]{2,1,0:T(8,128)(2,1)}), bf16[64,16,512]{2,1,0:T(8,128)(2,1)S(1)}, u32[]{:S(2)}, u32[]{:S(2)}) async-start(bf16[64,16,512]{2,1,0:T(8,128)(2,1)} %broadcast_in_dim.36), calls=%async_computation.3 | async-start | bytes 2097152 | tf_op jit(solution)/shard_map/all_to_all | solution.py:376
  175.5 13.6 %slice-start = ((bf16[16,6272]{1,0:T(8,128)(2,1)}), bf16[16,4096]{1,0:T(8,128)(2,1)S(1)}, s32[]{:S(2)}) async-start(bf16[16,6272]{1,0:T(8,128)(2,1)} %copy-done.14), calls=%async_computation.4 | async-start | bytes 262144 | tf_op jit(solution)/shard_map/slice | solution.py:609
  182.5 6.6 %copy-start.6 = (bf16[64,16,512]{2,1,0:T(8,128)(2,1)}, bf16[64,16,512]{2,1,0:T(8,128)(2,1)S(1)}, u32[]{:S(2)}) copy-start(bf16[64,16,512]{2,1,0:T(8,128)(2,1)S(1)} %all-to-all-done.3) | copy-start | bytes 3145732
  182.5 26.6 %all-to-all-start.2 = ((bf16[128,40,128]{2,1,0:T(8,128)(2,1)}), bf16[128,40,128]{2,1,0:T(8,128)(2,1)S(1)}, u32[]{:S(2)}, u32[]{:S(2)}) async-start(bf16[128,40,128]{2,1,0:T(8,128)(2,1)} %pack.1), calls=%async_computation.2 | async-start | bytes 2621440 | tf_op jit(solution)/shard_map/all_to_all | solution.py:376
  187.2 42.7 %collective-permute-start.15 = (bf16[1024,512]{1,0:T(8,128)(2,1)S(1)}, bf16[1024,512]{1,0:T(8,128)(2,1)}, u32[]{:S(2)}, u32[]{:S(2)}) collective-permute-start(bf16[1024,512]{1,0:T(8,128)(2,1)S(1)} %bitcast.83), channel_id=1, source_target_pairs={{0,1},{1,0},{2,3},{3,2},{4,5},{5,4},{6,7},{7,6},{8,9},{9,8},{10,11... | collective-permute-start | bytes 3145736 | tf_op jit(solution)/shard_map/ppermute | solution.py:617
  190.8 27.8 %copy-start.16 = (f32[16,2176]{1,0:T(8,128)S(1)}, f32[16,2176]{1,0:T(8,128)}, u32[]{:S(2)}) copy-start(f32[16,2176]{1,0:T(8,128)} %copy-done.15) | copy-start | bytes 417796
  190.8 28.5 %collective-permute-start.14 = (bf16[64,4096]{1,0:T(8,128)(2,1)}, bf16[64,4096]{1,0:T(8,128)(2,1)}, u32[]{:S(2)}, u32[]{:S(2)}) collective-permute-start(bf16[64,4096]{1,0:T(8,128)(2,1)} %pad_maximum_fusion.7.held), channel_id=1, source_target_pairs={{0,1},{1,0},{2,3},{3,2},{4,5},{5,4},{6,7},{7,6},{8,9},{9,8},{10,11... | collective-permute-start | bytes 1572872 | tf_op jit(solution)/shard_map/ppermute | solution.py:613
  (16 other events, 25.2 us)

commit v6 on v5

--- a/solution.py
+++ b/solution.py
@@ -124,34 +124,52 @@
     )(wanted, table)
 
 
-def pool_kernel(position, hot_index, hot_rows, arrived, out, wide, total):
+def hot_spread_kernel(hot_index, hot_rows, out):
     features, samples = hot_index.shape
+    slots = lax.broadcasted_iota(I32, (HOT, samples), 0)
+    for f in range(features):
+        picked = (slots == hot_index[f : f + 1, :]).astype(F32).astype(BF16)
+        out[f * samples : (f + 1) * samples, :] = contract_rows(picked, hot_rows[...])
+
+
+def hot_spread(hot_index, hot_rows):
+    return pl.pallas_call(
+        hot_spread_kernel,
+        out_shape=jax.ShapeDtypeStruct((hot_index.size, 128), F32),
+        in_specs=[VMEM, VMEM],
+        out_specs=VMEM,
+        name="hot_spread",
+    )(hot_index, hot_rows)
+
+
+def pool_kernel(position, hot_part, arrived, out, wide, total):
+    samples = total.shape[0]
+    features = hot_part.shape[0] // samples
     wide[...] = arrived[...].astype(F32)
-    slots = lax.broadcasted_iota(I32, (HOT, samples), 0)
 
     def feature(f, carried):
         for s in range(samples):
             total[s : s + 1, :] = (
                 wide[pl.ds(position[f, s], 1), :] + wide[pl.ds(position[features + f, s], 1), :]
             )
-        picked = (slots == hot_index[pl.ds(f, 1), :]).astype(F32).astype(BF16)
-        both = total[...] + contract_rows(picked, hot_rows[...])
+        at = pl.multiple_of(f * samples, samples)
+        both = total[...] + hot_part[pl.ds(at, samples), :]
         out[:, pl.ds(pl.multiple_of(f * 128, 128), 128)] = both.astype(BF16)
         return carried
 
     lax.fori_loop(0, features, feature, 0)
 
 
-def pool(position, hot_index, hot_rows, arrived):
-    features, samples = hot_index.shape
+def pool(position, hot_part, arrived):
+    samples = position.shape[1]
     return pl.pallas_call(
         pool_kernel,
-        out_shape=jax.ShapeDtypeStruct((samples, features * 128), BF16),
-        in_specs=[SMEM, VMEM, VMEM, VMEM],
+        out_shape=jax.ShapeDtypeStruct((samples, hot_part.shape[0] // samples * 128), BF16),
+        in_specs=[SMEM, VMEM, VMEM],
         out_specs=VMEM,
         scratch_shapes=[pltpu.VMEM(arrived.shape, F32), pltpu.VMEM((samples, 128), F32)],
         name="pool",
-    )(position, hot_index, hot_rows, arrived)
+    )(position, hot_part, arrived)
 
 
 def pack_kernel(inverse, grad, out, wide, picked):
@@ -188,12 +206,12 @@
 def hot_block_kernel(hot_index, grad, out):
     features, samples = hot_index.shape
     slots = lax.broadcasted_iota(I32, (HOT, samples), 0)
-    total = jnp.zeros((HOT, 128), F32)
-    for f in range(features):
-        one_hot = (slots == hot_index[f : f + 1, :]).astype(F32).astype(BF16)
-        part = grad[:, f * 128 : (f + 1) * 128]
-        total = total + jnp.dot(one_hot, part, preferred_element_type=F32)
-    total = total.astype(BF16)
+    one_hot = jnp.concatenate(
+        [(slots == hot_index[f : f + 1, :]).astype(F32).astype(BF16) for f in range(features)],
+        axis=1,
+    )
+    rows = jnp.concatenate([grad[:, f * 128 : (f + 1) * 128] for f in range(features)])
+    total = jnp.dot(one_hot, rows, preferred_element_type=F32).astype(BF16)
     for b in range(HOT // 8):
         out[:, b * 128 : (b + 1) * 128] = total[b * 8 : (b + 1) * 8, :]
 
@@ -525,14 +543,15 @@
     send, inverse, position = route(ids_rows, hot_list, location.reshape(-1, 128))
     got = exchange(send.reshape(devices, 1, 128), GRP_DEV).reshape(devices, 128)
     rows = fetch(got, cold_table)
-    arrived = exchange(rows.reshape(devices, CAP, width), GRP_DEV).reshape(devices * CAP, width)
+    arrived = exchange(rows.reshape(devices, CAP, width), GRP_DEV)
+    arrived = arrived.reshape(devices * CAP, width)
 
     mlp_weight = by_core(mlp_weight)
     mlp_bias = by_core(mlp_bias)
     out_weight = by_core(out_weight)
     hot_rows = hot_table[hot_list[0]]
     hot_index = hot_index.T
-    first_input = pool(position, hot_index, hot_rows, arrived)
+    first_input = pool(position, hot_spread(hot_index, hot_rows), arrived)
     cross_low = jnp.dot(first_input, cross_u, preferred_element_type=F32).astype(BF16)
     cross_term = jnp.dot(cross_low, cross_v, preferred_element_type=F32) + cross_bias
     input_wide = first_input.astype(F32)
@@ -541,7 +560,7 @@
     hidden = jax.nn.silu(hidden_in).astype(BF16)
     logits = jnp.dot(hidden, out_weight, preferred_element_type=F32)
     logit_grad = jax.nn.sigmoid(logits) - labels.astype(F32)
-    out_grad = jnp.dot(logit_grad, hidden.astype(F32), precision=lax.Precision.HIGHEST)
+    out_grad = jnp.sum(logit_grad[:, None] * hidden.astype(F32), axis=0)
     hidden_grad = (
         logit_grad[:, None] * out_weight.astype(F32)[None, :] * silu_slope(hidden_in)
     ).astype(BF16)

time: 235 us -> 237 us (level)
  matrix products: 18.4 us -> 21.5 us
    pallas_call x1 -> x2, Pallas kernels: 6.13 us -> 7.31 us  [the longest x1 5.39 us: pool(): pl.pallas_call(pool_kernel, out_shape=jax.ShapeDtypeStruct((samples, hot_...]
    unnamed x55 -> x49, local copies, waits for them, and re-layouts: 5.11 us -> 4.84 us
  transfers between devices with their start and end apart: 20 -> 20, of which waited for: 11 -> 11; matrix products, arithmetic and copies ran while one was open for 11% -> 11% of each run, Pallas kernels for 12% -> 13%
where the time goes in v6:
time: 237 us; the launch traced here: 236 us
  waiting for transfers between devices  79 us (33%)
  Pallas kernels  63.6 us (27%)
  starting transfers between devices  41.3 us (17%)
  local copies, waits for them, and re-layouts  22.4 us (9%)
  matrix products  21.5 us (9%)
  other arithmetic  6.79 us (3%)
    all_to_all x4, waiting for transfers between devices, exchange(): return lax.all_to_all(x, axes, split_axis=0, concat_axis=0, tiled=True)  42.9 us
    ppermute x12, waiting for transfers between devices, send_on(): lax.ppermute(p, GRP_DEV, route_pairs(phase, s))  36.2 us
    all_to_all x4, starting transfers between devices, exchange(): return lax.all_to_all(x, axes, split_axis=0, concat_axis=0, tiled=True)  26.5 us
    ppermute x12, starting transfers between devices, send_on(): lax.ppermute(p, GRP_DEV, route_pairs(phase, s))  13.8 us
    pallas_call x1, Pallas kernels, hot_sum(): pl.pallas_call(hot_kernel, out_shape=jax.ShapeDtypeStruct((hot_rows, 128)...  10.6 us
    pallas_call x1, Pallas kernels, route(): pl.pallas_call(route_kernel, out_shape=(jax.ShapeDtypeStruct((128, 128),...  9.34 us
    pallas_call x1, Pallas kernels, cold_sum(): pl.pallas_call(cold_kernel, out_shape=jax.ShapeDtypeStruct((shard_rows, 1...  8.49 us
    transpose x7, local copies, waits for them, and re-layouts, by_core(): half = parts[:, :, :, c].transpose(*ORDER[c], *rest)  7.9 us
  transfers between devices with their start and end apart: 20, of which 11 were waited for; matrix products, arithmetic and copies ran while one was open for 11% of the time, Pallas kernels for 13%

profile of v6, /device:TPU:0, one launch (start us, length us, event | category | flops | bytes accessed | tf_op | source)
XLA Modules:
  0.0 235.6 jit_solution(804393784503438227)
XLA Ops:
  2.1 9.3 %route.1 = (s32[128,128]{1,0:T(8,128)}, s32[128,64]{1,0:T(8,128)}, s32[26,128]{1,0:T(8,128)}) custom-call(s32[26,128]{1,0:T(8,128)} %reshape.287.ids.ids_lanes, s32[1,32]{1,0:T(1,128)} %hot_list.1, s32[26,128]{1,0:T(8,128)} %reshape.287.ids.ids_lanes, s32[2048,128]{1,0:T(8,128)} %bitcast.84), custom_call_target="tpu_custom_call" | custom-call | tf_op jit(solution)/shard_map/route/pallas_call | solution.py:84
  11.4 11.2 %all-to-all-start = ((s32[128,1,128]{2,1,0:T(1,128)}), s32[128,1,128]{2,1,0:T(1,128)S(1)}, u32[]{:S(2)}, u32[]{:S(2)}) async-start(s32[128,1,128]{2,1,0:T(1,128)} %bitcast.92), calls=%async_computation | async-start | bytes 131072 | tf_op jit(solution)/shard_map/all_to_all | solution.py:394
  23.7 8.1 %all-to-all-done = s32[128,1,128]{2,1,0:T(1,128)S(1)} async-done(((s32[128,1,128]{2,1,0:T(1,128)}), s32[128,1,128]{2,1,0:T(1,128)S(1)}, u32[]{:S(2)}, u32[]{:S(2)}) %all-to-all-start) | async-done | bytes 65568 | tf_op jit(solution)/shard_map/all_to_all | solution.py:394
  32.4 7.7 %fetch.1 = bf16[5120,128]{1,0:T(8,128)(2,1)} custom-call(s32[128,128]{1,0:T(8,128)} %bitcast.85, bf16[2048,128]{1,0:T(8,128)(2,1)} %table.1), custom_call_target="tpu_custom_call" | custom-call | tf_op jit(solution)/shard_map/fetch/pallas_call | solution.py:114
  40.1 4.8 %all-to-all-start.1 = ((bf16[128,40,128]{2,1,0:T(8,128)(2,1)}), bf16[128,40,128]{2,1,0:T(8,128)(2,1)S(1)}, u32[]{:S(2)}, u32[]{:S(2)}) async-start(bf16[128,40,128]{2,1,0:T(8,128)(2,1)} %bitcast.77), calls=%async_computation.1 | async-start | bytes 2621440 | tf_op jit(solution)/shard_map/all_to_all | solution.py:394
  45.0 3.6 %slice_bitcast_fusion.1 = (bf16[4,4,4,16,1664]{4,3,0,1,2:T(8,128)(2,1)S(1)}, bf16[4,4,4,16,1664]{4,3,1,2,0:T(8,128)(2,1)S(1)}) fusion(bf16[4,4,4,2,16,1664]{5,4,3,2,1,0:T(8,128)(2,1)} %bitcast.75), kind=kLoop, calls=%fused_computation.5 | loop fusion | bytes 13631488 | tf_op jit(solution)/shard_map/transpose | solution.py:514
  48.5 2.2 copy.36
  50.7 2.1 copy.37
  56.4 10.5 %all-to-all-done.1 = bf16[128,40,128]{2,1,0:T(8,128)(2,1)S(1)} async-done(((bf16[128,40,128]{2,1,0:T(8,128)(2,1)}), bf16[128,40,128]{2,1,0:T(8,128)(2,1)S(1)}, u32[]{:S(2)}, u32[]{:S(2)}) %all-to-all-start.1) | async-done | bytes 1310752 | tf_op jit(solution)/shard_map/all_to_all | solution.py:394
  68.0 5.4 %pool.1 = bf16[128,1664]{1,0:T(8,128)(2,1)} custom-call(s32[26,128]{1,0:T(8,128)} %get-tuple-element.28.position, f32[1664,128]{1,0:T(8,128)} %hot_spread.1.hot_part, bf16[5120,128]{1,0:T(8,128)(2,1)} %bitcast.76), custom_call_target="tpu_custom_call" | custom-call | tf_op jit(solution)/shard_map/pool/pallas_call | solution.py:165
  75.1 2.2 fusion.13
  77.3 4.5 %multiply_convert_fusion.1 = (bf16[128,2048]{1,0:T(8,128)(2,1)S(1)}, f32[128,2048]{1,0:T(8,128)S(1)}) fusion(f32[2048]{0:T(1024)S(1)} %pad_maximum_fusion.11, bf16[128,1664]{1,0:T(8,128)(2,1)S(1)} %get-tuple-element.62, bf16[1024,1664]{1,0:T(8,128)(2,1)} %bitcast.82, bf16[1024,1664]{1,0:T(8,128)(2,1)S(1)} %bitcast.80), kind=kOutput, calls=%fused_computation.47 | convolution fusion | flops 887619584 | bytes 8822784 | tf_op jit(solution)/shard_map/dot_general | solution.py:390
  87.8 2.8 %fusion.3.grad = bf16[128,1664]{1,0:T(8,128)(2,1)} fusion(bf16[128,256]{1,0:T(8,128)(2,1)S(1)} %convolution_convert_fusion.3, bf16[1664,256]{1,0:T(8,128)(2,1)} %param.20, f32[128,1664]{1,0:T(8,128)} %get-tuple-element.66, f32[128,1664]{1,0:T(8,128)} %get-tuple-element.63), kind=kOutput, calls=%fused_computation.12 | convolution fusion | flops 109903872 | bytes 3047424 | tf_op jit(solution)/shard_map/dot_general | solution.py:390
  98.3 2.5 %collective-permute-start.3 = (bf16[256,1664]{1,0:T(8,128)(2,1)}, bf16[256,1664]{1,0:T(8,128)(2,1)}, u32[]{:S(2)}, u32[]{:S(2)}) collective-permute-start(bf16[256,1664]{1,0:T(8,128)(2,1)} %convolution_convert_fusion.1), channel_id=1, source_target_pairs={{0,6},{1,97},{2,0},{3,99},{4,2},{5,101},{6,4},{7,103},{8,14},{9,10... | collective-permute-start | bytes 2555912 | tf_op jit(solution)/shard_map/ppermute | solution.py:416
  104.3 2.9 %collective-permute-start.6 = (bf16[264,512]{1,0:T(8,128)(2,1)}, bf16[264,512]{1,0:T(8,128)(2,1)}, u32[]{:S(2)}, u32[]{:S(2)}) collective-permute-start(bf16[264,512]{1,0:T(8,128)(2,1)} %get-tuple-element.59), channel_id=1, source_target_pairs={{0,6},{1,97},{2,0},{3,99},{4,2},{5,101},{6,4},{7,103},{8,14},{9,10... | collective-permute-start | bytes 811016 | tf_op jit(solution)/shard_map/ppermute | solution.py:416
  107.2 15.5 %collective-permute-done.5.refs_3_ = bf16[264,512]{1,0:T(8,128)(2,1)} collective-permute-done((bf16[264,512]{1,0:T(8,128)(2,1)}, bf16[264,512]{1,0:T(8,128)(2,1)}, u32[]{:S(2)}, u32[]{:S(2)}) %collective-permute-start.5) | collective-permute-done | bytes 270368 | tf_op jit(solution)/shard_map/ppermute | solution.py:416
  126.2 4.8 %collective-permute-done.7.refs_5_ = bf16[264,512]{1,0:T(8,128)(2,1)} collective-permute-done((bf16[264,512]{1,0:T(8,128)(2,1)}, bf16[264,512]{1,0:T(8,128)(2,1)}, u32[]{:S(2)}, u32[]{:S(2)}) %collective-permute-start.7) | collective-permute-done | bytes 270368 | tf_op jit(solution)/shard_map/ppermute | solution.py:416
  131.0 4.5 %fold_first.1 = (bf16[64,2432]{1,0:T(8,128)(2,1)}, bf16[64,2432]{1,0:T(8,128)(2,1)}, bf16[64,2432]{1,0:T(8,128)(2,1)}, f32[64,2176]{1,0:T(8,128)}, bf16[64,256]{1,0:T(8,128)(2,1)}) custom-call(s32[1]{0:T(128)} %bitcast.25.here, f32[256,1664]{1,0:T(8,128)} %fusion.26.mlp, f32[256,512]{1,0:T(8,128)} %convolution_add_fusion.5.cross, ...), custom_call_target="tpu_custom_call" | custom-call | tf_op jit(solution)/shard_map/fold_first/pallas_call | solution.py:460
  136.6 2.2 collective-permute-start.9
  138.8 5.4 %collective-permute-done.10.refs_2_ = bf16[64,2432]{1,0:T(8,128)(2,1)S(1)} collective-permute-done((bf16[64,2432]{1,0:T(8,128)(2,1)}, bf16[64,2432]{1,0:T(8,128)(2,1)S(1)}, u32[]{:S(2)}, u32[]{:S(2)}) %collective-permute-start.10) | collective-permute-done | bytes 311328 | tf_op jit(solution)/shard_map/ppermute | solution.py:416
  144.2 3.0 %collective-permute-done.8.refs_0_ = bf16[64,2432]{1,0:T(8,128)(2,1)S(1)} collective-permute-done((bf16[64,2432]{1,0:T(8,128)(2,1)}, bf16[64,2432]{1,0:T(8,128)(2,1)S(1)}, u32[]{:S(2)}, u32[]{:S(2)}) %collective-permute-start.8) | collective-permute-done | bytes 311328 | tf_op jit(solution)/shard_map/ppermute | solution.py:416
  148.0 2.5 %fold_second.1 = (bf16[16,6272]{1,0:T(8,128)(2,1)}, bf16[16,6272]{1,0:T(8,128)(2,1)}, bf16[16,6272]{1,0:T(8,128)(2,1)}, f32[16,2176]{1,0:T(8,128)}, bf16[16,4096]{1,0:T(8,128)(2,1)}) custom-call(s32[1]{0:T(128)} %bitcast.24.here, f32[64,2176]{1,0:T(8,128)} %get-tuple-element.29.own_in, bf16[64,256]{1,0:T(8,128)(2,1)} %get-tuple-element.30.hot, ...), custom_call_target="tpu_custom_call" | custom-call | tf_op jit(solution)/shard_map/fold_second/pallas_call | solution.py:497
  150.9 2.8 %collective-permute-start.12 = (bf16[16,6272]{1,0:T(8,128)(2,1)}, bf16[16,6272]{1,0:T(8,128)(2,1)S(1)}, u32[]{:S(2)}, u32[]{:S(2)}) collective-permute-start(bf16[16,6272]{1,0:T(8,128)(2,1)} %get-tuple-element.36), channel_id=1, source_target_pairs={{0,96},{1,25},{2,98},{3,27},{4,100},{5,29},{6,102},{7,31},{8,104},... | collective-permute-start | bytes 602120 | tf_op jit(solution)/shard_map/ppermute | solution.py:416
  153.7 3.9 %collective-permute-done.11 = bf16[16,6272]{1,0:T(8,128)(2,1)S(1)} collective-permute-done((bf16[16,6272]{1,0:T(8,128)(2,1)}, bf16[16,6272]{1,0:T(8,128)(2,1)S(1)}, u32[]{:S(2)}, u32[]{:S(2)}) %collective-permute-start.11) | collective-permute-done | bytes 200736 | tf_op jit(solution)/shard_map/ppermute | solution.py:416
  164.0 5.8 %all-to-all-start.3 = ((bf16[64,16,512]{2,1,0:T(8,128)(2,1)}), bf16[64,16,512]{2,1,0:T(8,128)(2,1)S(1)}, u32[]{:S(2)}, u32[]{:S(2)}) async-start(bf16[64,16,512]{2,1,0:T(8,128)(2,1)} %broadcast_in_dim.37), calls=%async_computation.3 | async-start | bytes 2097152 | tf_op jit(solution)/shard_map/all_to_all | solution.py:394
  169.8 7.7 %pack.1 = bf16[128,40,128]{2,1,0:T(8,128)(2,1)} custom-call(s32[128,64]{1,0:T(8,128)} %get-tuple-element.27.inverse, bf16[128,1664]{1,0:T(8,128)(2,1)} %fusion.3.grad), custom_call_target="tpu_custom_call" | custom-call | tf_op jit(solution)/shard_map/pack/pallas_call | solution.py:193
  177.5 7.0 %all-to-all-done.3 = bf16[64,16,512]{2,1,0:T(8,128)(2,1)S(1)} async-done(((bf16[64,16,512]{2,1,0:T(8,128)(2,1)}), bf16[64,16,512]{2,1,0:T(8,128)(2,1)S(1)}, u32[]{:S(2)}, u32[]{:S(2)}) %all-to-all-start.3) | async-done | bytes 1048608 | tf_op jit(solution)/shard_map/all_to_all | solution.py:394
  184.6 4.6 %all-to-all-start.2 = ((bf16[128,40,128]{2,1,0:T(8,128)(2,1)}), bf16[128,40,128]{2,1,0:T(8,128)(2,1)S(1)}, u32[]{:S(2)}, u32[]{:S(2)}) async-start(bf16[128,40,128]{2,1,0:T(8,128)(2,1)} %pack.1), calls=%async_computation.2 | async-start | bytes 2621440 | tf_op jit(solution)/shard_map/all_to_all | solution.py:394
  194.0 17.2 %all-to-all-done.2.came = bf16[128,40,128]{2,1,0:T(8,128)(2,1)S(1)} async-done(((bf16[128,40,128]{2,1,0:T(8,128)(2,1)}), bf16[128,40,128]{2,1,0:T(8,128)(2,1)S(1)}, u32[]{:S(2)}, u32[]{:S(2)}) %all-to-all-start.2) | async-done | bytes 1310752 | tf_op jit(solution)/shard_map/all_to_all | solution.py:394
  212.2 8.5 %cold_sum.1 = f32[2048,128]{1,0:T(8,128)} custom-call(s32[128,128]{1,0:T(8,128)} %bitcast.86, bf16[128,40,128]{2,1,0:T(8,128)(2,1)} %copy-done.5), custom_call_target="tpu_custom_call" | custom-call | tf_op jit(solution)/shard_map/cold_sum/pallas_call | solution.py:251
  221.4 10.6 %hot_sum.1 = f32[4096,128]{1,0:T(8,128)} custom-call(s32[2,64]{1,0:T(2,128)} %pad_add_fusion.owners, s32[128,128]{1,0:T(8,128)} %bitcast.87, bf16[64,4096]{1,0:T(8,128)(2,1)} %pad_maximum_fusion.7.held, bf16[64,4096]{1,0:T(8,128)(2,1)} %collective-permute-done.14.came), custom_call_target="tpu_custom_call" | custom-call | tf_op jit(solution)/shard_map/hot_sum/pallas_call | solution.py:288
  231.9 3.7 %unpack.1 = (f32[1664,256]{1,0:T(8,128)}, f32[256,1664]{1,0:T(8,128)}, f32[13,128]{1,0:T(8,128)}, f32[16,128]{1,0:T(8,128)}, f32[16,128]{1,0:T(8,128)}) custom-call(s32[1]{0:T(128)} %bitcast.27.core, bf16[1024,512]{1,0:T(8,128)(2,1)} %bitcast.79, bf16[1024,512]{1,0:T(8,128)(2,1)} %collective-permute-done.15.came), custom_call_target="tpu_custom_call" | custom-call | tf_op jit(solution)/shard_map/unpack/pallas_call | solution.py:364
  (128 shorter events, 45.0 us)
Async XLA Ops:
  0.6 52.6 %copy-start = (bf16[4096,128]{1,0:T(8,128)(2,1)S(1)}, bf16[4096,128]{1,0:T(8,128)(2,1)}, u32[]{:S(2)}) copy-start(bf16[4096,128]{1,0:T(8,128)(2,1)} %param.18) | copy-start | bytes 3145732
  11.4 20.4 %all-to-all-start = ((s32[128,1,128]{2,1,0:T(1,128)}), s32[128,1,128]{2,1,0:T(1,128)S(1)}, u32[]{:S(2)}, u32[]{:S(2)}) async-start(s32[128,1,128]{2,1,0:T(1,128)} %bitcast.92), calls=%async_computation | async-start | bytes 131072 | tf_op jit(solution)/shard_map/all_to_all | solution.py:394
  40.1 26.8 %all-to-all-start.1 = ((bf16[128,40,128]{2,1,0:T(8,128)(2,1)}), bf16[128,40,128]{2,1,0:T(8,128)(2,1)S(1)}, u32[]{:S(2)}, u32[]{:S(2)}) async-start(bf16[128,40,128]{2,1,0:T(8,128)(2,1)} %bitcast.77), calls=%async_computation.1 | async-start | bytes 2621440 | tf_op jit(solution)/shard_map/all_to_all | solution.py:394
  68.0 7.1 %copy-start.9 = (bf16[256,1664]{1,0:T(8,128)(2,1)S(1)}, bf16[256,1664]{1,0:T(8,128)(2,1)}, u32[]{:S(2)}) copy-start(bf16[256,1664]{1,0:T(8,128)(2,1)} %param.21) | copy-start | bytes 2555908
  68.0 7.1 %copy-start.20 = (f32[1664]{0:T(1024)S(1)}, f32[1664]{0:T(1024)}, u32[]{:S(2)}) copy-start(f32[1664]{0:T(1024)} %param.22) | copy-start | bytes 19972
  73.3 4.0 %copy-start.7 = (bf16[4,4,4,16,1664]{4,3,2,1,0:T(8,128)(2,1)S(1)}, bf16[4,4,4,16,1664]{4,3,2,1,0:T(8,128)(2,1)}, u32[]{:S(2)}) copy-start(bf16[4,4,4,16,1664]{4,3,2,1,0:T(8,128)(2,1)} %copy.36) | copy-start | bytes 10223620
  77.3 4.5 %copy-start.23 = (s32[128]{0:T(128)S(1)}, s32[128]{0:T(128)}, u32[]{:S(2)}) copy-start(s32[128]{0:T(128)} %param.19) | copy-start | bytes 1540
  77.3 5.3 %copy-start.8 = (bf16[4,4,4,16,1664]{4,3,2,1,0:T(8,128)(2,1)S(1)}, bf16[4,4,4,16,1664]{4,3,2,1,0:T(8,128)(2,1)}, u32[]{:S(2)}) copy-start(bf16[4,4,4,16,1664]{4,3,2,1,0:T(8,128)(2,1)} %copy.37) | copy-start | bytes 10223620
  86.4 6.1 %collective-permute-start.1 = (bf16[128,2304]{1,0:T(8,128)(2,1)}, bf16[128,2304]{1,0:T(8,128)(2,1)S(1)}, u32[]{:S(2)}, u32[]{:S(2)}) collective-permute-start(bf16[128,2304]{1,0:T(8,128)(2,1)} %get-tuple-element.50), channel_id=1, source_target_pairs={{0,1},{1,0},{2,3},{3,2},{4,5},{5,4},{6,7},{7,6},{8,9},{9,8},{10,11... | collective-permute-start | bytes 1769480 | tf_op jit(solution)/shard_map/ppermute | solution.py:596
  87.3 5.4 %collective-permute-start = (bf16[128,2688]{1,0:T(8,128)(2,1)}, bf16[128,2688]{1,0:T(8,128)(2,1)}, u32[]{:S(2)}, u32[]{:S(2)}) collective-permute-start(bf16[128,2688]{1,0:T(8,128)(2,1)} %pad_maximum_fusion.6), channel_id=1, source_target_pairs={{0,1},{1,0},{2,3},{3,2},{4,5},{5,4},{6,7},{7,6},{8,9},{9,8},{10,11... | collective-permute-start | bytes 2064392 | tf_op jit(solution)/shard_map/ppermute | solution.py:572
  94.8 7.8 %copy-start.2 = (bf16[128,1024]{1,0:T(8,128)(2,1)}, bf16[128,1024]{1,0:T(8,128)(2,1)S(1)}, u32[]{:S(2)}) copy-start(bf16[128,1024]{1,0:T(8,128)(2,1)S(1)} %slice.80) | copy-start | bytes 786436
  96.2 34.8 %collective-permute-start.4 = (bf16[256,1664]{1,0:T(8,128)(2,1)}, bf16[256,1664]{1,0:T(8,128)(2,1)}, u32[]{:S(2)}, u32[]{:S(2)}) collective-permute-start(bf16[256,1664]{1,0:T(8,128)(2,1)} %convolution_convert_fusion), channel_id=1, source_target_pairs={{0,4},{1,65},{2,6},{3,67},{4,0},{5,69},{6,2},{7,71},{8,12},{9,73},... | collective-permute-start | bytes 2555912 | tf_op jit(solution)/shard_map/ppermute | solution.py:416
  98.3 32.7 %collective-permute-start.3 = (bf16[256,1664]{1,0:T(8,128)(2,1)}, bf16[256,1664]{1,0:T(8,128)(2,1)}, u32[]{:S(2)}, u32[]{:S(2)}) collective-permute-start(bf16[256,1664]{1,0:T(8,128)(2,1)} %convolution_convert_fusion.1), channel_id=1, source_target_pairs={{0,6},{1,97},{2,0},{3,99},{4,2},{5,101},{6,4},{7,103},{8,14},{9,10... | collective-permute-start | bytes 2555912 | tf_op jit(solution)/shard_map/ppermute | solution.py:416
  102.1 28.9 %collective-permute-start.2 = (bf16[256,1664]{1,0:T(8,128)(2,1)}, bf16[256,1664]{1,0:T(8,128)(2,1)}, u32[]{:S(2)}, u32[]{:S(2)}) collective-permute-start(bf16[256,1664]{1,0:T(8,128)(2,1)} %convolution_convert_fusion.2), channel_id=1, source_target_pairs={{0,2},{1,33},{2,4},{3,35},{4,6},{5,37},{6,0},{7,39},{8,10},{9,41},... | collective-permute-start | bytes 2555912 | tf_op jit(solution)/shard_map/ppermute | solution.py:416
  104.0 18.7 %collective-permute-start.5 = (bf16[264,512]{1,0:T(8,128)(2,1)}, bf16[264,512]{1,0:T(8,128)(2,1)}, u32[]{:S(2)}, u32[]{:S(2)}) collective-permute-start(bf16[264,512]{1,0:T(8,128)(2,1)} %get-tuple-element.60), channel_id=1, source_target_pairs={{0,2},{1,33},{2,4},{3,35},{4,6},{5,37},{6,0},{7,39},{8,10},{9,41},... | collective-permute-start | bytes 811016 | tf_op jit(solution)/shard_map/ppermute | solution.py:416
  104.3 20.3 %copy-start.3 = (bf16[128,1024]{1,0:T(8,128)(2,1)S(1)}, bf16[128,1024]{1,0:T(8,128)(2,1)}, u32[]{:S(2)}) copy-start(bf16[128,1024]{1,0:T(8,128)(2,1)} %copy-done.2) | copy-start | bytes 786436
  104.3 21.9 %collective-permute-start.6 = (bf16[264,512]{1,0:T(8,128)(2,1)}, bf16[264,512]{1,0:T(8,128)(2,1)}, u32[]{:S(2)}, u32[]{:S(2)}) collective-permute-start(bf16[264,512]{1,0:T(8,128)(2,1)} %get-tuple-element.59), channel_id=1, source_target_pairs={{0,6},{1,97},{2,0},{3,99},{4,2},{5,101},{6,4},{7,103},{8,14},{9,10... | collective-permute-start | bytes 811016 | tf_op jit(solution)/shard_map/ppermute | solution.py:416
  122.7 8.3 %collective-permute-start.7 = (bf16[264,512]{1,0:T(8,128)(2,1)}, bf16[264,512]{1,0:T(8,128)(2,1)}, u32[]{:S(2)}, u32[]{:S(2)}) collective-permute-start(bf16[264,512]{1,0:T(8,128)(2,1)} %get-tuple-element.58), channel_id=1, source_target_pairs={{0,4},{1,65},{2,6},{3,67},{4,0},{5,69},{6,2},{7,71},{8,12},{9,73},... | collective-permute-start | bytes 811016 | tf_op jit(solution)/shard_map/ppermute | solution.py:416
  135.5 8.7 %collective-permute-start.10 = (bf16[64,2432]{1,0:T(8,128)(2,1)}, bf16[64,2432]{1,0:T(8,128)(2,1)S(1)}, u32[]{:S(2)}, u32[]{:S(2)}) collective-permute-start(bf16[64,2432]{1,0:T(8,128)(2,1)} %get-tuple-element.33), channel_id=1, source_target_pairs={{0,16},{1,5},{2,18},{3,7},{4,20},{5,1},{6,22},{7,3},{8,24},{9,13},... | collective-permute-start | bytes 933896 | tf_op jit(solution)/shard_map/ppermute | solution.py:416
  135.5 11.7 %collective-permute-start.8 = (bf16[64,2432]{1,0:T(8,128)(2,1)}, bf16[64,2432]{1,0:T(8,128)(2,1)S(1)}, u32[]{:S(2)}, u32[]{:S(2)}) collective-permute-start(bf16[64,2432]{1,0:T(8,128)(2,1)} %get-tuple-element.31), channel_id=1, source_target_pairs={{0,8},{1,3},{2,10},{3,5},{4,12},{5,7},{6,14},{7,1},{8,16},{9,11},{... | collective-permute-start | bytes 933896 | tf_op jit(solution)/shard_map/ppermute | solution.py:416
  136.6 10.6 %collective-permute-start.9 = (bf16[64,2432]{1,0:T(8,128)(2,1)}, bf16[64,2432]{1,0:T(8,128)(2,1)S(1)}, u32[]{:S(2)}, u32[]{:S(2)}) collective-permute-start(bf16[64,2432]{1,0:T(8,128)(2,1)} %get-tuple-element.32), channel_id=1, source_target_pairs={{0,24},{1,7},{2,26},{3,1},{4,28},{5,3},{6,30},{7,5},{8,0},{9,15},{... | collective-permute-start | bytes 933896 | tf_op jit(solution)/shard_map/ppermute | solution.py:416
  150.5 7.1 %collective-permute-start.11 = (bf16[16,6272]{1,0:T(8,128)(2,1)}, bf16[16,6272]{1,0:T(8,128)(2,1)S(1)}, u32[]{:S(2)}, u32[]{:S(2)}) collective-permute-start(bf16[16,6272]{1,0:T(8,128)(2,1)} %get-tuple-element.35), channel_id=1, source_target_pairs={{0,32},{1,9},{2,34},{3,11},{4,36},{5,13},{6,38},{7,15},{8,40},{9,1... | collective-permute-start | bytes 602120 | tf_op jit(solution)/shard_map/ppermute | solution.py:416
  150.9 8.5 %collective-permute-start.12 = (bf16[16,6272]{1,0:T(8,128)(2,1)}, bf16[16,6272]{1,0:T(8,128)(2,1)S(1)}, u32[]{:S(2)}, u32[]{:S(2)}) collective-permute-start(bf16[16,6272]{1,0:T(8,128)(2,1)} %get-tuple-element.36), channel_id=1, source_target_pairs={{0,96},{1,25},{2,98},{3,27},{4,100},{5,29},{6,102},{7,31},{8,104},... | collective-permute-start | bytes 602120 | tf_op jit(solution)/shard_map/ppermute | solution.py:416
  153.7 7.4 %collective-permute-start.13 = (bf16[16,6272]{1,0:T(8,128)(2,1)}, bf16[16,6272]{1,0:T(8,128)(2,1)S(1)}, u32[]{:S(2)}, u32[]{:S(2)}) collective-permute-start(bf16[16,6272]{1,0:T(8,128)(2,1)} %get-tuple-element.37), channel_id=1, source_target_pairs={{0,64},{1,17},{2,66},{3,19},{4,68},{5,21},{6,70},{7,23},{8,72},{9,... | collective-permute-start | bytes 602120 | tf_op jit(solution)/shard_map/ppermute | solution.py:416
  157.6 3.5 %copy-start.11 = (bf16[16,6272]{1,0:T(8,128)(2,1)}, bf16[16,6272]{1,0:T(8,128)(2,1)S(1)}, u32[]{:S(2)}) copy-start(bf16[16,6272]{1,0:T(8,128)(2,1)S(1)} %collective-permute-done.11) | copy-start | bytes 602116
  164.0 20.6 %all-to-all-start.3 = ((bf16[64,16,512]{2,1,0:T(8,128)(2,1)}), bf16[64,16,512]{2,1,0:T(8,128)(2,1)S(1)}, u32[]{:S(2)}, u32[]{:S(2)}) async-start(bf16[64,16,512]{2,1,0:T(8,128)(2,1)} %broadcast_in_dim.37), calls=%async_computation.3 | async-start | bytes 2097152 | tf_op jit(solution)/shard_map/all_to_all | solution.py:394
  177.5 13.6 %slice-start = ((bf16[16,6272]{1,0:T(8,128)(2,1)}), bf16[16,4096]{1,0:T(8,128)(2,1)S(1)}, s32[]{:S(2)}) async-start(bf16[16,6272]{1,0:T(8,128)(2,1)} %copy-done.11), calls=%async_computation.4 | async-start | bytes 262144 | tf_op jit(solution)/shard_map/slice | solution.py:628
  184.6 6.6 %copy-start.6 = (bf16[64,16,512]{2,1,0:T(8,128)(2,1)}, bf16[64,16,512]{2,1,0:T(8,128)(2,1)S(1)}, u32[]{:S(2)}) copy-start(bf16[64,16,512]{2,1,0:T(8,128)(2,1)S(1)} %all-to-all-done.3) | copy-start | bytes 3145732
  184.6 26.6 %all-to-all-start.2 = ((bf16[128,40,128]{2,1,0:T(8,128)(2,1)}), bf16[128,40,128]{2,1,0:T(8,128)(2,1)S(1)}, u32[]{:S(2)}, u32[]{:S(2)}) async-start(bf16[128,40,128]{2,1,0:T(8,128)(2,1)} %pack.1), calls=%async_computation.2 | async-start | bytes 2621440 | tf_op jit(solution)/shard_map/all_to_all | solution.py:394
  189.2 42.7 %collective-permute-start.15 = (bf16[1024,512]{1,0:T(8,128)(2,1)S(1)}, bf16[1024,512]{1,0:T(8,128)(2,1)}, u32[]{:S(2)}, u32[]{:S(2)}) collective-permute-start(bf16[1024,512]{1,0:T(8,128)(2,1)S(1)} %bitcast.78), channel_id=1, source_target_pairs={{0,1},{1,0},{2,3},{3,2},{4,5},{5,4},{6,7},{7,6},{8,9},{9,8},{10,11... | collective-permute-start | bytes 3145736 | tf_op jit(solution)/shard_map/ppermute | solution.py:636
  192.9 27.8 %copy-start.13 = (f32[16,2176]{1,0:T(8,128)S(1)}, f32[16,2176]{1,0:T(8,128)}, u32[]{:S(2)}) copy-start(f32[16,2176]{1,0:T(8,128)} %copy-done.12) | copy-start | bytes 417796
  192.9 28.5 %collective-permute-start.14 = (bf16[64,4096]{1,0:T(8,128)(2,1)}, bf16[64,4096]{1,0:T(8,128)(2,1)}, u32[]{:S(2)}, u32[]{:S(2)}) collective-permute-start(bf16[64,4096]{1,0:T(8,128)(2,1)} %pad_maximum_fusion.7.held), channel_id=1, source_target_pairs={{0,1},{1,0},{2,3},{3,2},{4,5},{5,4},{6,7},{7,6},{8,9},{9,8},{10,11... | collective-permute-start | bytes 1572872 | tf_op jit(solution)/shard_map/ppermute | solution.py:632
  (13 other events, 18.1 us)

commit v7 on v6

--- a/solution.py
+++ b/solution.py
@@ -226,37 +226,41 @@
     )(hot_index, grad)
 
 
-def cold_kernel(wanted, came, out, wide, *sums):
+def cold_kernel(start, wanted, came, *refs):
+    base, (out, wide, *sums) = (refs[0], refs[1:]) if start else (None, refs)
+    count = wide.shape[0]
     for way in sums:
         way[...] = jnp.zeros(way.shape, F32)
-    wide[...] = came[...].astype(F32)
+    wide[...] = came[start : start + count, :, :].astype(F32)
 
     def source(d, carried):
         for i in range(CAP // WAYS):
             for k, way in enumerate(sums):
                 at = k * (CAP // WAYS) + i
-                here = pl.ds(wanted[d, at], 1)
+                here = pl.ds(wanted[start + d, at], 1)
                 way[here, :] = way[here, :] + wide[d, at : at + 1, :]
         return carried
 
-    lax.fori_loop(0, wide.shape[0], source, 0)
+    lax.fori_loop(0, count, source, 0)
     shard = out.shape[0]
     total = sums[0][:shard, :]
     for way in sums[1:]:
         total = total + way[:shard, :]
-    out[...] = total
-
-
-def cold_sum(wanted, came, shard_rows):
-    return pl.pallas_call(
-        cold_kernel,
+    out[...] = total + base[...] if start else total
+
+
+def cold_sum(wanted, came, shard_rows, base=()):
+    half = came.shape[0] // 2
+    start = half if base else 0
+    return pl.pallas_call(
+        lambda *refs: cold_kernel(start, *refs),
         out_shape=jax.ShapeDtypeStruct((shard_rows, 128), F32),
-        in_specs=[SMEM, VMEM],
+        in_specs=[SMEM, VMEM] + [VMEM] * len(base),
         out_specs=VMEM,
-        scratch_shapes=[pltpu.VMEM((came.shape[0], CAP, 128), F32)]
+        scratch_shapes=[pltpu.VMEM((half, CAP, 128), F32)]
         + [pltpu.VMEM((shard_rows + 8, 128), F32)] * WAYS,
-        name="cold_sum",
-    )(wanted, came)
+        name="cold_last" if base else "cold_first",
+    )(wanted, came, *base)
 
 
 def hot_kernel(owners, listed, held, came, out, wide_held, wide_came):
@@ -560,7 +564,7 @@
     hidden = jax.nn.silu(hidden_in).astype(BF16)
     logits = jnp.dot(hidden, out_weight, preferred_element_type=F32)
     logit_grad = jax.nn.sigmoid(logits) - labels.astype(F32)
-    out_grad = jnp.sum(logit_grad[:, None] * hidden.astype(F32), axis=0)
+    out_grad = jnp.dot(logit_grad, hidden.astype(F32), precision=lax.Precision.HIGHEST)
     hidden_grad = (
         logit_grad[:, None] * out_weight.astype(F32)[None, :] * silu_slope(hidden_in)
     ).astype(BF16)
@@ -630,7 +634,8 @@
     shared = jnp.broadcast_to(sums[None, :, inputs:].astype(BF16), (chips, 16, WIDE))
     shared = exchange(shared, CHIPS).reshape(-1, WIDE)
     hot_other = lax.ppermute(hot_part, CORE, SWAP)
-    cold_grad = cold_sum(got, back, cold_table.shape[0])
+    cold_half = cold_sum(got, back, cold_table.shape[0])
+    cold_grad = cold_sum(got, back, cold_table.shape[0], (cold_half,))
     owners = hot_owners([lax.axis_index(axis) for axis in CHIPS], core)
     hot_grad = hot_sum(owners, got, hot_part, hot_other, hot_table.shape[0])
     other_shared = lax.ppermute(shared, CORE, SWAP)

time: 237 us -> 236 us (level)
  matrix products: 21.5 us -> 17.2 us
  Pallas kernels: 63.6 us -> 67.4 us
  waiting for transfers between devices: 79 us -> 81.7 us
  other arithmetic: 6.79 us -> 4.11 us
    pallas_call x1 -> x2, Pallas kernels: 8.49 us -> 12.2 us  [cold_sum(): pl.pallas_call(lambda *refs: cold_kernel(start, *refs), out_shape=jax.Sha...]
    all_to_all x4, waiting for transfers between devices: 42.9 us -> 45.8 us  [exchange(): return lax.all_to_all(x, axes, split_axis=0, concat_axis=0, tiled=True)]
    unnamed x49 -> x53, local copies, waits for them, and re-layouts: 4.84 us -> 5.62 us
  transfers between devices with their start and end apart: 20 -> 20, of which waited for: 11 -> 11; matrix products, arithmetic and copies ran while one was open for 11% -> 9% of each run, Pallas kernels for 13% -> 15%
where the time goes in v7:
time: 236 us; the launch traced here: 235 us
  waiting for transfers between devices  81.7 us (35%)
  Pallas kernels  67.4 us (29%)
  starting transfers between devices  41.8 us (18%)
  local copies, waits for them, and re-layouts  21.3 us (9%)
  matrix products  17.2 us (7%)
  other arithmetic  4.11 us (2%)
    all_to_all x4, waiting for transfers between devices, exchange(): return lax.all_to_all(x, axes, split_axis=0, concat_axis=0, tiled=True)  45.8 us
    ppermute x12, waiting for transfers between devices, send_on(): lax.ppermute(p, GRP_DEV, route_pairs(phase, s))  35.8 us
    all_to_all x4, starting transfers between devices, exchange(): return lax.all_to_all(x, axes, split_axis=0, concat_axis=0, tiled=True)  26.4 us
    ppermute x12, starting transfers between devices, send_on(): lax.ppermute(p, GRP_DEV, route_pairs(phase, s))  13.9 us
    pallas_call x2, Pallas kernels, cold_sum(): pl.pallas_call(lambda *refs: cold_kernel(start, *refs), out_shape=jax.Sha...  12.2 us
    pallas_call x1, Pallas kernels, hot_sum(): pl.pallas_call(hot_kernel, out_shape=jax.ShapeDtypeStruct((hot_rows, 128)...  10.7 us
    pallas_call x1, Pallas kernels, route(): pl.pallas_call(route_kernel, out_shape=(jax.ShapeDtypeStruct((128, 128),...  9.33 us
    transpose x7, local copies, waits for them, and re-layouts, by_core(): half = parts[:, :, :, c].transpose(*ORDER[c], *rest)  7.9 us
  transfers between devices with their start and end apart: 20, of which 11 were waited for; matrix products, arithmetic and copies ran while one was open for 9% of the time, Pallas kernels for 15%

profile of v7, /device:TPU:0, one launch (start us, length us, event | category | flops | bytes accessed | tf_op | source)
XLA Modules:
  0.0 234.7 jit_solution(10994729253259121842)
XLA Ops:
  2.1 9.3 %route.1 = (s32[128,128]{1,0:T(8,128)}, s32[128,64]{1,0:T(8,128)}, s32[26,128]{1,0:T(8,128)}) custom-call(s32[26,128]{1,0:T(8,128)} %reshape.287.ids.ids_lanes, s32[1,32]{1,0:T(1,128)} %hot_list.1, s32[26,128]{1,0:T(8,128)} %reshape.287.ids.ids_lanes, s32[2048,128]{1,0:T(8,128)} %bitcast.93), custom_call_target="tpu_custom_call" | custom-call | tf_op jit(solution)/shard_map/route/pallas_call | solution.py:84
  11.4 11.2 %all-to-all-start = ((s32[128,1,128]{2,1,0:T(1,128)}), s32[128,1,128]{2,1,0:T(1,128)S(1)}, u32[]{:S(2)}, u32[]{:S(2)}) async-start(s32[128,1,128]{2,1,0:T(1,128)} %bitcast.98), calls=%async_computation | async-start | bytes 131072 | tf_op jit(solution)/shard_map/all_to_all | solution.py:398
  23.7 8.1 %all-to-all-done = s32[128,1,128]{2,1,0:T(1,128)S(1)} async-done(((s32[128,1,128]{2,1,0:T(1,128)}), s32[128,1,128]{2,1,0:T(1,128)S(1)}, u32[]{:S(2)}, u32[]{:S(2)}) %all-to-all-start) | async-done | bytes 65568 | tf_op jit(solution)/shard_map/all_to_all | solution.py:398
  32.4 7.7 %fetch.1 = bf16[5120,128]{1,0:T(8,128)(2,1)} custom-call(s32[128,128]{1,0:T(8,128)} %bitcast.89, bf16[2048,128]{1,0:T(8,128)(2,1)} %table.1), custom_call_target="tpu_custom_call" | custom-call | tf_op jit(solution)/shard_map/fetch/pallas_call | solution.py:114
  40.1 4.8 %all-to-all-start.1 = ((bf16[128,40,128]{2,1,0:T(8,128)(2,1)}), bf16[128,40,128]{2,1,0:T(8,128)(2,1)S(1)}, u32[]{:S(2)}, u32[]{:S(2)}) async-start(bf16[128,40,128]{2,1,0:T(8,128)(2,1)} %bitcast.82), calls=%async_computation.1 | async-start | bytes 2621440 | tf_op jit(solution)/shard_map/all_to_all | solution.py:398
  45.0 3.6 %slice_bitcast_fusion.1 = (bf16[4,4,4,16,1664]{4,3,0,1,2:T(8,128)(2,1)S(1)}, bf16[4,4,4,16,1664]{4,3,1,2,0:T(8,128)(2,1)S(1)}) fusion(bf16[4,4,4,2,16,1664]{5,4,3,2,1,0:T(8,128)(2,1)} %bitcast.80), kind=kLoop, calls=%fused_computation.5 | loop fusion | bytes 13631488 | tf_op jit(solution)/shard_map/transpose | solution.py:518
  48.5 2.1 copy.36
  50.7 2.1 copy.37
  54.5 2.0 hot_spread.1.hot_part
  56.5 10.4 %all-to-all-done.1 = bf16[128,40,128]{2,1,0:T(8,128)(2,1)S(1)} async-done(((bf16[128,40,128]{2,1,0:T(8,128)(2,1)}), bf16[128,40,128]{2,1,0:T(8,128)(2,1)S(1)}, u32[]{:S(2)}, u32[]{:S(2)}) %all-to-all-start.1) | async-done | bytes 1310752 | tf_op jit(solution)/shard_map/all_to_all | solution.py:398
  68.0 5.4 %pool.1 = bf16[128,1664]{1,0:T(8,128)(2,1)} custom-call(s32[26,128]{1,0:T(8,128)} %get-tuple-element.28.position, f32[1664,128]{1,0:T(8,128)} %hot_spread.1.hot_part, bf16[5120,128]{1,0:T(8,128)(2,1)} %bitcast.81), custom_call_target="tpu_custom_call" | custom-call | tf_op jit(solution)/shard_map/pool/pallas_call | solution.py:165
  76.2 4.5 %multiply_convert_fusion.1 = (bf16[128,2048]{1,0:T(8,128)(2,1)S(1)}, f32[128,2048]{1,0:T(8,128)S(1)}) fusion(f32[2048]{0:T(1024)S(1)} %pad_maximum_fusion.11, bf16[128,1664]{1,0:T(8,128)(2,1)S(1)} %get-tuple-element.61, bf16[1024,1664]{1,0:T(8,128)(2,1)} %bitcast.87, bf16[1024,1664]{1,0:T(8,128)(2,1)S(1)} %bitcast.85), kind=kOutput, calls=%fused_computation.46 | convolution fusion | flops 887619584 | bytes 8822784 | tf_op jit(solution)/shard_map/dot_general | solution.py:394
  94.0 2.5 %collective-permute-start.3 = (bf16[256,1664]{1,0:T(8,128)(2,1)}, bf16[256,1664]{1,0:T(8,128)(2,1)}, u32[]{:S(2)}, u32[]{:S(2)}) collective-permute-start(bf16[256,1664]{1,0:T(8,128)(2,1)} %convolution_convert_fusion.1), channel_id=1, source_target_pairs={{0,6},{1,97},{2,0},{3,99},{4,2},{5,101},{6,4},{7,103},{8,14},{9,10... | collective-permute-start | bytes 2555912 | tf_op jit(solution)/shard_map/ppermute | solution.py:420
  100.0 2.9 %collective-permute-start.6 = (bf16[264,512]{1,0:T(8,128)(2,1)}, bf16[264,512]{1,0:T(8,128)(2,1)S(1)}, u32[]{:S(2)}, u32[]{:S(2)}) collective-permute-start(bf16[264,512]{1,0:T(8,128)(2,1)} %get-tuple-element.59), channel_id=1, source_target_pairs={{0,6},{1,97},{2,0},{3,99},{4,2},{5,101},{6,4},{7,103},{8,14},{9,10... | collective-permute-start | bytes 811016 | tf_op jit(solution)/shard_map/ppermute | solution.py:420
  103.0 15.3 %collective-permute-done.5.refs_3_ = bf16[264,512]{1,0:T(8,128)(2,1)} collective-permute-done((bf16[264,512]{1,0:T(8,128)(2,1)}, bf16[264,512]{1,0:T(8,128)(2,1)}, u32[]{:S(2)}, u32[]{:S(2)}) %collective-permute-start.5) | collective-permute-done | bytes 270368 | tf_op jit(solution)/shard_map/ppermute | solution.py:420
  121.7 4.7 %collective-permute-done.7.refs_5_ = bf16[264,512]{1,0:T(8,128)(2,1)S(1)} collective-permute-done((bf16[264,512]{1,0:T(8,128)(2,1)}, bf16[264,512]{1,0:T(8,128)(2,1)S(1)}, u32[]{:S(2)}, u32[]{:S(2)}) %collective-permute-start.7) | collective-permute-done | bytes 270368 | tf_op jit(solution)/shard_map/ppermute | solution.py:420
  127.1 4.5 %fold_first.1 = (bf16[64,2432]{1,0:T(8,128)(2,1)}, bf16[64,2432]{1,0:T(8,128)(2,1)}, bf16[64,2432]{1,0:T(8,128)(2,1)}, f32[64,2176]{1,0:T(8,128)}, bf16[64,256]{1,0:T(8,128)(2,1)}) custom-call(s32[1]{0:T(128)} %bitcast.25.here, f32[256,1664]{1,0:T(8,128)} %fusion.26.mlp, f32[256,512]{1,0:T(8,128)} %convolution_add_fusion.5.cross, ...), custom_call_target="tpu_custom_call" | custom-call | tf_op jit(solution)/shard_map/fold_first/pallas_call | solution.py:464
  132.7 2.2 collective-permute-start.9
  134.9 5.4 %collective-permute-done.10.refs_2_ = bf16[64,2432]{1,0:T(8,128)(2,1)S(1)} collective-permute-done((bf16[64,2432]{1,0:T(8,128)(2,1)}, bf16[64,2432]{1,0:T(8,128)(2,1)S(1)}, u32[]{:S(2)}, u32[]{:S(2)}) %collective-permute-start.10) | collective-permute-done | bytes 311328 | tf_op jit(solution)/shard_map/ppermute | solution.py:420
  140.3 3.0 %collective-permute-done.8.refs_0_ = bf16[64,2432]{1,0:T(8,128)(2,1)S(1)} collective-permute-done((bf16[64,2432]{1,0:T(8,128)(2,1)}, bf16[64,2432]{1,0:T(8,128)(2,1)S(1)}, u32[]{:S(2)}, u32[]{:S(2)}) %collective-permute-start.8) | collective-permute-done | bytes 311328 | tf_op jit(solution)/shard_map/ppermute | solution.py:420
  144.1 2.5 %fold_second.1 = (bf16[16,6272]{1,0:T(8,128)(2,1)}, bf16[16,6272]{1,0:T(8,128)(2,1)}, bf16[16,6272]{1,0:T(8,128)(2,1)}, f32[16,2176]{1,0:T(8,128)}, bf16[16,4096]{1,0:T(8,128)(2,1)}) custom-call(s32[1]{0:T(128)} %bitcast.24.here, f32[64,2176]{1,0:T(8,128)} %get-tuple-element.29.own_in, bf16[64,256]{1,0:T(8,128)(2,1)} %get-tuple-element.30.hot, ...), custom_call_target="tpu_custom_call" | custom-call | tf_op jit(solution)/shard_map/fold_second/pallas_call | solution.py:501
  147.1 2.8 %collective-permute-start.12 = (bf16[16,6272]{1,0:T(8,128)(2,1)}, bf16[16,6272]{1,0:T(8,128)(2,1)S(1)}, u32[]{:S(2)}, u32[]{:S(2)}) collective-permute-start(bf16[16,6272]{1,0:T(8,128)(2,1)} %get-tuple-element.36), channel_id=1, source_target_pairs={{0,96},{1,25},{2,98},{3,27},{4,100},{5,29},{6,102},{7,31},{8,104},... | collective-permute-start | bytes 602120 | tf_op jit(solution)/shard_map/ppermute | solution.py:420
  149.8 3.9 %collective-permute-done.11 = bf16[16,6272]{1,0:T(8,128)(2,1)S(1)} collective-permute-done((bf16[16,6272]{1,0:T(8,128)(2,1)}, bf16[16,6272]{1,0:T(8,128)(2,1)S(1)}, u32[]{:S(2)}, u32[]{:S(2)}) %collective-permute-start.11) | collective-permute-done | bytes 200736 | tf_op jit(solution)/shard_map/ppermute | solution.py:420
  159.3 5.8 %all-to-all-start.3 = ((bf16[64,16,512]{2,1,0:T(8,128)(2,1)}), bf16[64,16,512]{2,1,0:T(8,128)(2,1)S(1)}, u32[]{:S(2)}, u32[]{:S(2)}) async-start(bf16[64,16,512]{2,1,0:T(8,128)(2,1)} %broadcast_in_dim.36), calls=%async_computation.3 | async-start | bytes 2097152 | tf_op jit(solution)/shard_map/all_to_all | solution.py:398
  165.1 7.7 %pack.1 = bf16[128,40,128]{2,1,0:T(8,128)(2,1)} custom-call(s32[128,64]{1,0:T(8,128)} %get-tuple-element.27.inverse, bf16[128,1664]{1,0:T(8,128)(2,1)} %fusion.3.grad), custom_call_target="tpu_custom_call" | custom-call | tf_op jit(solution)/shard_map/pack/pallas_call | solution.py:193
  172.8 7.0 %all-to-all-done.3 = bf16[64,16,512]{2,1,0:T(8,128)(2,1)S(1)} async-done(((bf16[64,16,512]{2,1,0:T(8,128)(2,1)}), bf16[64,16,512]{2,1,0:T(8,128)(2,1)S(1)}, u32[]{:S(2)}, u32[]{:S(2)}) %all-to-all-start.3) | async-done | bytes 1048608 | tf_op jit(solution)/shard_map/all_to_all | solution.py:398
  179.9 4.6 %all-to-all-start.2 = ((bf16[128,40,128]{2,1,0:T(8,128)(2,1)}), bf16[128,40,128]{2,1,0:T(8,128)(2,1)S(1)}, u32[]{:S(2)}, u32[]{:S(2)}) async-start(bf16[128,40,128]{2,1,0:T(8,128)(2,1)} %pack.1), calls=%async_computation.2 | async-start | bytes 2621440 | tf_op jit(solution)/shard_map/all_to_all | solution.py:398
  186.1 20.3 %all-to-all-done.2.refs_1_ = bf16[128,40,128]{2,1,0:T(8,128)(2,1)S(1)} async-done(((bf16[128,40,128]{2,1,0:T(8,128)(2,1)}), bf16[128,40,128]{2,1,0:T(8,128)(2,1)S(1)}, u32[]{:S(2)}, u32[]{:S(2)}) %all-to-all-start.2) | async-done | bytes 1310752 | tf_op jit(solution)/shard_map/all_to_all | solution.py:398
  207.5 6.1 %cold_first.1.refs_2_ = f32[2048,128]{1,0:T(8,128)} custom-call(s32[128,128]{1,0:T(8,128)} %bitcast.90, bf16[128,40,128]{2,1,0:T(8,128)(2,1)} %copy-done.2), custom_call_target="tpu_custom_call" | custom-call | tf_op jit(solution)/shard_map/cold_first/pallas_call | solution.py:255
  213.6 6.1 %cold_last.1 = f32[2048,128]{1,0:T(8,128)} custom-call(s32[128,128]{1,0:T(8,128)} %bitcast.91, bf16[128,40,128]{2,1,0:T(8,128)(2,1)} %copy-done.2, f32[2048,128]{1,0:T(8,128)} %cold_first.1.refs_2_), custom_call_target="tpu_custom_call" | custom-call | tf_op jit(solution)/shard_map/cold_last/pallas_call | solution.py:255
  220.3 10.7 %hot_sum.1 = f32[4096,128]{1,0:T(8,128)} custom-call(s32[2,64]{1,0:T(2,128)} %pad_add_fusion.owners, s32[128,128]{1,0:T(8,128)} %bitcast.92, bf16[64,4096]{1,0:T(8,128)(2,1)} %copy-done.13, bf16[64,4096]{1,0:T(8,128)(2,1)} %collective-permute-done.14.came), custom_call_target="tpu_custom_call" | custom-call | tf_op jit(solution)/shard_map/hot_sum/pallas_call | solution.py:292
  231.0 3.7 %unpack.1 = (f32[1664,256]{1,0:T(8,128)}, f32[256,1664]{1,0:T(8,128)}, f32[13,128]{1,0:T(8,128)}, f32[16,128]{1,0:T(8,128)}, f32[16,128]{1,0:T(8,128)}) custom-call(s32[1]{0:T(128)} %bitcast.29.core, bf16[1024,512]{1,0:T(8,128)(2,1)} %bitcast.84, bf16[1024,512]{1,0:T(8,128)(2,1)} %collective-permute-done.15.came), custom_call_target="tpu_custom_call" | custom-call | tf_op jit(solution)/shard_map/unpack/pallas_call | solution.py:368
  (133 shorter events, 40.6 us)
Async XLA Ops:
  0.6 52.6 %copy-start = (bf16[4096,128]{1,0:T(8,128)(2,1)S(1)}, bf16[4096,128]{1,0:T(8,128)(2,1)}, u32[]{:S(2)}) copy-start(bf16[4096,128]{1,0:T(8,128)(2,1)} %param.18) | copy-start | bytes 3145732
  11.4 20.4 %all-to-all-start = ((s32[128,1,128]{2,1,0:T(1,128)}), s32[128,1,128]{2,1,0:T(1,128)S(1)}, u32[]{:S(2)}, u32[]{:S(2)}) async-start(s32[128,1,128]{2,1,0:T(1,128)} %bitcast.98), calls=%async_computation | async-start | bytes 131072 | tf_op jit(solution)/shard_map/all_to_all | solution.py:398
  40.1 26.8 %all-to-all-start.1 = ((bf16[128,40,128]{2,1,0:T(8,128)(2,1)}), bf16[128,40,128]{2,1,0:T(8,128)(2,1)S(1)}, u32[]{:S(2)}, u32[]{:S(2)}) async-start(bf16[128,40,128]{2,1,0:T(8,128)(2,1)} %bitcast.82), calls=%async_computation.1 | async-start | bytes 2621440 | tf_op jit(solution)/shard_map/all_to_all | solution.py:398
  54.4 18.9 %copy-start.9 = (bf16[1664,256]{1,0:T(8,128)(2,1)S(1)}, bf16[1664,256]{1,0:T(8,128)(2,1)}, u32[]{:S(2)}) copy-start(bf16[1664,256]{1,0:T(8,128)(2,1)} %param.20) | copy-start | bytes 2555908
  67.9 6.9 %copy-start.8 = (bf16[256,1664]{1,0:T(8,128)(2,1)S(1)}, bf16[256,1664]{1,0:T(8,128)(2,1)}, u32[]{:S(2)}) copy-start(bf16[256,1664]{1,0:T(8,128)(2,1)} %param.21) | copy-start | bytes 2555908
  68.0 6.9 %copy-start.22 = (f32[1664]{0:T(1024)S(1)}, f32[1664]{0:T(1024)}, u32[]{:S(2)}) copy-start(f32[1664]{0:T(1024)} %param.22) | copy-start | bytes 19972
  76.2 4.6 %copy-start.25 = (s32[128]{0:T(128)S(1)}, s32[128]{0:T(128)}, u32[]{:S(2)}) copy-start(s32[128]{0:T(128)} %param.19) | copy-start | bytes 1540
  76.2 5.3 %copy-start.7 = (bf16[4,4,4,16,1664]{4,3,2,1,0:T(8,128)(2,1)S(1)}, bf16[4,4,4,16,1664]{4,3,2,1,0:T(8,128)(2,1)}, u32[]{:S(2)}) copy-start(bf16[4,4,4,16,1664]{4,3,2,1,0:T(8,128)(2,1)} %copy.37) | copy-start | bytes 10223620
  84.6 4.5 %collective-permute-start.1 = (bf16[128,2304]{1,0:T(8,128)(2,1)}, bf16[128,2304]{1,0:T(8,128)(2,1)S(1)}, u32[]{:S(2)}, u32[]{:S(2)}) collective-permute-start(bf16[128,2304]{1,0:T(8,128)(2,1)} %get-tuple-element.50), channel_id=1, source_target_pairs={{0,1},{1,0},{2,3},{3,2},{4,5},{5,4},{6,7},{7,6},{8,9},{9,8},{10,11... | collective-permute-start | bytes 1769480 | tf_op jit(solution)/shard_map/ppermute | solution.py:600
  84.7 4.6 %collective-permute-start = (bf16[128,2688]{1,0:T(8,128)(2,1)S(1)}, bf16[128,2688]{1,0:T(8,128)(2,1)}, u32[]{:S(2)}, u32[]{:S(2)}) collective-permute-start(bf16[128,2688]{1,0:T(8,128)(2,1)S(1)} %pad_maximum_fusion.6), channel_id=1, source_target_pairs={{0,1},{1,0},{2,3},{3,2},{4,5},{5,4},{6,7},{7,6},{8,9},{9,8},{10,11... | collective-permute-start | bytes 2064392 | tf_op jit(solution)/shard_map/ppermute | solution.py:576
  91.8 34.6 %collective-permute-start.4 = (bf16[256,1664]{1,0:T(8,128)(2,1)S(1)}, bf16[256,1664]{1,0:T(8,128)(2,1)}, u32[]{:S(2)}, u32[]{:S(2)}) collective-permute-start(bf16[256,1664]{1,0:T(8,128)(2,1)S(1)} %convolution_convert_fusion), channel_id=1, source_target_pairs={{0,4},{1,65},{2,6},{3,67},{4,0},{5,69},{6,2},{7,71},{8,12},{9,73},... | collective-permute-start | bytes 2555912 | tf_op jit(solution)/shard_map/ppermute | solution.py:420
  94.0 32.4 %collective-permute-start.3 = (bf16[256,1664]{1,0:T(8,128)(2,1)}, bf16[256,1664]{1,0:T(8,128)(2,1)}, u32[]{:S(2)}, u32[]{:S(2)}) collective-permute-start(bf16[256,1664]{1,0:T(8,128)(2,1)} %convolution_convert_fusion.1), channel_id=1, source_target_pairs={{0,6},{1,97},{2,0},{3,99},{4,2},{5,101},{6,4},{7,103},{8,14},{9,10... | collective-permute-start | bytes 2555912 | tf_op jit(solution)/shard_map/ppermute | solution.py:420
  97.9 29.2 %collective-permute-start.2 = (bf16[256,1664]{1,0:T(8,128)(2,1)}, bf16[256,1664]{1,0:T(8,128)(2,1)}, u32[]{:S(2)}, u32[]{:S(2)}) collective-permute-start(bf16[256,1664]{1,0:T(8,128)(2,1)} %convolution_convert_fusion.2), channel_id=1, source_target_pairs={{0,2},{1,33},{2,4},{3,35},{4,6},{5,37},{6,0},{7,39},{8,10},{9,41},... | collective-permute-start | bytes 2555912 | tf_op jit(solution)/shard_map/ppermute | solution.py:420
  99.7 18.5 %collective-permute-start.5 = (bf16[264,512]{1,0:T(8,128)(2,1)}, bf16[264,512]{1,0:T(8,128)(2,1)}, u32[]{:S(2)}, u32[]{:S(2)}) collective-permute-start(bf16[264,512]{1,0:T(8,128)(2,1)} %get-tuple-element.60), channel_id=1, source_target_pairs={{0,2},{1,33},{2,4},{3,35},{4,6},{5,37},{6,0},{7,39},{8,10},{9,41},... | collective-permute-start | bytes 811016 | tf_op jit(solution)/shard_map/ppermute | solution.py:420
  100.0 21.7 %collective-permute-start.6 = (bf16[264,512]{1,0:T(8,128)(2,1)}, bf16[264,512]{1,0:T(8,128)(2,1)S(1)}, u32[]{:S(2)}, u32[]{:S(2)}) collective-permute-start(bf16[264,512]{1,0:T(8,128)(2,1)} %get-tuple-element.59), channel_id=1, source_target_pairs={{0,6},{1,97},{2,0},{3,99},{4,2},{5,101},{6,4},{7,103},{8,14},{9,10... | collective-permute-start | bytes 811016 | tf_op jit(solution)/shard_map/ppermute | solution.py:420
  118.2 8.2 %collective-permute-start.7 = (bf16[264,512]{1,0:T(8,128)(2,1)}, bf16[264,512]{1,0:T(8,128)(2,1)S(1)}, u32[]{:S(2)}, u32[]{:S(2)}) collective-permute-start(bf16[264,512]{1,0:T(8,128)(2,1)} %get-tuple-element.58), channel_id=1, source_target_pairs={{0,4},{1,65},{2,6},{3,67},{4,0},{5,69},{6,2},{7,71},{8,12},{9,73},... | collective-permute-start | bytes 811016 | tf_op jit(solution)/shard_map/ppermute | solution.py:420
  121.7 4.7 %copy-start.18 = (bf16[264,512]{1,0:T(8,128)(2,1)}, bf16[264,512]{1,0:T(8,128)(2,1)S(1)}, u32[]{:S(2)}) copy-start(bf16[264,512]{1,0:T(8,128)(2,1)S(1)} %collective-permute-done.6.refs_4_) | copy-start | bytes 811012
  131.6 8.7 %collective-permute-start.10 = (bf16[64,2432]{1,0:T(8,128)(2,1)}, bf16[64,2432]{1,0:T(8,128)(2,1)S(1)}, u32[]{:S(2)}, u32[]{:S(2)}) collective-permute-start(bf16[64,2432]{1,0:T(8,128)(2,1)} %get-tuple-element.33), channel_id=1, source_target_pairs={{0,16},{1,5},{2,18},{3,7},{4,20},{5,1},{6,22},{7,3},{8,24},{9,13},... | collective-permute-start | bytes 933896 | tf_op jit(solution)/shard_map/ppermute | solution.py:420
  131.6 11.7 %collective-permute-start.8 = (bf16[64,2432]{1,0:T(8,128)(2,1)}, bf16[64,2432]{1,0:T(8,128)(2,1)S(1)}, u32[]{:S(2)}, u32[]{:S(2)}) collective-permute-start(bf16[64,2432]{1,0:T(8,128)(2,1)} %get-tuple-element.31), channel_id=1, source_target_pairs={{0,8},{1,3},{2,10},{3,5},{4,12},{5,7},{6,14},{7,1},{8,16},{9,11},{... | collective-permute-start | bytes 933896 | tf_op jit(solution)/shard_map/ppermute | solution.py:420
  132.7 10.6 %collective-permute-start.9 = (bf16[64,2432]{1,0:T(8,128)(2,1)}, bf16[64,2432]{1,0:T(8,128)(2,1)S(1)}, u32[]{:S(2)}, u32[]{:S(2)}) collective-permute-start(bf16[64,2432]{1,0:T(8,128)(2,1)} %get-tuple-element.32), channel_id=1, source_target_pairs={{0,24},{1,7},{2,26},{3,1},{4,28},{5,3},{6,30},{7,5},{8,0},{9,15},{... | collective-permute-start | bytes 933896 | tf_op jit(solution)/shard_map/ppermute | solution.py:420
  140.3 3.0 %copy-start.15 = (bf16[64,2432]{1,0:T(8,128)(2,1)}, bf16[64,2432]{1,0:T(8,128)(2,1)S(1)}, u32[]{:S(2)}) copy-start(bf16[64,2432]{1,0:T(8,128)(2,1)S(1)} %collective-permute-done.10.refs_2_) | copy-start | bytes 933892
  146.6 7.1 %collective-permute-start.11 = (bf16[16,6272]{1,0:T(8,128)(2,1)}, bf16[16,6272]{1,0:T(8,128)(2,1)S(1)}, u32[]{:S(2)}, u32[]{:S(2)}) collective-permute-start(bf16[16,6272]{1,0:T(8,128)(2,1)} %get-tuple-element.35), channel_id=1, source_target_pairs={{0,32},{1,9},{2,34},{3,11},{4,36},{5,13},{6,38},{7,15},{8,40},{9,1... | collective-permute-start | bytes 602120 | tf_op jit(solution)/shard_map/ppermute | solution.py:420
  147.1 8.5 %collective-permute-start.12 = (bf16[16,6272]{1,0:T(8,128)(2,1)}, bf16[16,6272]{1,0:T(8,128)(2,1)S(1)}, u32[]{:S(2)}, u32[]{:S(2)}) collective-permute-start(bf16[16,6272]{1,0:T(8,128)(2,1)} %get-tuple-element.36), channel_id=1, source_target_pairs={{0,96},{1,25},{2,98},{3,27},{4,100},{5,29},{6,102},{7,31},{8,104},... | collective-permute-start | bytes 602120 | tf_op jit(solution)/shard_map/ppermute | solution.py:420
  149.8 7.4 %collective-permute-start.13 = (bf16[16,6272]{1,0:T(8,128)(2,1)}, bf16[16,6272]{1,0:T(8,128)(2,1)S(1)}, u32[]{:S(2)}, u32[]{:S(2)}) collective-permute-start(bf16[16,6272]{1,0:T(8,128)(2,1)} %get-tuple-element.37), channel_id=1, source_target_pairs={{0,64},{1,17},{2,66},{3,19},{4,68},{5,21},{6,70},{7,23},{8,72},{9,... | collective-permute-start | bytes 602120 | tf_op jit(solution)/shard_map/ppermute | solution.py:420
  159.3 20.5 %all-to-all-start.3 = ((bf16[64,16,512]{2,1,0:T(8,128)(2,1)}), bf16[64,16,512]{2,1,0:T(8,128)(2,1)S(1)}, u32[]{:S(2)}, u32[]{:S(2)}) async-start(bf16[64,16,512]{2,1,0:T(8,128)(2,1)} %broadcast_in_dim.36), calls=%async_computation.3 | async-start | bytes 2097152 | tf_op jit(solution)/shard_map/all_to_all | solution.py:398
  172.8 11.9 %copy-start.20 = (bf16[16,4096]{1,0:T(8,128)(2,1)S(1)}, bf16[16,4096]{1,0:T(8,128)(2,1)}, u32[]{:S(2)}) copy-start(bf16[16,4096]{1,0:T(8,128)(2,1)} %get-tuple-element.34) | copy-start | bytes 393220
  179.9 4.8 %copy-start.5 = (bf16[64,16,512]{2,1,0:T(8,128)(2,1)}, bf16[64,16,512]{2,1,0:T(8,128)(2,1)S(1)}, u32[]{:S(2)}) copy-start(bf16[64,16,512]{2,1,0:T(8,128)(2,1)S(1)} %all-to-all-done.3) | copy-start | bytes 3145732
  179.9 26.6 %all-to-all-start.2 = ((bf16[128,40,128]{2,1,0:T(8,128)(2,1)}), bf16[128,40,128]{2,1,0:T(8,128)(2,1)S(1)}, u32[]{:S(2)}, u32[]{:S(2)}) async-start(bf16[128,40,128]{2,1,0:T(8,128)(2,1)} %pack.1), calls=%async_computation.2 | async-start | bytes 2621440 | tf_op jit(solution)/shard_map/all_to_all | solution.py:398
  184.5 46.5 %collective-permute-start.15 = (bf16[1024,512]{1,0:T(8,128)(2,1)S(1)}, bf16[1024,512]{1,0:T(8,128)(2,1)}, u32[]{:S(2)}, u32[]{:S(2)}) collective-permute-start(bf16[1024,512]{1,0:T(8,128)(2,1)S(1)} %bitcast.83), channel_id=1, source_target_pairs={{0,1},{1,0},{2,3},{3,2},{4,5},{5,4},{6,7},{7,6},{8,9},{9,8},{10,11... | collective-permute-start | bytes 3145736 | tf_op jit(solution)/shard_map/ppermute | solution.py:641
  184.7 28.8 %copy-start.13 = (bf16[64,4096]{1,0:T(8,128)(2,1)}, bf16[64,4096]{1,0:T(8,128)(2,1)S(1)}, u32[]{:S(2)}) copy-start(bf16[64,4096]{1,0:T(8,128)(2,1)S(1)} %pad_maximum_fusion.7.held) | copy-start | bytes 1572868
  184.7 35.6 %collective-permute-start.14 = (bf16[64,4096]{1,0:T(8,128)(2,1)S(1)}, bf16[64,4096]{1,0:T(8,128)(2,1)}, u32[]{:S(2)}, u32[]{:S(2)}) collective-permute-start(bf16[64,4096]{1,0:T(8,128)(2,1)S(1)} %pad_maximum_fusion.7.held), channel_id=1, source_target_pairs={{0,1},{1,0},{2,3},{3,2},{4,5},{5,4},{6,7},{7,6},{8,9},{9,8},{10,11... | collective-permute-start | bytes 1572872 | tf_op jit(solution)/shard_map/ppermute | solution.py:636
  220.3 14.4 %copy-start.1 = (bf16[4096,128]{1,0:T(8,128)(2,1)S(1)}, bf16[4096,128]{1,0:T(8,128)(2,1)}, u32[]{:S(2)}) copy-start(bf16[4096,128]{1,0:T(8,128)(2,1)} %param.18) | copy-start | bytes 3145732
  (14 other events, 21.0 us)
